TPU v7x, 16 devices: a whole 2x2x2 slice. The times are simulated.
16 devices in a mesh: dp: 4 (over z, y), dap: 4 (over x, core).
Axes of the slice: x: 2, y: 2, z: 2, core: 2. Of those that a mesh axis runs over, the one named last changes fastest.
Arguments:
- single_rep: bfloat16 [4, 128, 384], P('dp', 'dap')
- pair_rep: bfloat16 [4, 128, 128, 128], P('dp', 'dap')
- token_mask: int32 [4, 128], P('dp')
- d_single_out: bfloat16 [4, 128, 384], P('dp', 'dap')
- d_pair_out: bfloat16 [4, 128, 128, 128], P('dp', 'dap')
- mul_out_in: bfloat16 [128, 512], replicated
- mul_out_gate: bfloat16 [128, 128], replicated
- mul_out_proj: bfloat16 [128, 128], replicated
- mul_in_in: bfloat16 [128, 512], replicated
- mul_in_gate: bfloat16 [128, 128], replicated
- mul_in_proj: bfloat16 [128, 128], replicated
- att_st_qkvg: bfloat16 [128, 512], replicated
- att_st_bias: bfloat16 [128, 4], replicated
- att_st_proj: bfloat16 [128, 128], replicated
- att_en_qkvg: bfloat16 [128, 512], replicated
- att_en_bias: bfloat16 [128, 4], replicated
- att_en_proj: bfloat16 [128, 128], replicated
- pair_up: bfloat16 [128, 1024], replicated
- pair_down: bfloat16 [512, 128], replicated
- sing_qkvg: bfloat16 [384, 1536], replicated
- sing_qbias: bfloat16 [384], replicated
- sing_pbias: bfloat16 [128, 16], replicated
- sing_proj: bfloat16 [384, 384], replicated
- sing_up: bfloat16 [384, 3072], replicated
- sing_down: bfloat16 [1536, 384], replicated
Outputs:
- output 1: bfloat16 [4, 128, 384], P('dp', 'dap')
- output 2: bfloat16 [4, 128, 128, 128], P('dp', 'dap')
- output 3: bfloat16 [4, 128, 384], P('dp', 'dap')
- output 4: bfloat16 [4, 128, 128, 128], P('dp', 'dap')
- output 5: float32 [3067264], P('dp')
All inputs are finite; a program needn't handle non-finite values.
Results may differ from a plain program's by a relative error of at most 0.02.
Values are sent between devices in bfloat16 or wider.
A program may use at most 1 GiB of HBM per device.

v0:
```python
import functools
import jax
import jax.numpy as jnp
from jax import lax
from jax.sharding import PartitionSpec as P

BATCH_AXIS = 'dp'
GROUP_AXIS = 'dap'
NORM_EPS = 1e-5
MASK_PENALTY = 1.0e9


def layer_norm(x_in):
    x_f32 = x_in.astype(jnp.float32)
    centered = x_f32 - jnp.mean(x_f32, axis=-1, keepdims=True)
    row_var = jnp.mean(centered * centered, axis=-1, keepdims=True)
    return centered * lax.rsqrt(row_var + NORM_EPS)


def mul_pre(z_rows, w_in, w_gate):
    normed = layer_norm(z_rows).astype(jnp.bfloat16)
    proj_all = jnp.dot(normed, w_in, preferred_element_type=jnp.float32)
    inner_dim = w_in.shape[1] // 4
    left_proj = (jax.nn.sigmoid(proj_all[..., inner_dim:2 * inner_dim]) * proj_all[..., :inner_dim]).astype(jnp.bfloat16)
    right_proj = (jax.nn.sigmoid(proj_all[..., 3 * inner_dim:]) * proj_all[..., 2 * inner_dim:3 * inner_dim]).astype(jnp.bfloat16)
    gate_vals = jax.nn.sigmoid(jnp.dot(normed, w_gate, preferred_element_type=jnp.float32))
    return left_proj, right_proj, gate_vals


def mul_post(z_rows, mixed_sum, gate_vals, w_out):
    normed = layer_norm(mixed_sum).astype(jnp.bfloat16)
    update = gate_vals * jnp.dot(normed, w_out, preferred_element_type=jnp.float32)
    return (z_rows.astype(jnp.float32) + update).astype(jnp.bfloat16)


def att_pre(z_rows, w_qkvg, w_tb):
    normed = layer_norm(z_rows).astype(jnp.bfloat16)
    proj_all = jnp.dot(normed, w_qkvg, preferred_element_type=jnp.float32)
    inner_dim = w_qkvg.shape[1] // 4
    num_heads = w_tb.shape[1]
    head_shape = z_rows.shape[:2] + (num_heads, inner_dim // num_heads)
    q_rows = proj_all[..., :inner_dim].astype(jnp.bfloat16).reshape(head_shape)
    k_rows = proj_all[..., inner_dim:2 * inner_dim].astype(jnp.bfloat16).reshape(head_shape)
    v_rows = proj_all[..., 2 * inner_dim:3 * inner_dim].astype(jnp.bfloat16).reshape(head_shape)
    gate_vals = jax.nn.sigmoid(proj_all[..., 3 * inner_dim:])
    bias_rows = jnp.dot(normed, w_tb, preferred_element_type=jnp.float32).astype(jnp.bfloat16)
    return q_rows, k_rows, v_rows, gate_vals, bias_rows


def att_core(q_rows, k_rows, v_rows, bias_full, mask_bias):
    att_scale = q_rows.shape[-1] ** -0.5
    logits = jnp.einsum('ijhd,ikhd->ihjk', q_rows, k_rows, preferred_element_type=jnp.float32) * att_scale
    logits = logits + jnp.transpose(bias_full, (2, 0, 1)) + mask_bias
    prob_mat = jax.nn.softmax(logits, axis=-1).astype(jnp.bfloat16)
    return jnp.einsum('ihjk,ikhd->ijhd', prob_mat, v_rows, preferred_element_type=jnp.float32)


def gated_out(x_rows, attended, gate_vals, w_o):
    gated = (gate_vals * attended.reshape(gate_vals.shape)).astype(jnp.bfloat16)
    return (x_rows.astype(jnp.float32) + jnp.dot(gated, w_o, preferred_element_type=jnp.float32)).astype(jnp.bfloat16)


def transition(x_rows, w_up, w_down):
    normed = layer_norm(x_rows).astype(jnp.bfloat16)
    hidden = jnp.dot(normed, w_up, preferred_element_type=jnp.float32)
    inner_dim = w_down.shape[0]
    acted = (jax.nn.silu(hidden[..., :inner_dim]) * hidden[..., inner_dim:]).astype(jnp.bfloat16)
    return (x_rows.astype(jnp.float32) + jnp.dot(acted, w_down, preferred_element_type=jnp.float32)).astype(jnp.bfloat16)


def single_pre(s_rows, w_qkvg, q_bias):
    normed = layer_norm(s_rows).astype(jnp.bfloat16)
    proj_all = jnp.dot(normed, w_qkvg, preferred_element_type=jnp.float32)
    inner_dim = w_qkvg.shape[1] // 4
    q_rows = (proj_all[:, :inner_dim] + q_bias.astype(jnp.float32)).astype(jnp.bfloat16)
    k_rows = proj_all[:, inner_dim:2 * inner_dim].astype(jnp.bfloat16)
    v_rows = proj_all[:, 2 * inner_dim:3 * inner_dim].astype(jnp.bfloat16)
    gate_vals = jax.nn.sigmoid(proj_all[:, 3 * inner_dim:])
    return q_rows, k_rows, v_rows, gate_vals


def pair_bias(z_rows, w_pb):
    normed = layer_norm(z_rows).astype(jnp.bfloat16)
    return jnp.dot(normed, w_pb, preferred_element_type=jnp.float32).astype(jnp.bfloat16)


def single_core(q_rows, k_all, v_all, bias_rows, mask_bias):
    num_heads = bias_rows.shape[-1]
    head_dim = q_rows.shape[-1] // num_heads
    q_heads = q_rows.reshape(q_rows.shape[0], num_heads, head_dim)
    k_heads = k_all.reshape(k_all.shape[0], num_heads, head_dim)
    v_heads = v_all.reshape(v_all.shape[0], num_heads, head_dim)
    logits = jnp.einsum('ihd,jhd->hij', q_heads, k_heads, preferred_element_type=jnp.float32) * head_dim ** -0.5
    logits = logits + jnp.transpose(bias_rows, (2, 0, 1)).astype(jnp.float32) + mask_bias
    prob_mat = jax.nn.softmax(logits, axis=-1).astype(jnp.bfloat16)
    return jnp.einsum('hij,jhd->ihd', prob_mat, v_heads, preferred_element_type=jnp.float32)


def gather_rows(x_in):
    return lax.all_gather(x_in, GROUP_AXIS, axis=0, tiled=True)


def scatter_rows(x_in):
    return lax.psum_scatter(x_in, GROUP_AXIS, scatter_dimension=0, tiled=True)


def rows_to_cols(x_in):
    return jnp.transpose(lax.all_to_all(x_in, GROUP_AXIS, 1, 0, tiled=True), (1, 0, 2))


def cols_to_rows(x_in):
    return lax.all_to_all(jnp.transpose(x_in, (1, 0, 2)), GROUP_AXIS, 0, 1, tiled=True)


def mul_out_forward(z_rows, w_in, w_gate, w_out):
    (left_proj, right_proj, gate_vals), pull_pre = jax.vjp(mul_pre, z_rows, w_in, w_gate)
    right_all = gather_rows(right_proj)
    mixed_sum = jnp.einsum('ikc,jkc->ijc', left_proj, right_all, preferred_element_type=jnp.float32)
    z_new, pull_post = jax.vjp(mul_post, z_rows, mixed_sum, gate_vals, w_out)
    return z_new, (pull_pre, pull_post, left_proj, right_all)


def mul_out_backward(dz_new, saved_state):
    pull_pre, pull_post, left_proj, right_all = saved_state
    dz_post, d_mixed, d_gate, g_out = pull_post(dz_new)
    d_mixed = d_mixed.astype(jnp.bfloat16)
    d_left = jnp.einsum('ijc,jkc->ikc', d_mixed, right_all, preferred_element_type=jnp.float32).astype(jnp.bfloat16)
    right_part = jnp.einsum('ijc,ikc->jkc', d_mixed, left_proj, preferred_element_type=jnp.float32)
    d_right = scatter_rows(right_part).astype(jnp.bfloat16)
    dz_pre, g_in, g_gate = pull_pre((d_left, d_right, d_gate))
    return dz_post + dz_pre, [g_in, g_gate, g_out]


def mul_in_forward(z_rows, w_in, w_gate, w_out):
    (left_proj, right_proj, gate_vals), pull_pre = jax.vjp(mul_pre, z_rows, w_in, w_gate)
    left_cols = lax.all_to_all(left_proj, GROUP_AXIS, 1, 0, tiled=True)
    right_all = gather_rows(right_proj)
    mixed_sum = jnp.einsum('kic,kjc->ijc', left_cols, right_all, preferred_element_type=jnp.float32)
    z_new, pull_post = jax.vjp(mul_post, z_rows, mixed_sum, gate_vals, w_out)
    return z_new, (pull_pre, pull_post, left_cols, right_all)


def mul_in_backward(dz_new, saved_state):
    pull_pre, pull_post, left_cols, right_all = saved_state
    dz_post, d_mixed, d_gate, g_out = pull_post(dz_new)
    d_mixed = d_mixed.astype(jnp.bfloat16)
    d_left_cols = jnp.einsum('ijc,kjc->kic', d_mixed, right_all, preferred_element_type=jnp.float32).astype(jnp.bfloat16)
    d_left = lax.all_to_all(d_left_cols, GROUP_AXIS, 0, 1, tiled=True)
    right_part = jnp.einsum('ijc,kic->kjc', d_mixed, left_cols, preferred_element_type=jnp.float32)
    d_right = scatter_rows(right_part).astype(jnp.bfloat16)
    dz_pre, g_in, g_gate = pull_pre((d_left, d_right, d_gate))
    return dz_post + dz_pre, [g_in, g_gate, g_out]


def att_forward(z_rows, mask_bias, w_qkvg, w_tb, w_o):
    (q_rows, k_rows, v_rows, gate_vals, bias_rows), pull_pre = jax.vjp(att_pre, z_rows, w_qkvg, w_tb)
    bias_full = gather_rows(bias_rows).astype(jnp.float32)
    attended, pull_core = jax.vjp(functools.partial(att_core, mask_bias=mask_bias), q_rows, k_rows, v_rows, bias_full)
    z_new, pull_post = jax.vjp(gated_out, z_rows, attended, gate_vals, w_o)
    return z_new, (pull_pre, pull_core, pull_post)


def att_backward(dz_new, saved_state):
    pull_pre, pull_core, pull_post = saved_state
    dz_post, d_att, d_gate, g_out = pull_post(dz_new)
    d_query, d_key, d_value, d_bias_full = pull_core(d_att)
    d_bias = scatter_rows(d_bias_full).astype(jnp.bfloat16)
    dz_pre, g_qkvg, g_bias = pull_pre((d_query, d_key, d_value, d_gate, d_bias))
    return dz_post + dz_pre, [g_qkvg, g_bias, g_out]


def single_forward(s_rows, z_rows, mask_bias, w_qkvg, q_bias, w_pb, w_o, w_up, w_down):
    (q_rows, k_rows, v_rows, gate_vals), pull_pre = jax.vjp(single_pre, s_rows, w_qkvg, q_bias)
    bias_rows, pull_bias = jax.vjp(pair_bias, z_rows, w_pb)
    k_all = gather_rows(k_rows)
    v_all = gather_rows(v_rows)
    attended, pull_core = jax.vjp(functools.partial(single_core, mask_bias=mask_bias), q_rows, k_all, v_all, bias_rows)
    s_mid, pull_post = jax.vjp(gated_out, s_rows, attended, gate_vals, w_o)
    s_new, pull_trans = jax.vjp(transition, s_mid, w_up, w_down)
    return s_new, (pull_pre, pull_bias, pull_core, pull_post, pull_trans)


def single_backward(ds_new, saved_state):
    pull_pre, pull_bias, pull_core, pull_post, pull_trans = saved_state
    ds_mid, g_up, g_down = pull_trans(ds_new)
    ds_post, d_att, d_gate, g_out = pull_post(ds_mid)
    d_query, d_key_all, d_value_all, d_bias_rows = pull_core(d_att)
    d_key = scatter_rows(d_key_all.astype(jnp.float32)).astype(jnp.bfloat16)
    d_value = scatter_rows(d_value_all.astype(jnp.float32)).astype(jnp.bfloat16)
    ds_pre, g_qkvg, g_qbias = pull_pre((d_query, d_key, d_value, d_gate))
    dz_bias, g_pbias = pull_bias(d_bias_rows)
    return ds_post + ds_pre, dz_bias, [g_qkvg, g_qbias, g_pbias, g_out, g_up, g_down]


def device_step(single_blk, pair_blk, mask_blk, d_single_blk, d_pair_blk, *weights):
    s_rows = single_blk[0]
    z_rows = pair_blk[0]
    mask_bias = (mask_blk[0].astype(jnp.float32) - 1.0) * MASK_PENALTY
    z_one, saved_one = mul_out_forward(z_rows, weights[0], weights[1], weights[2])
    z_two, saved_two = mul_in_forward(z_one, weights[3], weights[4], weights[5])
    z_three, saved_three = att_forward(z_two, mask_bias, weights[6], weights[7], weights[8])
    zt_four, saved_four = att_forward(rows_to_cols(z_three), mask_bias, weights[9], weights[10], weights[11])
    z_four = cols_to_rows(zt_four)
    z_five, pull_pair = jax.vjp(transition, z_four, weights[12], weights[13])
    s_out, saved_single = single_forward(s_rows, z_five, mask_bias, *weights[14:20])
    ds_in, dz_bias, single_grads = single_backward(d_single_blk[0], saved_single)
    dz_four, g_pup, g_pdown = pull_pair(d_pair_blk[0] + dz_bias)
    dzt_three, end_grads = att_backward(rows_to_cols(dz_four), saved_four)
    dz_two, start_grads = att_backward(cols_to_rows(dzt_three), saved_three)
    dz_one, in_grads = mul_in_backward(dz_two, saved_two)
    dz_zero, out_grads = mul_out_backward(dz_one, saved_one)
    all_grads = out_grads + in_grads + start_grads + end_grads + [g_pup, g_pdown] + single_grads
    grad_flat = jnp.concatenate([g_item.astype(jnp.float32).reshape(-1) for g_item in all_grads])
    grad_flat = lax.psum(grad_flat, GROUP_AXIS)
    grad_flat = lax.psum_scatter(grad_flat, BATCH_AXIS, scatter_dimension=0, tiled=True)
    return s_out[None], z_five[None], ds_in[None], dz_zero[None], grad_flat


def solution(mesh):
    spec_single = P(BATCH_AXIS, GROUP_AXIS, None)
    spec_pair = P(BATCH_AXIS, GROUP_AXIS, None, None)
    spec_mask = P(BATCH_AXIS, None)

    def block_fn(single_rep, pair_rep, token_mask, d_single_out, d_pair_out, *weights):
        in_specs = (spec_single, spec_pair, spec_mask, spec_single, spec_pair) + tuple(P() for w_item in weights)
        out_specs = (spec_single, spec_pair, spec_single, spec_pair, P(BATCH_AXIS))
        mapped = jax.shard_map(device_step, mesh=mesh, in_specs=in_specs, out_specs=out_specs, check_vma=False)
        return mapped(single_rep, pair_rep, token_mask, d_single_out, d_pair_out, *weights)

    return block_fn
```

profile of v0, /device:TPU:1, one launch (start us, length us, event | category | flops | bytes accessed | tf_op | source)
XLA Modules:
  0.0 1275.4 jit_solution(5413466003880120689)
XLA Ops:
  17.8 34.8 %all-gather.3.cloned.1.call-done = bf16[128,128,128]{2,1,0:T(8,128)(2,1)} async-done(((bf16[32,128,128]{2,1,0:T(8,128)(2,1)}), bf16[128,128,128]{2,1,0:T(8,128)(2,1)}) %all-gather.3.cloned.1.call-update) | async-done | bytes 4194320 | tf_op jit(solution)/shard_map/all_gather | solution.py:100
  52.6 6.7 copy.530
  59.3 4.8 bitcast_reduce_fusion.2
  79.4 17.3 %all-to-all-start = ((bf16[32,128,128]{2,0,1:T(8,128)(2,1)}), bf16[32,128,128]{2,0,1:T(8,128)(2,1)S(1)}, u32[]{:S(2)}, u32[]{:S(2)}) async-start(bf16[32,128,128]{2,0,1:T(8,128)(2,1)} %copy.542), calls=%async_computation | async-start | bytes 2097152 | tf_op jit(solution)/shard_map/all_to_all | solution.py:136
  96.7 23.0 %all-to-all-done = bf16[32,128,128]{2,0,1:T(8,128)(2,1)S(1)} async-done(((bf16[32,128,128]{2,0,1:T(8,128)(2,1)}), bf16[32,128,128]{2,0,1:T(8,128)(2,1)S(1)}, u32[]{:S(2)}, u32[]{:S(2)}) %all-to-all-start) | async-done | bytes 1048608 | tf_op jit(solution)/shard_map/all_to_all | solution.py:136
  123.5 7.1 copy.545
  141.5 5.8 all_gather.22
  149.9 5.5 fusion.381
  170.4 8.2 fusion.382
  178.6 4.9 divide_convert_fusion.1
  197.7 12.3 all-to-all-done.1
  216.5 6.6 all_gather.23
  225.7 5.5 fusion.383
  245.1 8.8 fusion.384
  253.9 4.8 divide_convert_fusion
  275.2 10.9 all_gather.19
  287.7 5.5 all_gather.18
  309.9 4.0 fusion.233
  341.1 10.9 convert_multiply_fusion.3
  352.0 9.4 fusion.74
  364.9 3.8 all-to-all-start.3
  370.0 12.0 all-to-all-done.3
  392.6 5.4 fusion.7
  406.8 14.2 %all-reduce.33 = bf16[128,128,4]{1,2,0:T(4,128)(2,1)S(1)} all-reduce(f32[128,128,4]{1,2,0:T(4,128)S(1)} %copy.592), channel_id=4, replica_groups=mesh['dp'=4,'dap'=4] {'dap'}, use_global_device_ids=true, to_apply=%region_39.40.clone | all-reduce | flops 65536 | bytes 393216
  421.1 3.9 fusion.116
  434.3 4.1 all-to-all-start.4
  438.4 13.2 %all-to-all-done.4 = bf16[128,32,128]{2,1,0:T(8,128)(2,1)S(1)} async-done(((bf16[128,32,128]{2,1,0:T(8,128)(2,1)}), bf16[128,32,128]{2,1,0:T(8,128)(2,1)S(1)}, u32[]{:S(2)}, u32[]{:S(2)}) %all-to-all-start.4) | async-done | bytes 1048608 | tf_op jit(solution)/shard_map/all_to_all | solution.py:112
  463.7 5.7 fusion.11
  478.1 14.4 %all-reduce.34 = bf16[128,128,4]{1,2,0:T(4,128)(2,1)S(1)} all-reduce(f32[128,128,4]{1,2,0:T(4,128)S(1)} %copy.601), channel_id=5, replica_groups=mesh['dp'=4,'dap'=4] {'dap'}, use_global_device_ids=true, to_apply=%region_44.45.clone | all-reduce | flops 65536 | bytes 393216
  504.6 8.4 copy.761
  513.0 4.5 fusion.144
  519.8 4.2 all-to-all-start.5
  526.6 13.2 %all-to-all-done.5 = bf16[128,32,128]{2,1,0:T(8,128)(2,1)S(1)} async-done(((bf16[128,32,128]{2,1,0:T(8,128)(2,1)}), bf16[128,32,128]{2,1,0:T(8,128)(2,1)S(1)}, u32[]{:S(2)}, u32[]{:S(2)}) %all-to-all-start.5) | async-done | bytes 1048608 | tf_op jit(solution)/shard_map/all_to_all | solution.py:148
  543.6 40.4 %reduce-scatter.9.cloned.1.call-done = f32[32,128,128]{1,2,0:T(8,128)} async-done(((f32[128,128,128]{1,2,0:T(8,128)}), f32[32,128,128]{1,2,0:T(8,128)}) %reduce-scatter.9.cloned.1.call-update) | async-done | bytes 2097168 | tf_op jit(solution)/shard_map/reduce_scatter | solution.py:104
  584.0 5.1 convert_multiply_fusion.16
  603.4 4.6 fusion.213
  608.0 9.3 copy.622
  629.7 6.8 fusion.148
  673.8 15.9 %reduce-scatter.11.cloned.1.call-done = f32[32,128,128]{1,2,0:T(8,128)} async-done(((f32[128,128,128]{1,2,0:T(8,128)}), f32[32,128,128]{1,2,0:T(8,128)}) %reduce-scatter.11.cloned.1.call-update) | async-done | bytes 2097168 | tf_op jit(solution)/shard_map/reduce_scatter | solution.py:104
  689.6 5.7 convert_multiply_fusion.9
  718.2 4.5 fusion.155
  726.7 5.8 dynamic-update-slice.17
  732.5 37.2 %dynamic-update-slice.18 = bf16[3067264]{0:T(1024)(128)(2,1)} dynamic-update-slice(bf16[3067264]{0:T(1024)(128)(2,1)} %dynamic-update-slice.17, bf16[1179648]{0:T(1024)(128)(2,1)} %bitcast.638, s32[]{} %constant.160) | dynamic-update-slice | bytes 4718596
  769.7 18.8 %dynamic-update-slice.19 = bf16[3067264]{0:T(1024)(128)(2,1)} dynamic-update-slice(bf16[3067264]{0:T(1024)(128)(2,1)} %dynamic-update-slice.18, bf16[589824]{0:T(1024)(128)(2,1)S(1)} %copy-done.78, s32[]{} %constant.161) | dynamic-update-slice | bytes 2359300 | tf_op jit(solution)/shard_map/concatenate | solution.py:213
  788.5 407.4 %all-reduce.35 = f32[3067264]{0:T(1024)} all-reduce(bf16[3067264]{0:T(1024)(128)(2,1)} %dynamic-update-slice.19), channel_id=8, replica_groups=mesh['dp'=4,'dap'=4] {'dp'}, use_global_device_ids=true, to_apply=%region_59.60.clone | all-reduce | flops 3067264 | bytes 18403584
  1195.9 4.4 dynamic-slice.5
  1201.2 4.3 fusion.118
  1210.3 54.4 %all-reduce.32.cloned.1.call-done = f32[766816]{0:T(1024)} async-done(((f32[766816]{0:T(1024)}), f32[766816]{0:T(1024)}) %all-reduce.32.cloned.1.call-update) | async-done | bytes 3067280 | tf_op jit(solution)/shard_map/psum | solution.py:214
  (762 shorter events, 328.2 us)
Async XLA Ops:
  7.2 323.1 %copy-start = (bf16[384,3072]{1,0:T(8,128)(2,1)S(1)}, bf16[384,3072]{1,0:T(8,128)(2,1)}, u32[]{:S(2)}) copy-start(bf16[384,3072]{1,0:T(8,128)(2,1)} %param.48) | copy-start | bytes 7077892
  7.2 45.4 %all-gather.3.cloned.1.call-start = ((), (), s32[]{:S(2)}) async-start(), calls=%async_computation.10 | async-start | bytes 5242880 | tf_op jit(solution)/shard_map/all_gather | solution.py:100
  9.0 57.7 %copy-start.15 = (bf16[1,32,128,128]{2,3,1,0:T(8,128)(2,1)}, bf16[1,32,128,128]{2,3,1,0:T(8,128)(2,1)S(1)}, u32[]{:S(2)}) copy-start(bf16[1,32,128,128]{2,3,1,0:T(8,128)(2,1)S(1)} %copy.521) | copy-start | bytes 3145732
  9.2 57.5 %copy-start.117 = (f32[32,128]{1,0:T(8,128)}, f32[32,128]{1,0:T(8,128)S(1)}, u32[]{:S(2)}) copy-start(f32[32,128]{1,0:T(8,128)S(1)} %broadcast_multiply_fusion.7) | copy-start | bytes 49156
  10.2 56.5 %copy-start.133 = (f32[32,128]{1,0:T(8,128)}, f32[32,128]{1,0:T(8,128)S(1)}, u32[]{:S(2)}) copy-start(f32[32,128]{1,0:T(8,128)S(1)} %fusion.308) | copy-start | bytes 49156
  17.7 105.8 %all-gather.5.cloned.1.call-start = ((), (), s32[]{:S(2)}) async-start(), calls=%async_computation.11 | async-start | bytes 5242880 | tf_op jit(solution)/shard_map/all_gather | solution.py:100
  69.4 67.2 %copy-start.119 = (f32[32,128]{1,0:T(8,128)}, f32[32,128]{1,0:T(8,128)S(1)}, u32[]{:S(2)}) copy-start(f32[32,128]{1,0:T(8,128)S(1)} %broadcast_multiply_fusion.5) | copy-start | bytes 49156
  70.4 66.2 %copy-start.135 = (f32[32,128]{1,0:T(8,128)}, f32[32,128]{1,0:T(8,128)S(1)}, u32[]{:S(2)}) copy-start(f32[32,128]{1,0:T(8,128)S(1)} %fusion.310) | copy-start | bytes 49156
  77.7 19.0 %copy-start.234 = (s32[1,128]{1,0:T(1,128)S(1)}, s32[1,128]{1,0:T(1,128)}, u32[]{:S(2)}) copy-start(s32[1,128]{1,0:T(1,128)} %param.27) | copy-start | bytes 1540
  79.4 40.3 %all-to-all-start = ((bf16[32,128,128]{2,0,1:T(8,128)(2,1)}), bf16[32,128,128]{2,0,1:T(8,128)(2,1)S(1)}, u32[]{:S(2)}, u32[]{:S(2)}) async-start(bf16[32,128,128]{2,0,1:T(8,128)(2,1)} %copy.542), calls=%async_computation | async-start | bytes 2097152 | tf_op jit(solution)/shard_map/all_to_all | solution.py:136
  96.7 148.5 %copy-start.225 = (f32[128]{0:T(128)}, f32[128]{0:T(128)S(1)}, u32[]{:S(2)}) copy-start(f32[128]{0:T(128)S(1)} %multiply_bitcast_fusion.1) | copy-start | bytes 1540
  140.2 47.0 %copy-start.39 = (bf16[32,128,128]{1,2,0:T(8,128)(2,1)}, bf16[32,128,128]{1,2,0:T(8,128)(2,1)S(1)}, u32[]{:S(2)}) copy-start(bf16[32,128,128]{1,2,0:T(8,128)(2,1)S(1)} %get-tuple-element.35) | copy-start | bytes 3145732
  140.2 15.2 %copy-start.137 = (f32[32,128]{1,0:T(8,128)}, f32[32,128]{1,0:T(8,128)S(1)}, u32[]{:S(2)}) copy-start(f32[32,128]{1,0:T(8,128)S(1)} %broadcast_multiply_fusion.3) | copy-start | bytes 49156
  141.2 14.2 %copy-start.153 = (f32[32,128]{1,0:T(8,128)}, f32[32,128]{1,0:T(8,128)S(1)}, u32[]{:S(2)}) copy-start(f32[32,128]{1,0:T(8,128)S(1)} %fusion.312) | copy-start | bytes 49156
  193.1 16.9 %all-to-all-start.1 = ((bf16[32,128,128]{2,0,1:T(8,128)(2,1)}), bf16[32,128,128]{2,0,1:T(8,128)(2,1)S(1)}, u32[]{:S(2)}, u32[]{:S(2)}) async-start(bf16[32,128,128]{2,0,1:T(8,128)(2,1)} %copy.559), calls=%async_computation.1 | async-start | bytes 2097152 | tf_op jit(solution)/shard_map/all_to_all | solution.py:108
  197.5 73.2 %copy-start.213 = (f32[32]{0:T(128)}, f32[32]{0:T(128)S(1)}, u32[]{:S(2)}) copy-start(f32[32]{0:T(128)S(1)} %broadcast_multiply_fusion.9) | copy-start | bytes 388
  197.7 13.1 %copy-start.228 = (f32[32]{0:T(128)}, f32[32]{0:T(128)S(1)}, u32[]{:S(2)}) copy-start(f32[32]{0:T(128)S(1)} %fusion.276) | copy-start | bytes 388
  197.7 73.0 %copy-start.217 = (f32[32]{0:T(128)}, f32[32]{0:T(128)S(1)}, u32[]{:S(2)}) copy-start(f32[32]{0:T(128)S(1)} %fusion.325) | copy-start | bytes 388
  216.2 15.0 %copy-start.53 = (bf16[32,128,128]{2,1,0:T(8,128)(2,1)}, bf16[32,128,128]{2,1,0:T(8,128)(2,1)S(1)}, u32[]{:S(2)}) copy-start(bf16[32,128,128]{2,1,0:T(8,128)(2,1)S(1)} %multiply_convert_fusion.2) | copy-start | bytes 3145732
  238.7 20.1 %copy-start.57 = (bf16[32,128,128]{1,2,0:T(8,128)(2,1)}, bf16[32,128,128]{1,2,0:T(8,128)(2,1)S(1)}, u32[]{:S(2)}) copy-start(bf16[32,128,128]{1,2,0:T(8,128)(2,1)S(1)} %copy.563) | copy-start | bytes 3145732
  266.9 30.2 %all-to-all-start.2 = ((bf16[128,32,128]{2,1,0:T(8,128)(2,1)}), bf16[128,32,128]{2,1,0:T(8,128)(2,1)S(1)}, u32[]{:S(2)}, u32[]{:S(2)}) async-start(bf16[128,32,128]{2,1,0:T(8,128)(2,1)} %copy.569), calls=%async_computation.2 | async-start | bytes 2097152 | tf_op jit(solution)/shard_map/all_to_all | solution.py:112
  305.0 57.2 %copy-start.139 = (f32[32,128]{1,0:T(8,128)}, f32[32,128]{1,0:T(8,128)S(1)}, u32[]{:S(2)}) copy-start(f32[32,128]{1,0:T(8,128)S(1)} %rsqrt.111) | copy-start | bytes 49156
  322.2 17.9 %copy-start.38 = (bf16[32,128,128]{1,2,0:T(8,128)(2,1)}, bf16[32,128,128]{1,2,0:T(8,128)(2,1)S(1)}, u32[]{:S(2)}) copy-start(bf16[32,128,128]{1,2,0:T(8,128)(2,1)S(1)} %get-tuple-element.90) | copy-start | bytes 3145732
  341.0 21.2 %copy-start.84 = (bf16[32,128,128]{1,2,0:T(8,128)(2,1)}, bf16[32,128,128]{1,2,0:T(8,128)(2,1)S(1)}, u32[]{:S(2)}) copy-start(bf16[32,128,128]{1,2,0:T(8,128)(2,1)S(1)} %fusion.196) | copy-start | bytes 3145732
  341.0 10.9 copy-start.6
  341.0 10.9 copy-start.108
  364.9 19.6 %copy-start.51 = (f32[32,128,128]{1,2,0:T(8,128)S(1)}, f32[32,128,128]{1,2,0:T(8,128)}, u32[]{:S(2)}) copy-start(f32[32,128,128]{1,2,0:T(8,128)} %copy.708) | copy-start | bytes 6291460
  364.9 19.6 %copy-start.206 = (bf16[128,128]{1,0:T(8,128)(2,1)S(1)}, bf16[128,128]{1,0:T(8,128)(2,1)}, u32[]{:S(2)}) copy-start(bf16[128,128]{1,0:T(8,128)(2,1)} %param.41) | copy-start | bytes 98308
  364.9 17.1 %all-to-all-start.3 = ((bf16[32,128,128]{2,0,1:T(8,128)(2,1)}), bf16[32,128,128]{2,0,1:T(8,128)(2,1)S(1)}, u32[]{:S(2)}, u32[]{:S(2)}) async-start(bf16[32,128,128]{2,0,1:T(8,128)(2,1)} %copy.589), calls=%async_computation.5 | async-start | bytes 2097152 | tf_op jit(solution)/shard_map/all_to_all | solution.py:108
  384.6 45.4 %copy-start.72 = (bf16[4,32,32,128]{3,1,0,2:T(8,128)(2,1)}, bf16[4,32,32,128]{3,1,0,2:T(8,128)(2,1)S(1)}, u32[]{:S(2)}) copy-start(bf16[4,32,32,128]{3,1,0,2:T(8,128)(2,1)S(1)} %copy.591) | copy-start | bytes 3145732
  404.3 16.7 %copy-start.188 = (bf16[128,512]{1,0:T(8,128)(2,1)S(1)}, bf16[128,512]{1,0:T(8,128)(2,1)}, u32[]{:S(2)}) copy-start(bf16[128,512]{1,0:T(8,128)(2,1)} %param.39) | copy-start | bytes 393220
  434.3 17.3 %all-to-all-start.4 = ((bf16[128,32,128]{2,1,0:T(8,128)(2,1)}), bf16[128,32,128]{2,1,0:T(8,128)(2,1)S(1)}, u32[]{:S(2)}, u32[]{:S(2)}) async-start(bf16[128,32,128]{2,1,0:T(8,128)(2,1)} %copy.599), calls=%async_computation.6 | async-start | bytes 2097152 | tf_op jit(solution)/shard_map/all_to_all | solution.py:112
  438.4 145.6 %reduce-scatter.9.cloned.1.call-start = ((), (), s32[]{:S(2)}) async-start(), calls=%async_computation.14 | async-start | bytes 10485760 | tf_op jit(solution)/shard_map/reduce_scatter | solution.py:104
  463.7 28.9 %copy-start.116 = (bf16[32,4,32,128]{3,2,1,0:T(8,128)(2,1)}, bf16[32,4,32,128]{3,2,1,0:T(8,128)(2,1)S(1)}, u32[]{:S(2)}) copy-start(bf16[32,4,32,128]{3,2,1,0:T(8,128)(2,1)S(1)} %fusion.390) | copy-start | bytes 3145732
  475.7 16.9 %copy-start.189 = (bf16[128,512]{1,0:T(8,128)(2,1)S(1)}, bf16[128,512]{1,0:T(8,128)(2,1)}, u32[]{:S(2)}) copy-start(bf16[128,512]{1,0:T(8,128)(2,1)} %param.36) | copy-start | bytes 393220
  519.8 20.0 %all-to-all-start.5 = ((bf16[128,32,128]{2,1,0:T(8,128)(2,1)}), bf16[128,32,128]{2,1,0:T(8,128)(2,1)S(1)}, u32[]{:S(2)}, u32[]{:S(2)}) async-start(bf16[128,32,128]{2,1,0:T(8,128)(2,1)} %copy.613), calls=%async_computation.8 | async-start | bytes 2097152 | tf_op jit(solution)/shard_map/all_to_all | solution.py:148
  524.0 123.5 %reduce-scatter.7.cloned.1.call-start = ((), (), s32[]{:S(2)}) async-start(), calls=%async_computation.13 | async-start | bytes 245760 | tf_op jit(solution)/shard_map/reduce_scatter | solution.py:104
  525.3 123.0 %reduce-scatter.5.cloned.1.call-start = ((), (), s32[]{:S(2)}) async-start(), calls=%async_computation.12 | async-start | bytes 245760 | tf_op jit(solution)/shard_map/reduce_scatter | solution.py:104
  526.5 163.1 %reduce-scatter.11.cloned.1.call-start = ((), (), s32[]{:S(2)}) async-start(), calls=%async_computation.15 | async-start | bytes 10485760 | tf_op jit(solution)/shard_map/reduce_scatter | solution.py:104
  617.3 647.4 %all-reduce.32.cloned.1.call-start = ((), (), s32[]{:S(2)}) async-start(), calls=%async_computation.16 | async-start | bytes 6135808 | tf_op jit(solution)/shard_map/psum | solution.py:214
  619.2 10.6 copy-start.7
  619.2 10.6 copy-start.140
  673.7 21.7 %copy-start.16 = (bf16[1,32,128,128]{2,3,1,0:T(8,128)(2,1)S(1)}, bf16[1,32,128,128]{2,3,1,0:T(8,128)(2,1)}, u32[]{:S(2)}) copy-start(bf16[1,32,128,128]{2,3,1,0:T(8,128)(2,1)} %copy-done.15) | copy-start | bytes 3145732
  673.8 21.6 %copy-start.118 = (f32[32,128]{1,0:T(8,128)S(1)}, f32[32,128]{1,0:T(8,128)}, u32[]{:S(2)}) copy-start(f32[32,128]{1,0:T(8,128)} %copy-done.117) | copy-start | bytes 49156
  673.8 21.6 %copy-start.134 = (f32[32,128]{1,0:T(8,128)S(1)}, f32[32,128]{1,0:T(8,128)}, u32[]{:S(2)}) copy-start(f32[32,128]{1,0:T(8,128)} %copy-done.133) | copy-start | bytes 49156
  707.1 10.4 copy-start.115
  732.5 37.2 %copy-start.78 = (bf16[589824]{0:T(1024)(128)(2,1)S(1)}, bf16[589824]{0:T(1024)(128)(2,1)}, u32[]{:S(2)}) copy-start(bf16[589824]{0:T(1024)(128)(2,1)} %reshape.539) | copy-start | bytes 3538948
  1209.0 59.5 %copy-start.1 = (bf16[384,3072]{1,0:T(8,128)(2,1)S(1)}, bf16[384,3072]{1,0:T(8,128)(2,1)}, u32[]{:S(2)}) copy-start(bf16[384,3072]{1,0:T(8,128)(2,1)} %param.48) | copy-start | bytes 7077892
  (206 other events, 664.9 us)
Sparse Core Ops, SparseCore 0:
  17.9 34.7 all-gather.2
  77.8 42.1 all-gather.4
  513.1 70.8 reduce-scatter.8
  586.3 15.3 reduce-scatter.6
  603.9 15.9 reduce-scatter.4
  622.4 67.2 reduce-scatter.10
  1200.4 64.2 all-reduce.31
where the time goes:
time: 1300 us; the launch traced here: 1280 us
  blocking collectives  465 us (36%)
  local copies, waits for them, and re-layouts  262 us (20%)
  waiting for transfers between devices  219 us (17%)
  matrix products  198 us (15%)
  other arithmetic  76.2 us (6%)
  starting transfers between devices  37 us (3%)
  between operations  18.6 us (1%)
    unnamed x3, blocking collectives  436 us
    unnamed x511, local copies, waits for them, and re-layouts  127 us
    reduce_scatter x4, waiting for transfers between devices, scatter_rows(): return lax.psum_scatter(x_in, GROUP_AXIS, scatter_dimension=0, tiled=True)  56.3 us
    psum x1, waiting for transfers between devices, device_step(): grad_flat = lax.psum(grad_flat, GROUP_AXIS)  54.4 us
    all_gather x2, waiting for transfers between devices, gather_rows(): return lax.all_gather(x_in, GROUP_AXIS, axis=0, tiled=True)  34.9 us
    all_gather x4, blocking collectives, gather_rows(): return lax.all_gather(x_in, GROUP_AXIS, axis=0, tiled=True)  28.9 us
  transfers between devices with their start and end apart: 13, of which 9 were waited for; matrix products, arithmetic and copies ran while one was open for 9% of the time, Pallas kernels for 0%

commit v1 on v0

v1 whole, which is shorter than its diff:
```python
import functools
import jax
import jax.numpy as jnp
from jax import lax
from jax.experimental import pallas as pl
from jax.experimental.pallas import tpu as pltpu
from jax.sharding import PartitionSpec as P

BATCH_AXIS = 'dp'
GROUP_AXIS = 'dap'
NORM_EPS = 1e-5
MASK_PENALTY = 1.0e9


def gather_rows(x_in):
    return lax.all_gather(x_in, GROUP_AXIS, axis=0, tiled=True)


F32 = jnp.float32
NOMINAL_BYTES = 4 << 20
GIGA = 1 << 30
BF16 = jnp.bfloat16
ROWS = 32
COLS = 128
CH = 128
HALF = 2 * CH
N_POS = ROWS * COLS
TRI_HEADS = 4
GRP = 4
OFFSETS = (1, 2, 3)
MESH_ID = pl.DeviceIdType.MESH
FOUR = 4
N_DEV = 16
WIDE = FOUR * COLS
TRI_DIM = 32
TRI_SCALE = TRI_DIM ** -0.5
STEP_ROWS = 4
CHUNK = STEP_ROWS * COLS


def dot_nn(a, b):
    return lax.dot_general(a, b, (((1,), (0,)), ((), ())), preferred_element_type=F32)


def dot_nt(a, b):
    return lax.dot_general(a, b, (((1,), (1,)), ((), ())), preferred_element_type=F32)


def dot_tn(a, b):
    return lax.dot_general(a, b, (((0,), (0,)), ((), ())), preferred_element_type=F32)


def cat0(xs):
    return jnp.concatenate(xs, axis=0)


def cat1(xs):
    return jnp.concatenate(xs, axis=1)


def loop(count, step, unroll=1):
    def body(i, carry):
        step(i)
        return carry

    lax.fori_loop(0, count, body, 0, unroll=unroll)


def col_mean(x):
    return jnp.mean(x, axis=0, keepdims=True)


def col_sum(x):
    return jnp.sum(x, axis=0, keepdims=True)


def row_mean(x):
    return jnp.mean(x, axis=-1, keepdims=True)


def softmax_cols(x):
    e = jnp.exp(x - jnp.max(x, axis=0, keepdims=True))
    return e * (1.0 / col_sum(e))


def col_norm(x):
    c = x - col_mean(x)
    r = lax.rsqrt(col_mean(c * c) + NORM_EPS)
    return c * r, r


def swap_all(x, split, join):
    return lax.all_to_all(x, GROUP_AXIS, split, join, tiled=True)


def norm_parts(x):
    c = x - row_mean(x)
    r = lax.rsqrt(row_mean(c * c) + NORM_EPS)
    return c * r, r


def norm_back(dn, nhat, r):
    return r * (dn - row_mean(dn) - nhat * row_mean(dn * nhat))


def chunk_ds(t, size=CHUNK):
    return pl.ds(pl.multiple_of(t * size, size), size)


def call(kernel, out_shape, scratch=(), flops=0, name=None, comm=None):
    n_out = len(out_shape)
    vm = pl.BlockSpec(memory_space=pltpu.VMEM)

    def run(*args):
        return pl.pallas_call(
            kernel, out_shape=tuple(out_shape), in_specs=[vm] * len(args), out_specs=tuple([vm] * n_out),
            scratch_shapes=list(scratch), name=name,
            compiler_params=pltpu.CompilerParams(collective_id=comm, has_side_effects=comm is not None),
            cost_estimate=pl.CostEstimate(flops=flops, bytes_accessed=NOMINAL_BYTES, transcendentals=0),
        )(*args)

    def run_one(*args):
        return run(*args)[0]

    return run if n_out > 1 else run_one


def sds(shape, dtype):
    return jax.ShapeDtypeStruct(shape, dtype)


def greet(me):
    sem = pltpu.get_barrier_semaphore()
    for off in OFFSETS:
        pl.semaphore_signal(sem, inc=1, device_id={GROUP_AXIS: lax.rem(me + off, GRP)}, device_id_type=MESH_ID)


def await_group():
    pl.semaphore_wait(pltpu.get_barrier_semaphore(), len(OFFSETS))


class Exchange:
    def __init__(self, me, src_at, dst_at, send_sem, recv_sem):
        self.copies = []
        for i, off in enumerate(OFFSETS):
            dest = lax.rem(me + off, GRP)
            self.copies.append(pltpu.make_async_remote_copy(
                src_ref=src_at(dest), dst_ref=dst_at(me), send_sem=send_sem.at[i], recv_sem=recv_sem.at[i],
                device_id={GROUP_AXIS: dest}, device_id_type=MESH_ID))
        for c in self.copies:
            c.start()

    def arrive(self):
        for c in self.copies:
            c.wait_recv()

    def leave(self):
        for c in self.copies:
            c.wait_send()


def own_rows(p, size=ROWS):
    return pl.ds(pl.multiple_of(p * size, size), size)


class Turn:
    def __init__(self, me, scr_ref, stage_ref, out_ref, send, recv):
        self.me, self.scr, self.stage, self.out, self.send, self.recv = me, scr_ref, stage_ref, out_ref, send, recv
        self.sent = []

    def half(self, n):
        lo = n * HALF_ROWS

        def cast(j):
            rows = self.scr[pl.ds(pl.multiple_of(j * ROWS + lo, HALF_ROWS), HALF_ROWS), :]
            self.stage[j // ROWS, lax.rem(j, ROWS), lo:lo + HALF_ROWS, :] = rows.astype(BF16)

        loop(COLS, cast, FOUR)
        part = (slice(None), slice(lo, lo + HALF_ROWS))
        self.sent.append(Exchange(self.me, lambda p: self.stage.at[(p, *part)], lambda m: self.out.at[(m, *part)], self.send.at[n], self.recv.at[n]))

    def finish(self):
        self.out[self.me] = self.stage[self.me]
        for ex in self.sent:
            ex.arrive()
            ex.leave()


TURNED = (GRP, ROWS, ROWS, CH)
HALF_ROWS = ROWS // 2


def turn_scratch():
    sems = pltpu.SemaphoreType.DMA((2, len(OFFSETS)))
    return [pltpu.VMEM((N_POS, CH), F32), pltpu.VMEM(TURNED, BF16), sems, sems]


def peer_sems():
    sems = pltpu.SemaphoreType.DMA((len(OFFSETS),))
    return [sems, sems]


ATT_STEP = 4
PACK = 8
BWD_STEP = 4


def fill_bias(bias_ref, mask_ref, bm_ref):
    mask = mask_ref[...]
    for h in range(TRI_HEADS):
        cols = slice(h * COLS, (h + 1) * COLS)
        bm_ref[:, cols] = bias_ref[:, cols].astype(F32).T + mask


def head_rows(x, h):
    return x[h * TRI_DIM:(h + 1) * TRI_DIM]


def spread_heads(xt):
    zero = jnp.zeros((TRI_DIM, COLS), xt.dtype)
    return cat1([
        cat0([head_rows(xt, h) if g == h else zero for g in range(TRI_HEADS)])
        for h in range(TRI_HEADS)])


def probs_of(k, q_wide, bm_ref):
    x = dot_nn(k, q_wide) * TRI_SCALE + bm_ref[...]
    return softmax_cols(x)


def heads_nn(xt, wide):
    return cat0([dot_nn(head_rows(xt, h), wide[:, h * COLS:(h + 1) * COLS]) for h in range(TRI_HEADS)])


def att_fwd_kernel(ending, z_ref, wbt_ref, mask_ref, wt_ref, wo_ref, o_ref, bias_ref, bm_ref, own_ref, send, recv, *rest):
    me = lax.axis_index(GROUP_AXIS)
    greet(me)
    turn = None if ending else Turn(me, rest[0], rest[1], o_ref, *rest[2:])

    def bias_step(t):
        nhat, _ = norm_parts(cat0([load_row(z_ref, t * PACK + r, ending) for r in range(PACK)]).astype(F32))
        nb = nhat.astype(BF16)
        b = [dot_nt(wbt_ref[...], nb[r * COLS:(r + 1) * COLS]) for r in range(PACK)]
        for h in range(TRI_HEADS):
            own_ref[chunk_ds(t, PACK), h * COLS:(h + 1) * COLS] = cat0([x[h:h + 1, :] for x in b])

    loop(ROWS // PACK, bias_step)
    bias_ref[own_rows(me), :] = own_ref[...].astype(BF16)
    await_group()
    ex = Exchange(me, lambda p: bias_ref.at[own_rows(me), :], lambda m: bias_ref.at[own_rows(m), :], send, recv)
    ex.arrive()
    fill_bias(bias_ref, mask_ref, bm_ref)

    def step(t):
        z = cat0([load_row(z_ref, t * ATT_STEP + r, ending) for r in range(ATT_STEP)]).astype(F32)
        nhat, _ = norm_parts(z)
        nb = nhat.astype(BF16)
        qt_all = dot_nt(wt_ref[:CH, :], nb)
        k_all = dot_nt(nb, wt_ref[CH:HALF, :]).astype(BF16)
        vg_all = dot_nt(wt_ref[HALF:, :], nb)
        gate = jax.nn.sigmoid(vg_all[CH:])
        outs = []
        for r in range(ATT_STEP):
            cols = slice(r * COLS, (r + 1) * COLS)
            q_wide = spread_heads(qt_all[:, cols]).astype(BF16)
            probs = probs_of(k_all[cols], q_wide, bm_ref).astype(BF16)
            outs.append(heads_nn(vg_all[:CH, cols].astype(BF16), probs))
        gated = (gate * cat1(outs)).astype(BF16)
        out = z + dot_tn(gated, wo_ref[...])
        for r in range(ATT_STEP):
            rows = slice(r * COLS, (r + 1) * COLS)
            if turn is None:
                o_ref[chunk_ds(t * ATT_STEP + r, COLS), :] = out[rows].astype(BF16)
            else:
                put_strided(turn.scr, t * ATT_STEP + r, out[rows])

    halves(ROWS // ATT_STEP, step, turn)
    ex.leave()


def halves(count, step, turn):
    if turn is None:
        loop(count, step)
        return
    loop(count // 2, step)
    turn.half(0)
    loop(count // 2, lambda t: step(t + count // 2))
    turn.half(1)
    turn.finish()


def att_fwd(z, w_b, mask_col, wt, w_o, ending):
    scr = [pltpu.VMEM((COLS, TRI_HEADS * COLS), F32), pltpu.VMEM((ROWS, TRI_HEADS * COLS), F32)] + peer_sems()
    out = sds((N_POS, CH) if ending else TURNED, BF16)
    return call(functools.partial(att_fwd_kernel, ending), [out, sds((COLS, TRI_HEADS * COLS), BF16)],
                scr if ending else scr + turn_scratch(), flops=3 * GIGA, name='att_fwd', comm=4 if ending else 3,
                )(z, w_b.T, mask_col, wt, w_o)


def att_bwd_kernel(z_blocked, dz_blocked, z_ref, dz_ref, bias_ref, mask_ref, wt_ref, wo_ref, dzo_ref, dwr_ref, dwo_ref, db_ref, bm_ref, acc_ref, dwqg_ref, dwkv_ref):
    fill_bias(bias_ref, mask_ref, bm_ref)
    acc_ref[...] = jnp.zeros_like(acc_ref)
    dwqg_ref[...] = jnp.zeros_like(dwqg_ref)
    dwkv_ref[...] = jnp.zeros_like(dwkv_ref)
    dwo_ref[...] = jnp.zeros_like(dwo_ref)

    def step(t):
        nhat, r_std = norm_parts(cat0([load_row(z_ref, t * BWD_STEP + r, z_blocked) for r in range(BWD_STEP)]).astype(F32))
        nb = nhat.astype(BF16)
        pt_all = dot_nt(wt_ref[...], nb)
        kv_all = dot_nt(nb, wt_ref[CH:3 * CH, :]).astype(BF16)
        gate = jax.nn.sigmoid(pt_all[3 * CH:])
        dz = cat0([load_row(dz_ref, t * BWD_STEP + r, dz_blocked) for r in range(BWD_STEP)])
        d_gated = dot_nt(wo_ref[...], dz)
        d_att = d_gated * gate
        outs, dqs, dkvs = [], [], []
        for r in range(BWD_STEP):
            cols = slice(r * COLS, (r + 1) * COLS)
            q_wide = spread_heads(pt_all[:CH, cols]).astype(BF16)
            do_wide = spread_heads(d_att[:, cols]).astype(BF16)
            p = probs_of(kv_all[cols, :CH], q_wide, bm_ref)
            pb = p.astype(BF16)
            outs.append(heads_nn(pt_all[2 * CH:3 * CH, cols].astype(BF16), pb))
            dp = dot_nn(kv_all[cols, CH:], do_wide)
            ds = p * (dp - col_sum(dp * p))
            acc_ref[...] += ds
            dsb = (ds * TRI_SCALE).astype(BF16)
            dqs.append(heads_nn(pt_all[CH:2 * CH, cols].astype(BF16), dsb))
            dkvs.append(cat1([dot_nt(dsb, q_wide), dot_nt(pb, do_wide)]).astype(BF16))
        o = cat1(outs)
        gated = (gate * o).astype(BF16)
        dgl = d_gated * o * gate * (1.0 - gate)
        dqg = cat0([cat1(dqs), dgl]).astype(BF16)
        dkv = cat0(dkvs)
        dwo_ref[...] += dot_nn(gated, dz)
        dwqg_ref[...] += dot_nn(dqg, nb)
        dwkv_ref[...] += dot_tn(nb, dkv)
        dn = dot_nn(dkv, wt_ref[CH:3 * CH, :]) + dot_tn(dqg[:CH], wt_ref[:CH, :]) + dot_tn(dqg[CH:], wt_ref[3 * CH:, :])
        dzo_ref[chunk_ds(t, BWD_STEP * COLS), :] = (dz.astype(F32) + norm_back(dn, nhat, r_std)).astype(BF16)

    loop(ROWS // BWD_STEP, step)
    for h in range(TRI_HEADS):
        cols = slice(h * COLS, (h + 1) * COLS)
        db_ref[:, cols] = acc_ref[:, cols].T
    for m in range(2):
        dwr_ref[pl.ds(3 * m, CH, stride=4), :] = dwqg_ref[m * CH:(m + 1) * CH, :].T
        dwr_ref[pl.ds(1 + m, CH, stride=4), :] = dwkv_ref[:, m * CH:(m + 1) * CH]


def att_bwd(z, dz, bias_all, mask_col, wt, w_o, z_blocked, dz_blocked):
    return call(functools.partial(att_bwd_kernel, z_blocked, dz_blocked),
                [sds((N_POS, CH), BF16), sds((4 * CH, CH), F32), sds((CH, CH), F32), sds((COLS, TRI_HEADS * COLS), F32)],
                [pltpu.VMEM((COLS, TRI_HEADS * COLS), F32), pltpu.VMEM((COLS, TRI_HEADS * COLS), F32),
                 pltpu.VMEM((2 * CH, CH), F32), pltpu.VMEM((CH, 2 * CH), F32)],
                flops=8 * GIGA, name='att_bwd')(z, dz, bias_all, mask_col, wt, w_o)


def bias_bwd_kernel(ending, z_ref, dz_ref, db_ref, wbt_ref, dzo_ref, dwt_ref, parts_ref, send, recv, *rest):
    me = lax.axis_index(GROUP_AXIS)
    greet(me)
    turn = Turn(me, rest[0], rest[1], dzo_ref, *rest[2:]) if ending else None
    dwt_ref[...] = jnp.zeros_like(dwt_ref)
    wbt = wbt_ref[...]
    await_group()
    ex = Exchange(me, lambda p: db_ref.at[own_rows(p), :], lambda m: parts_ref.at[m], send, recv)
    parts_ref[me] = db_ref[own_rows(me), :]
    ex.arrive()

    def step(t):
        block = sum(parts_ref[g, chunk_ds(t, PACK), :] for g in range(GRP))
        nhat, r_std = norm_parts(cat0([load_row(z_ref, t * PACK + r, ending) for r in range(PACK)]).astype(F32))
        nb = nhat.astype(BF16)
        dwt = jnp.zeros((TRI_HEADS, CH), F32)
        dns = []
        for r in range(PACK):
            db = cat0([block[r:r + 1, h * COLS:(h + 1) * COLS] for h in range(TRI_HEADS)]).astype(BF16)
            dwt += dot_nn(db, nb[r * COLS:(r + 1) * COLS])
            dns.append(dot_tn(db, wbt))
        out = dz_ref[chunk_ds(t, PACK * COLS), :].astype(F32) + norm_back(cat0(dns), nhat, r_std)
        if turn is None:
            dzo_ref[chunk_ds(t, PACK * COLS), :] = out.astype(BF16)
        else:
            for r in range(PACK):
                put_strided(turn.scr, t * PACK + r, out[r * COLS:(r + 1) * COLS])
        dwt_ref[...] += dwt

    halves(ROWS // PACK, step, turn)
    ex.leave()


def bias_bwd(z, dz, db, w_b, ending):
    scr = [pltpu.VMEM((GRP, ROWS, TRI_HEADS * COLS), F32)] + peer_sems()
    out = sds(TURNED if ending else (N_POS, CH), BF16)
    return call(functools.partial(bias_bwd_kernel, ending), [out, sds((TRI_HEADS, CH), F32)],
                scr + turn_scratch() if ending else scr, flops=GIGA, name='bias_bwd', comm=6 if ending else 5,
                )(z, dz, db, w_b.T)


SING_HEADS = 16


def trans_fwd_kernel(z_ref, wu_ref, wd_ref, wpt_ref, o_ref, b_ref, scr_ref):
    def step(t):
        z = z_ref[chunk_ds(t), :].astype(F32)
        nhat, _ = norm_parts(z)
        hid = dot_nn(nhat.astype(BF16), wu_ref[...])
        h1, h2 = hid[:, :4 * CH], hid[:, 4 * CH:]
        act = (jax.nn.sigmoid(h1) * h1 * h2).astype(BF16)
        out = (z + dot_nn(act, wd_ref[...])).astype(BF16)
        o_ref[chunk_ds(t), :] = out
        n5, _ = norm_parts(out.astype(F32))
        n5 = n5.astype(BF16)
        for r in range(STEP_ROWS):
            scr_ref[pl.ds(t * STEP_ROWS + r, SING_HEADS, stride=ROWS), :] = dot_nt(wpt_ref[...], n5[r * COLS:(r + 1) * COLS])

    loop(ROWS // STEP_ROWS, step)
    b_ref[...] = scr_ref[...].astype(BF16)


def trans_fwd(z, w_up, w_down, w_pb):
    return call(trans_fwd_kernel, [sds((N_POS, CH), BF16), sds((SING_HEADS * ROWS, COLS), BF16)],
                [pltpu.VMEM((SING_HEADS * ROWS, COLS), F32)],
                flops=2 * GIGA, name='trans_fwd')(z, w_up, w_down, w_pb.T)


def trans_bwd_kernel(z_ref, z5_ref, dz_ref, db_ref, wu_ref, wd_ref, wpt_ref, dzo_ref, dwr_ref, dwd_ref, dwpt_ref, dwu_ref, scr_ref):
    dwu_ref[...] = jnp.zeros_like(dwu_ref)
    dwd_ref[...] = jnp.zeros_like(dwd_ref)
    dwpt_ref[...] = jnp.zeros_like(dwpt_ref)
    scr_ref[...] = db_ref[...].astype(F32)

    def step(t):
        n5, r5 = norm_parts(z5_ref[chunk_ds(t), :].astype(F32))
        n5b = n5.astype(BF16)
        dn5 = []
        for r in range(STEP_ROWS):
            db = scr_ref[pl.ds(t * STEP_ROWS + r, SING_HEADS, stride=ROWS), :].astype(BF16)
            dwpt_ref[...] += dot_nn(db, n5b[r * COLS:(r + 1) * COLS])
            dn5.append(dot_tn(db, wpt_ref[...]))
        dz = dz_ref[chunk_ds(t), :].astype(F32) + norm_back(cat0(dn5), n5, r5)
        dzb = dz.astype(BF16)
        nhat, r_std = norm_parts(z_ref[chunk_ds(t), :].astype(F32))
        nb = nhat.astype(BF16)
        hid = dot_nn(nb, wu_ref[...])
        h1, h2 = hid[:, :4 * CH], hid[:, 4 * CH:]
        sg = jax.nn.sigmoid(h1)
        a1 = h1 * sg
        d_act = dot_nt(dzb, wd_ref[...])
        dwd_ref[...] += dot_tn((a1 * h2).astype(BF16), dzb)
        dhid = cat1([d_act * h2 * (sg + a1 * (1.0 - sg)), d_act * a1]).astype(BF16)
        dwu_ref[...] += dot_tn(nb, dhid)
        dn = dot_nt(dhid, wu_ref[...])
        dzo_ref[chunk_ds(t), :] = (dz + norm_back(dn, nhat, r_std)).astype(BF16)

    loop(ROWS // STEP_ROWS, step)
    store_rows(dwr_ref, dwu_ref[...], 8)


def trans_bwd(z, z5, dz, db, w_up, w_down, w_pb):
    return call(trans_bwd_kernel,
                [sds((N_POS, CH), BF16), sds((8 * CH, CH), F32), sds((4 * CH, CH), F32), sds((SING_HEADS, CH), F32)],
                [pltpu.VMEM((CH, 8 * CH), F32), pltpu.VMEM((SING_HEADS * ROWS, COLS), F32)],
                flops=6 * GIGA, name='trans_bwd')(z, z5, dz, db, w_up, w_down, w_pb.T)


def load_row(ref, i, blocked):
    if not blocked:
        return ref[chunk_ds(i, COLS), :]
    return cat0([ref[pl.ds(pl.multiple_of(s * ROWS * ROWS + i * ROWS, ROWS), ROWS), :] for s in range(GRP)])


def load_rows(ref, t, blocked):
    if not blocked:
        return ref[chunk_ds(t), :]
    return cat0([load_row(ref, t * STEP_ROWS + r, True) for r in range(STEP_ROWS)])


def put_strided(scr_ref, i, value):
    scr_ref[pl.ds(i, COLS, stride=ROWS), :] = value


def get_strided(scr_ref, i):
    return scr_ref[pl.ds(i, COLS, stride=ROWS), :]


def get_four(scr_ref, t):
    return cat1([get_strided(scr_ref, t * FOUR + r) for r in range(FOUR)])


def cast_out(scr_ref, o_ref):
    def step(t):
        o_ref[chunk_ds(t, 256), :] = scr_ref[chunk_ds(t, 256), :].astype(BF16)

    loop(N_POS // 256, step)


def group_rows(ref, c):
    return cat0([ref[s, chunk_ds(c, ROWS), :] for s in range(GRP)])


def make_proj(n_out, blocked):
    def kernel(z_ref, wt_ref, *rest):
        outs, scrs = rest[:n_out], rest[n_out:]

        def step(t):
            z = cat0([load_row(z_ref, t * FOUR + r, blocked) for r in range(FOUR)]).astype(F32)
            nhat, _ = norm_parts(z)
            pt = dot_nt(wt_ref[...], nhat.astype(BF16))
            for m in range(n_out):
                val = jax.nn.sigmoid(pt[(2 * m + 1) * CH:(2 * m + 2) * CH]) * pt[2 * m * CH:(2 * m + 1) * CH]
                for r in range(FOUR):
                    put_strided(scrs[m], t * FOUR + r, val[:, r * COLS:(r + 1) * COLS])

        loop(ROWS // FOUR, step)
        for m in range(n_out):
            cast_out(scrs[m], outs[m])

    return kernel


def mul_proj(z, wt, blocked=False):
    n_out = wt.shape[0] // (2 * CH)
    return call(make_proj(n_out, blocked), [sds((N_POS, CH), BF16)] * n_out, [pltpu.VMEM((N_POS, CH), F32)] * n_out,
                flops=GIGA, name='mul_proj')(z, wt)


def start_turn(rest):
    me = lax.axis_index(GROUP_AXIS)
    greet(me)
    out_ref, scr_ref, stage_ref, send, recv = rest
    return Turn(me, scr_ref, stage_ref, out_ref, send, recv)


def make_mix(outgoing):
    def kernel(left_ref, right_ref, z_ref, wg_ref, wo_ref, x_ref, o_ref, *rest):
        turn = start_turn(rest) if outgoing else None

        def mix(c):
            a = left_ref[chunk_ds(c, ROWS), :]
            b = group_rows(right_ref, c)
            x_ref[chunk_ds(c, ROWS), :] = dot_nt(a, b) if outgoing else dot_nn(a, b)

        loop(CH, mix, 8)

        def step(t):
            x = get_four(x_ref, t)
            xb = col_norm(x)[0].astype(BF16)
            z = z_ref[chunk_ds(t, WIDE), :].astype(F32)
            nhat, _ = norm_parts(z)
            gate = jax.nn.sigmoid(dot_nn(nhat.astype(BF16), wg_ref[...]))
            out = z + gate * dot_tn(xb, wo_ref[...])
            if outgoing:
                for r in range(FOUR):
                    put_strided(turn.scr, t * FOUR + r, out[r * COLS:(r + 1) * COLS])
            o_ref[chunk_ds(t, WIDE), :] = out.astype(BF16)

        if outgoing:
            await_group()
        halves(ROWS // FOUR, step, turn)

    return kernel


def mul_mix(left, right_all, z, w_gate, w_out, outgoing):
    outs = [sds((N_POS, COLS), F32), sds((N_POS, CH), BF16)]
    scr = []
    if outgoing:
        outs.append(sds(TURNED, BF16))
        scr = turn_scratch()
    return call(make_mix(outgoing), outs, scr, flops=3 * GIGA, name='mul_mix', comm=7 if outgoing else None)(left, right_all, z, w_gate, w_out)


def make_post_bwd(outgoing):
    def kernel(dz_ref, x_ref, z_ref, wg_ref, wo_ref, dx_ref, dgl_ref, dwo_ref, *rest):
        scr_ref, rest = rest[-1], rest[:-1]
        turn = start_turn(rest) if outgoing else None
        dwo_ref[...] = jnp.zeros_like(dwo_ref)

        def step(t):
            x = get_four(x_ref, t)
            xhat, r = col_norm(x)
            xb = xhat.astype(BF16)
            nhat, _ = norm_parts(z_ref[chunk_ds(t, WIDE), :].astype(F32))
            gate = jax.nn.sigmoid(dot_nn(nhat.astype(BF16), wg_ref[...]))
            du = dz_ref[chunk_ds(t, WIDE), :].astype(F32)
            dy = (gate * du).astype(BF16)
            dgl_ref[chunk_ds(t, WIDE), :] = (dot_tn(xb, wo_ref[...]) * du * gate * (1.0 - gate)).astype(BF16)
            dwo_ref[...] += dot_nn(xb, dy)
            dn = dot_nt(wo_ref[...], dy)
            dx = r * (dn - col_mean(dn) - xhat * col_mean(dn * xhat))
            for r in range(FOUR):
                part = dx[:, r * COLS:(r + 1) * COLS]
                put_strided(scr_ref, t * FOUR + r, part)
                if outgoing:
                    put_strided(turn.scr, t * FOUR + r, part.T)

        if outgoing:
            await_group()
        halves(ROWS // FOUR, step, turn)
        cast_out(scr_ref, dx_ref)

    return kernel


def mul_post_bwd(dz, x, z, w_gate, w_out, outgoing):
    outs = [sds((N_POS, COLS), BF16), sds((N_POS, CH), BF16), sds((CH, CH), F32)]
    scr = [pltpu.VMEM((N_POS, CH), F32)]
    if outgoing:
        outs.append(sds(TURNED, BF16))
        scr = turn_scratch() + scr
    return call(make_post_bwd(outgoing), outs, scr, flops=3 * GIGA, name='mul_post_bwd', comm=8 if outgoing else None)(dz, x, z, w_gate, w_out)


def make_pre_bwd(outgoing):
    def kernel(*refs):
        if outgoing:
            dx_ref, dxr_ref, left_ref, right_ref, z_ref, wt_ref, wg_ref, dgl_ref, dz_ref, dzo_ref, dwr_ref, dwg_ref, da_ref, db_ref, dwt_ref, scr_ref = refs

            def turn(j):
                put_strided(scr_ref, j, load_row(dxr_ref, j, True).astype(F32).T)

            loop(ROWS, turn, 2)

            def mix(c):
                da_ref[chunk_ds(c, ROWS), :] = dot_nn(dx_ref[chunk_ds(c, ROWS), :], group_rows(right_ref, c))
                db_ref[chunk_ds(c, ROWS), :] = dot_nn(scr_ref[chunk_ds(c, ROWS), :].astype(BF16), group_rows(left_ref, c))
        else:
            dx_ref, left_ref, right_ref, z_ref, wt_ref, wg_ref, dgl_ref, dz_ref, dzo_ref, dwr_ref, dwg_ref, da_ref, db_ref, dwt_ref = refs

            def mix(c):
                dx = group_rows(dx_ref, c)
                da_ref[chunk_ds(c, ROWS), :] = dot_nt(right_ref[chunk_ds(c, ROWS), :], dx)
                db_ref[chunk_ds(c, ROWS), :] = dot_nn(left_ref[chunk_ds(c, ROWS), :], dx)

        loop(CH, mix, 8)
        dwt_ref[...] = jnp.zeros_like(dwt_ref)
        dwg_ref[...] = jnp.zeros_like(dwg_ref)

        def step(t):
            nhat, r_std = norm_parts(z_ref[chunk_ds(t, WIDE), :].astype(F32))
            nb = nhat.astype(BF16)
            pt = dot_nt(wt_ref[...], nb)
            parts = []
            for m, d_ref in enumerate((da_ref, db_ref)):
                d = get_four(d_ref, t)
                val = pt[2 * m * CH:(2 * m + 1) * CH]
                sg = jax.nn.sigmoid(pt[(2 * m + 1) * CH:(2 * m + 2) * CH])
                dv = d * sg
                parts += [dv, dv * val * (1.0 - sg)]
            dpt = cat0(parts).astype(BF16)
            dgl = dgl_ref[chunk_ds(t, WIDE), :]
            dwt_ref[...] += dot_nn(dpt, nb)
            dwg_ref[...] += dot_tn(nb, dgl)
            dn = dot_tn(dpt, wt_ref[...]) + dot_nt(dgl, wg_ref[...])
            dzo_ref[chunk_ds(t, WIDE), :] = (dz_ref[chunk_ds(t, WIDE), :].astype(F32) + norm_back(dn, nhat, r_std)).astype(BF16)

        loop(ROWS // FOUR, step)
        for t in range(FOUR):
            dwr_ref[pl.ds(t, CH, stride=4), :] = dwt_ref[t * CH:(t + 1) * CH, :].T

    return kernel


def mul_pre_bwd(dx, left, right, z, wt, w_gate, dgl, dz, dx_turned=None):
    outgoing = dx_turned is not None
    args = [dx] + ([dx_turned] if outgoing else []) + [left, right, z, wt, w_gate, dgl, dz]
    scr = [pltpu.VMEM((N_POS, CH), F32)] * 2 + [pltpu.VMEM((4 * CH, CH), F32)]
    if outgoing:
        scr.append(pltpu.VMEM((N_POS, CH), F32))
    return call(make_pre_bwd(outgoing), [sds((N_POS, CH), BF16), sds((4 * CH, CH), F32), sds((CH, CH), F32)], scr,
                flops=6 * GIGA, name='mul_pre_bwd')(*args)


def gather_blocks(x):
    return lax.all_gather(x, GROUP_AXIS, axis=0)


def swap_rows(x_in):
    x_t = swap_all(x_in, 1, 0)
    return jnp.swapaxes(x_t, 0, 1).reshape(N_POS, CH)


def att_backward(z, dz, bias_all, mask_col, w_qkvg, w_tb, w_o, ending):
    dz_part, g_qkvg, g_out, db = att_bwd(z, dz, bias_all, mask_col, w_qkvg.T, w_o, ending, not ending)
    dz_new, g_bt = bias_bwd(z, dz_part, db, w_tb, ending)
    return dz_new.reshape(N_POS, CH), [g_qkvg, g_bt, g_out]


C_S = 384
SING_DIM = 24
SING_SCALE = SING_DIM ** -0.5
GRP_HEADS = SING_HEADS // GRP
GRP_W = GRP_HEADS * SING_DIM
TOKENS = 128


def store_rows(out_ref, value, tiles):
    n = value.shape[0]
    if tiles == 1:
        out_ref[...] = value
        return
    for t in range(tiles):
        out_ref[pl.ds(t, n, stride=tiles), :] = value[:, t * 128:(t + 1) * 128]


def sing_pre_kernel(s_ref, w_ref, qb_ref, qkv_ref, gate_ref):
    nhat, _ = norm_parts(s_ref[...].astype(F32))
    nb = nhat.astype(BF16)
    p_all = dot_nn(nb, w_ref[...])
    qkv_ref[:, :C_S] = (p_all[:, :C_S] + qb_ref[...].astype(F32)).astype(BF16)
    qkv_ref[:, C_S:] = p_all[:, C_S:3 * C_S].astype(BF16)
    gate_ref[...] = jax.nn.sigmoid(p_all[:, 3 * C_S:])


def sing_pre(s, w_qkvg, q_bias):
    return call(sing_pre_kernel, [sds((ROWS, 3 * C_S), BF16), sds((ROWS, C_S), F32)],
                flops=GIGA, name='sing_pre')(s, w_qkvg, q_bias[None, :])


def sing_stack(x):
    lane = lax.broadcasted_iota(jnp.int32, (TOKENS, GRP_W), 1) // SING_DIM
    x = x.astype(F32)
    return cat0([jnp.where(lane == h, x, 0.0) for h in range(GRP_HEADS)]).astype(BF16)


def sing_merge(parts):
    lane = lax.broadcasted_iota(jnp.int32, (TOKENS, GRP_W), 1) // SING_DIM
    out = jnp.where(lane == 0, parts[0], 0.0)
    for h in range(1, GRP_HEADS):
        out = jnp.where(lane == h, parts[h], out)
    return out


P_GATED, P_DMID, P_X2, P_DH, P_ACT, P_DOUT = 0, 384, 768, 1152, 4224, 5760
P_NS, P_DQ = 6144, 6528


P_ALL = 8064


def sing_fused_kernel(bias_ref, q_ref, k_ref, v_ref, gate_ref, s_ref, m_ref, wo_ref, wu_ref, wd_ref, wq_ref, ds_ref,
                      so_ref, dsi_ref, pk_ref, dbt_ref, qb_ref,
                      b_all, o_out, o_in, do_out, do_in, dq_out, dq_in, db_out, send, recv):
    me = lax.axis_index(GROUP_AXIS)
    greet(me)
    await_group()

    def block(ref):
        return lambda p: ref.at[p]

    def rows_block(ref):
        return lambda p: ref.at[pl.ds(pl.multiple_of(p * TOKENS, TOKENS), TOKENS), :]

    def start(i, src_at, dst_at):
        return Exchange(me, src_at, dst_at, send.at[i], recv.at[i])

    def lanes_of(x):
        return [x[:, g * GRP_W:(g + 1) * GRP_W] for g in range(GRP)]

    def rows_of(x):
        return [x[g * ROWS:(g + 1) * ROWS] for g in range(GRP)]

    stage = 0
    ex_bias = start(stage, rows_block(bias_ref), block(b_all))
    b_all[me] = bias_ref[pl.ds(pl.multiple_of(me * TOKENS, TOKENS), TOKENS), :]
    q, ks, vs = q_ref[...], sing_stack(k_ref[...]), sing_stack(v_ref[...])
    logits = dot_nt(ks, q) * SING_SCALE
    mask = m_ref[...]
    ex_bias.arrive()
    probs = []
    for h in range(GRP_HEADS):
        b = cat0([b_all[g, h * ROWS:(h + 1) * ROWS, :] for g in range(GRP)]).astype(F32)
        probs.append(softmax_cols(logits[h * TOKENS:(h + 1) * TOKENS] + b + mask))
    pb = [p.astype(BF16) for p in probs]
    for g, x in enumerate(rows_of(dot_tn(cat0(pb), vs))):
        o_out[g] = x
    stage += 1
    ex_o = start(stage, block(o_out), block(o_in))
    o_in[me] = o_out[me]
    gate, s = gate_ref[...], s_ref[...].astype(F32)
    ds = ds_ref[...]
    d_act = dot_nt(ds, wd_ref[...])
    n_s, r_s = norm_parts(s)
    ex_o.arrive()
    att = cat1([o_in[g] for g in range(GRP)])
    gated = (gate * att).astype(BF16)
    s_mid = (s + dot_nn(gated, wo_ref[...])).astype(BF16).astype(F32)
    nhat, r_std = norm_parts(s_mid)
    nb = nhat.astype(BF16)
    hid = dot_nn(nb, wu_ref[...])
    h1, h2 = hid[:, :4 * C_S], hid[:, 4 * C_S:]
    sg = jax.nn.sigmoid(h1)
    a1 = h1 * sg
    dhid = cat1([d_act * h2 * (sg + a1 * (1.0 - sg)), d_act * a1]).astype(BF16)
    dsm = ds.astype(F32) + norm_back(dot_nt(dhid, wu_ref[...]), nhat, r_std)
    dsmb = dsm.astype(BF16)
    d_gated = dot_nt(dsmb, wo_ref[...])
    for g, x in enumerate(lanes_of((d_gated * gate).astype(BF16))):
        do_out[g] = x
    stage += 1
    ex_do = start(stage, block(do_out), block(do_in))
    do_in[me] = do_out[me]
    act = (a1 * h2).astype(BF16)
    so_ref[...] = (s_mid + dot_nn(act, wd_ref[...])).astype(BF16)
    dgl = (d_gated * att * gate * (1.0 - gate)).astype(BF16)
    for at, x in ((P_GATED, gated), (P_DMID, dsmb), (P_X2, nb), (P_DH, dhid), (P_ACT, act), (P_DOUT, ds), (P_NS, n_s.astype(BF16))):
        pk_ref[:, at:at + x.shape[1]] = x
    ex_do.arrive()
    do = cat0([do_in[g] for g in range(GRP)])
    dp = dot_nt(vs, do)
    dsb, dk, dv = [], [], []
    for h in range(GRP_HEADS):
        d = dp[h * TOKENS:(h + 1) * TOKENS]
        dlog = probs[h] * (d - col_sum(probs[h] * d))
        for g, x in enumerate(rows_of(dlog.astype(BF16))):
            db_out[g, h * ROWS:(h + 1) * ROWS, :] = x
        dsb.append((dlog * SING_SCALE).astype(BF16))
    stage += 1
    ex_db = start(stage, block(db_out), rows_block(dbt_ref))
    rows_block(dbt_ref)(me)[...] = db_out[me]
    for h in range(GRP_HEADS):
        dk.append(dot_nn(dsb[h], q))
        dv.append(dot_nn(pb[h], do))
    for t, x in enumerate((dot_tn(cat0(dsb), ks), sing_merge(dk), sing_merge(dv))):
        for g, y in enumerate(rows_of(x.astype(BF16))):
            dq_out[g, t] = y
    stage += 1
    ex_dq = start(stage, block(dq_out), block(dq_in))
    dq_in[me] = dq_out[me]
    ex_dq.arrive()
    dp_all = cat1([dq_in[g, t] for t in range(3) for g in range(GRP)] + [dgl])
    pk_ref[:, P_DQ:] = dp_all
    dsi_ref[...] = (dsm + norm_back(dot_nt(dp_all, wq_ref[...]), n_s, r_s)).astype(BF16)
    qb = col_sum(dp_all[:, :C_S].astype(F32))
    qb_ref[...] = cat0([qb[:, t * CH:(t + 1) * CH] for t in range(3)])
    ex_db.arrive()
    for ex in (ex_bias, ex_o, ex_do, ex_db, ex_dq):
        ex.leave()


def sing_fused(*args):
    vm = pl.BlockSpec(memory_space=pltpu.VMEM)
    dma = pltpu.SemaphoreType.DMA
    piece = (GRP, ROWS, GRP_W)
    triple = (GRP, 3, ROWS, GRP_W)
    outs = (sds((ROWS, C_S), BF16), sds((ROWS, C_S), BF16), sds((ROWS, P_ALL), BF16), sds((GRP * TOKENS, TOKENS), BF16), sds((3, CH), F32))
    sems = dma((5, len(OFFSETS)))
    return pl.pallas_call(
        sing_fused_kernel, out_shape=outs, in_specs=[vm] * len(args), out_specs=(vm,) * len(outs),
        scratch_shapes=[pltpu.VMEM((GRP, TOKENS, TOKENS), BF16), pltpu.VMEM(piece, F32), pltpu.VMEM(piece, F32),
                        pltpu.VMEM(piece, BF16), pltpu.VMEM(piece, BF16), pltpu.VMEM(triple, BF16), pltpu.VMEM(triple, BF16),
                        pltpu.VMEM((GRP, TOKENS, TOKENS), BF16), sems, sems],
        compiler_params=pltpu.CompilerParams(collective_id=2, has_side_effects=True), name='sing_fused',
        cost_estimate=pl.CostEstimate(flops=2 * GIGA, bytes_accessed=NOMINAL_BYTES, transcendentals=0),
    )(*args)


QKVG, PROJ, UP, DOWN = (4360, 12, 3), (8987, 3, 1), (10139, 24, 6), (19355, 3, 3)
KEPT = (((QKVG, 0, 136),), ((QKVG, 128, 384), (PROJ, 0, 384), (UP, 0, 80)), ((UP, 72, 328),), ((UP, 320, 384), (DOWN, 0, 384)))
W_ROWS = 1632


def kept_blocks(d):
    at = 0
    for weight, lo, hi in KEPT[d]:
        for t in range(weight[-1]):
            yield weight, lo, hi, t, at
            at += hi - lo


def sing_wgrad_kernel(m_ref, o_ref):
    k = lax.axis_index(GROUP_AXIS)

    def lanes(base, tiles, idx):
        width = tiles * CH
        return m_ref[:, pl.ds(pl.multiple_of(base + idx * width, CH), width)]

    def whole(base):
        return m_ref[:, base:base + C_S]

    grads = {
        QKVG: dot_tn(whole(P_NS), lanes(P_DQ, QKVG[-1], k)),
        PROJ: dot_tn(whole(P_GATED), lanes(P_DMID, 1, jnp.minimum(k, 2))),
        UP: dot_tn(whole(P_X2), lanes(P_DH, UP[-1], k)),
        DOWN: dot_tn(lanes(P_ACT, DOWN[-1], k), whole(P_DOUT)),
    }
    for d in range(GRP):
        end = 0
        for weight, lo, hi, t, at in kept_blocks(d):
            end = at + hi - lo
            o_ref[d, at:end, :] = grads[weight][lo:hi, t * CH:(t + 1) * CH]
        if end < W_ROWS:
            o_ref[d, end:, :] = jnp.zeros((W_ROWS - end, CH), F32)


def sing_wgrad(packed_all):
    return call(sing_wgrad_kernel, [sds((4, W_ROWS, 128), F32)], flops=GIGA, name='sing_wgrad')(packed_all)


PART = 766816
OUT_ROWS = 5992
SHIFT_ROWS = 56
SMALL_AT = ((0, 2048, 4, 24), (0, 2692, 4, 32), (1, 2978, 3, 0), (1, 2981, 16, 8))
LATE_ROWS = 1536
PIECE = LATE_ROWS // 16
LATE_SIZES = (512, 128, 128, 512, 128, 128)
EARLY_SIZES = (512, 128, 512, 128, 1024, 512)
EARLY_AT = (1536, 2052, 2180, 2696, 2824, 3848)


def finish_kernel(*refs):
    late_refs, (g_ref, p_ref, small_ref, o_ref, w_ref, x_ref, buf_ref, sum_ref, copy_sem, send1, recv1, send2, recv2) = refs[:6], refs[6:]
    d, k = lax.axis_index(BATCH_AXIS), lax.axis_index(GROUP_AXIS)
    me = 4 * d + k
    row, fills = 0, []
    for i, ref in enumerate(late_refs):
        fills.append(pltpu.make_async_copy(ref, x_ref.at[pl.ds(row, LATE_SIZES[i]), :], copy_sem.at[i]))
        row += LATE_SIZES[i]
    for c in fills:
        c.start()
    barrier = pltpu.get_barrier_semaphore()

    def device(p):
        return {BATCH_AXIS: p // 4, GROUP_AXIS: lax.rem(p, 4)}

    def piece(p):
        return pl.ds(pl.multiple_of(p * PIECE, PIECE), PIECE)

    for off in range(1, N_DEV):
        pl.semaphore_signal(barrier, inc=1, device_id=device(lax.rem(me + off, N_DEV)), device_id_type=MESH_ID)
    for c in fills:
        c.wait()
    pl.semaphore_wait(barrier, 15)
    first = []
    for off in range(1, N_DEV):
        p = lax.rem(me + off, N_DEV)
        c = pltpu.make_async_remote_copy(
            src_ref=x_ref.at[piece(p), :], dst_ref=buf_ref.at[off - 1], send_sem=send1.at[off - 1], recv_sem=recv1.at[off - 1],
            device_id=device(p), device_id_type=MESH_ID)
        c.start()
        first.append(c)

    def lay_out(part):
        begin = part * PART // 128
        lanes_off = part * PART % 128
        for weight, lo, hi, t, at in kept_blocks(part):
            base, tiles, own = weight
            for k in range(GRP):
                if weight == DOWN:
                    first_row = base + own * CH * k * tiles + t - begin
                else:
                    first_row = base + own * k + t - begin
                    if own * k + t >= tiles:
                        continue
                r0 = max(lo, -(first_row // tiles))
                r1 = min(hi, (OUT_ROWS - first_row) // tiles + 1)
                src = at + r0 - lo
                w_ref[pl.ds(first_row + r0 * tiles, r1 - r0, stride=tiles), :] = g_ref[k, src:src + r1 - r0, :]
        if part:
            lane = lax.broadcasted_iota(jnp.int32, (SHIFT_ROWS, CH), 1)
            for i in range(OUT_ROWS // SHIFT_ROWS):
                rows = slice(i * SHIFT_ROWS, (i + 1) * SHIFT_ROWS)
                a = pltpu.roll(w_ref[rows, :], CH - lanes_off, 1)
                b = pltpu.roll(w_ref[rows.start + 1:rows.stop + 1, :], CH - lanes_off, 1)
                o_ref[rows, :] = jnp.where(lane < CH - lanes_off, a, b)
        else:
            o_ref[LATE_ROWS:, :] = w_ref[LATE_ROWS:OUT_ROWS, :]

    for part in range(GRP):
        @pl.when(d == part)
        def _():
            if part == 0:
                src = 0
                for n, at in zip(EARLY_SIZES, EARLY_AT):
                    w_ref[at:at + n, :] = p_ref[src:src + n, :]
                    src += n
            for own, at, n, src in SMALL_AT:
                if own == part:
                    w_ref[at:at + n, :] = small_ref[src:src + n, :]
            lay_out(part)

    for c in first:
        c.wait_recv()
    total = x_ref[piece(me), :]
    for i in range(15):
        total += buf_ref[i]
    sum_ref[...] = total

    def second(k, src):
        return pltpu.make_async_remote_copy(
            src_ref=sum_ref, dst_ref=o_ref.at[piece(src), :], send_sem=send2.at[k], recv_sem=recv2.at[src],
            device_id={BATCH_AXIS: 0, GROUP_AXIS: k}, device_id_type=MESH_ID)

    for k in range(FOUR):
        @pl.when(me != k)
        def _():
            second(k, me).start()

    @pl.when(d == 0)
    def _():
        o_ref[piece(me), :] = total

    for k in range(FOUR):
        @pl.when(me != k)
        def _():
            second(k, me).wait_send()

    @pl.when(d == 0)
    def _():
        for off in range(1, N_DEV):
            second(0, lax.rem(me + off, N_DEV)).wait_recv()

    for c in first:
        c.wait_send()


def finish(late, g_all, early, small):
    vm = pl.BlockSpec(memory_space=pltpu.VMEM)
    dma = pltpu.SemaphoreType.DMA
    return pl.pallas_call(
        finish_kernel, out_shape=sds((OUT_ROWS, 128), F32), in_specs=[vm] * 9, out_specs=vm,
        scratch_shapes=[pltpu.VMEM((6016, 128), F32), pltpu.VMEM((LATE_ROWS, 128), F32), pltpu.VMEM((15, PIECE, 128), F32),
                        pltpu.VMEM((PIECE, 128), F32), dma((6,)), dma((15,)), dma((15,)), dma((4,)), dma((16,))],
        compiler_params=pltpu.CompilerParams(collective_id=1, has_side_effects=True), name='finish',
        cost_estimate=pl.CostEstimate(flops=GIGA, bytes_accessed=NOMINAL_BYTES, transcendentals=0),
    )(*late, g_all, early, small)


def flat_cols(x):
    return x.T.reshape(x.shape)


def to_heads(x, n):
    x = x.reshape(ROWS, n, GRP, GRP_W)
    x = swap_all(jnp.transpose(x, (2, 1, 0, 3)), 0, 0)
    x = jnp.transpose(x, (1, 0, 2, 3)).reshape(n, TOKENS, GRP_W)
    return [x[t] for t in range(n)]


def device_step(single_blk, pair_blk, mask_blk, d_single_blk, d_pair_blk, *weights):
    (w1_in, w1_gate, w1_out, w2_in, w2_gate, w2_out, st_qkvg, st_bias, st_proj, en_qkvg,
     en_bias, en_proj, p_up, p_down, s_qkvg, s_qbias, s_pbias, s_proj, s_up, s_down) = weights
    s_rows = single_blk[0]
    z_zero = pair_blk[0].reshape(N_POS, CH)
    mask_bias = (mask_blk[0].astype(jnp.float32) - 1.0) * MASK_PENALTY
    mask_col = mask_bias[:, None]
    wt_out, wt_in = w1_in.T, w2_in.T
    right_out = mul_proj(z_zero, wt_out[HALF:])
    right_out_all = gather_blocks(right_out)
    left_out = mul_proj(z_zero, wt_out[:HALF])
    x_out, z_one, z_one_turned = mul_mix(left_out, right_out_all, z_zero, w1_gate, w1_out, True)
    right_in = mul_proj(z_one, wt_in[HALF:])
    right_in_all = gather_blocks(right_in)
    zt_one = z_one_turned.reshape(N_POS, CH)
    left_in = mul_proj(z_one, wt_in[:HALF])
    left_in_t = mul_proj(zt_one, wt_in[:HALF], True)
    x_in, z_two = mul_mix(left_in_t, right_in_all, z_one, w2_gate, w2_out, False)
    left_out, z_two = lax.optimization_barrier((left_out, z_two))
    left_out_all = gather_blocks(left_out)
    z_three_turned, bias_st = att_fwd(z_two, st_bias, mask_col, st_qkvg.T, st_proj, False)
    zt_three = z_three_turned.reshape(N_POS, CH)
    d_pair, zt_three = lax.optimization_barrier((d_pair_blk[0], zt_three))
    dzt_out = swap_rows(d_pair)
    zt_four, bias_en = att_fwd(zt_three, en_bias, mask_col, en_qkvg.T, en_proj, True)
    s_qkv, s_gate = sing_pre(s_rows, s_qkvg, s_qbias)
    qkv_heads = to_heads(s_qkv, 3)
    zt_four, left_out_all, dzt_out, qkv_heads = lax.optimization_barrier((zt_four, left_out_all, dzt_out, qkv_heads))
    zt_five, bias_t = trans_fwd(zt_four, p_up, p_down, s_pbias)
    s_out, ds_in, packed, d_bias_t, g_qb = sing_fused(
        bias_t, *qkv_heads, s_gate, s_rows, mask_col, s_proj, s_up, s_down, s_qkvg, d_single_blk[0])
    packed, zt_five, d_bias_t, dzt_out = lax.optimization_barrier((packed, zt_five, d_bias_t, dzt_out))
    packed_all = gather_rows(packed)
    z_five = swap_rows(zt_five.reshape(ROWS, COLS, CH))
    dzt_four, g_pup, g_pdown, g_pbt = trans_bwd(zt_four, zt_five, dzt_out, d_bias_t, p_up, p_down, s_pbias)
    windows = sing_wgrad(packed_all)
    dzt_four, windows = lax.optimization_barrier((dzt_four, windows))
    piece = lax.psum_scatter(windows.reshape(4 * W_ROWS, 128), BATCH_AXIS, scatter_dimension=0, tiled=True)
    dz_three, end_grads = att_backward(zt_three, dzt_four, bias_en, mask_col, en_qkvg, en_bias, en_proj, True)
    dz_three, piece = lax.optimization_barrier((dz_three, piece))
    pieces = gather_rows(piece)
    dz_two, start_grads = att_backward(z_two, dz_three, bias_st, mask_col, st_qkvg, st_bias, st_proj, False)
    dz_two, pieces, z_five = lax.optimization_barrier((dz_two, pieces, z_five))
    dx_in, dgl_in, g_in_out = mul_post_bwd(dz_two, x_in, z_one, w2_gate, w2_out, False)
    dx_all = gather_blocks(dx_in)
    five = jnp.zeros((5, 128), F32)
    early = cat0([start_grads[0], start_grads[2], end_grads[0], end_grads[2], g_pup, g_pdown, g_qb, five, g_pbt,
                             start_grads[1], five[:4], end_grads[1], five[:4]])
    dx_all, early = lax.optimization_barrier((dx_all, early))
    early = lax.psum(early, (BATCH_AXIS, GROUP_AXIS))
    tail = early[sum(EARLY_SIZES):]
    small = cat0([tail[:8], flat_cols(tail[8:24]), flat_cols(tail[24:28]), five[:4], flat_cols(tail[32:36]), five[:4]])
    dz_one, g_in_in, g_in_gate = mul_pre_bwd(dx_all, left_in, right_in, z_one, wt_in, w2_gate, dgl_in, dz_two)
    dx_out, dgl_out, g_out_out, dx_turned = mul_post_bwd(dz_one, x_out, z_zero, w1_gate, w1_out, True)
    dz_zero, g_out_in, g_out_gate = mul_pre_bwd(dx_out, left_out_all, right_out_all, z_zero, wt_out, w1_gate, dgl_out, dz_one, dx_turned.reshape(N_POS, CH))
    late = (g_out_in, g_out_gate, g_out_out, g_in_in, g_in_gate, g_in_out)
    grad_flat = finish(late, pieces.reshape(4, W_ROWS, 128), early, small).reshape(-1)[:PART]
    z_five = z_five.reshape(ROWS, COLS, CH)
    dz_zero = dz_zero.reshape(ROWS, COLS, CH)
    return s_out[None], z_five[None], ds_in[None], dz_zero[None], grad_flat


def solution(mesh):
    spec_single = P(BATCH_AXIS, GROUP_AXIS, None)
    spec_pair = P(BATCH_AXIS, GROUP_AXIS, None, None)
    spec_mask = P(BATCH_AXIS, None)

    def block_fn(single_rep, pair_rep, token_mask, d_single_out, d_pair_out, *weights):
        in_specs = (spec_single, spec_pair, spec_mask, spec_single, spec_pair) + tuple(P() for w_item in weights)
        out_specs = (spec_single, spec_pair, spec_single, spec_pair, P(BATCH_AXIS))
        mapped = jax.shard_map(device_step, mesh=mesh, in_specs=in_specs, out_specs=out_specs, check_vma=False)
        return mapped(single_rep, pair_rep, token_mask, d_single_out, d_pair_out, *weights)

    return block_fn
```

time: 1300 us -> 555 us (0.43); the launches traced: 1280 us -> 547 us
  blocking collectives: 465 us -> 24.8 us
  Pallas kernels: 0 us -> 390 us
  local copies, waits for them, and re-layouts: 262 us -> 29.6 us
  matrix products: 198 us -> 0 us
  waiting for transfers between devices: 219 us -> 80 us
  other arithmetic: 76.2 us -> 0.01 us
  starting transfers between devices: 37 us -> 8.03 us
    unnamed x3 -> x0, blocking collectives: 436 us -> none
    pallas_call x0 -> x23, Pallas kernels: none -> 390 us  [the longest x21 340 us: run(): pl.pallas_call(kernel, out_shape=tuple(out_shape), in_specs=[vm] * len(ar...]
    dot_general x79 -> x0, matrix products: 181 us -> none  [the longest x6 24.9 us: att_pre(): proj_all = jnp.dot(normed, w_qkvg, preferred_element_type=jnp.float32)]
    unnamed x511 -> x50, local copies, waits for them, and re-layouts: 127 us -> 9.31 us
    all_to_all x6 -> x2, waiting for transfers between devices: 73.7 us -> 0.01 us  [swap_all(): return lax.all_to_all(x, GROUP_AXIS, split, join, tiled=True)]
    all_gather x0 -> x4, waiting for transfers between devices: none -> 71.5 us  [gather_blocks(): return lax.all_gather(x, GROUP_AXIS, axis=0)]
    reduce_scatter x4 -> x1, waiting for transfers between devices: 56.3 us -> 0.02 us  [device_step(): lax.psum_scatter(windows.reshape(4 * W_ROWS, 128), BATCH_AXIS, scatter_di...]
    psum x1, waiting for transfers between devices: 54.4 us -> 6.08 us  [device_step(): early = lax.psum(early, (BATCH_AXIS, GROUP_AXIS))]
  transfers between devices with their start and end apart: 13 -> 10, of which waited for: 9 -> 5; matrix products, arithmetic and copies ran while one was open for 9% -> 3% of each run, Pallas kernels for 0% -> 48%
where the time goes in v1:
time: 555 us; the launch traced here: 547 us
  Pallas kernels  390 us (70%)
  waiting for transfers between devices  80 us (14%)
  local copies, waits for them, and re-layouts  29.6 us (5%)
  blocking collectives  24.8 us (4%)
  between operations  15 us (3%)
  starting transfers between devices  8.03 us (1%)
    pallas_call x21, Pallas kernels, run(): pl.pallas_call(kernel, out_shape=tuple(out_shape), in_specs=[vm] * len(ar...  340 us
    all_gather x4, waiting for transfers between devices, gather_blocks(): return lax.all_gather(x, GROUP_AXIS, axis=0)  71.5 us
    pallas_call x1, Pallas kernels, finish(): pl.pallas_call(finish_kernel, out_shape=sds((OUT_ROWS, 128), F32), in_spe...  29.8 us
    all_to_all x1, blocking collectives, swap_all(): return lax.all_to_all(x, GROUP_AXIS, split, join, tiled=True)  24.8 us
    pallas_call x1, Pallas kernels, sing_fused(): pl.pallas_call(sing_fused_kernel, out_shape=outs, in_specs=[vm] * len(arg...  19.8 us
  transfers between devices with their start and end apart: 10, of which 5 were waited for; matrix products, arithmetic and copies ran while one was open for 3% of the time, Pallas kernels for 48%

profile of v1, /device:TPU:1, one launch (start us, length us, event | category | flops | bytes accessed | tf_op | source)
XLA Modules:
  0.0 547.5 jit_solution(14596339796786780195)
XLA Ops:
  7.2 1.0 copy.75
  8.2 0.7 fusion.1
  8.9 7.1 %mul_proj.6 = bf16[4096,128]{1,0:T(8,128)(2,1)} custom-call(bf16[4096,128]{1,0:T(8,128)(2,1)} %bitcast.88, bf16[256,128]{1,0:T(8,128)(2,1)} %get-tuple-element.149.wt_ref), custom_call_target="tpu_custom_call" | custom-call | flops 1073741824 | bytes 4194304 | tf_op jit(solution)/shard_map/mul_proj/pallas_call | solution.py:115
  16.3 7.1 %mul_proj.5.left_ref = bf16[4096,128]{1,0:T(8,128)(2,1)} custom-call(bf16[4096,128]{1,0:T(8,128)(2,1)} %bitcast.89, bf16[256,128]{1,0:T(8,128)(2,1)} %get-tuple-element.150.wt_ref), custom_call_target="tpu_custom_call" | custom-call | flops 1073741824 | bytes 4194304 | tf_op jit(solution)/shard_map/mul_proj/pallas_call | solution.py:115
  24.1 26.9 %all-gather.15.cloned.1.call-done = bf16[16384,128]{1,0:T(8,128)(2,1)} async-done(((bf16[4096,128]{1,0:T(8,128)(2,1)}), bf16[16384,128]{1,0:T(8,128)(2,1)}) %all-gather.15.cloned.1.call-update) | async-done | bytes 4194320 | tf_op jit(solution)/shard_map/all_gather | solution.py:675
  51.0 25.2 %mul_mix.2 = (f32[4096,128]{1,0:T(8,128)}, bf16[4096,128]{1,0:T(8,128)(2,1)}, bf16[4,32,32,128]{3,2,1,0:T(8,128)(2,1)}) custom-call(bf16[4096,128]{1,0:T(8,128)(2,1)} %mul_proj.5.left_ref, bf16[4,4096,128]{2,1,0:T(8,128)(2,1)} %bitcast.83, bf16[4096,128]{1,0:T(8,128)(2,1)} %bitcast.90, bf16[128,128]{1,0:T(8,128)(2,1)} %refs_6_.1, bf16[128,128]{1,0:T(8,128)(2,1)} %wo_ref.17), custom_call_target="tpu_custom_call" | custom-call | flops 3221225472 | bytes 4194304 | tf_op jit(solution)/shard_map/mul_mix/pallas_call | solution.py:115
  76.2 7.1 %mul_proj.8.refs_2_ = bf16[4096,128]{1,0:T(8,128)(2,1)} custom-call(bf16[4096,128]{1,0:T(8,128)(2,1)} %get-tuple-element.76.z_ref.refs_3_, bf16[256,128]{1,0:T(8,128)(2,1)} %get-tuple-element.147.wt_ref), custom_call_target="tpu_custom_call" | custom-call | flops 1073741824 | bytes 4194304 | tf_op jit(solution)/shard_map/mul_proj/pallas_call | solution.py:115
  83.4 7.1 %mul_proj.7.left_ref = bf16[4096,128]{1,0:T(8,128)(2,1)} custom-call(bf16[4096,128]{1,0:T(8,128)(2,1)} %bitcast.107, bf16[256,128]{1,0:T(8,128)(2,1)} %get-tuple-element.148.wt_ref), custom_call_target="tpu_custom_call" | custom-call | flops 1073741824 | bytes 4194304 | tf_op jit(solution)/shard_map/mul_proj/pallas_call | solution.py:115
  90.5 26.4 %all-gather.17.cloned.1.call-done = bf16[16384,128]{1,0:T(8,128)(2,1)} async-done(((bf16[4096,128]{1,0:T(8,128)(2,1)}), bf16[16384,128]{1,0:T(8,128)(2,1)}) %all-gather.17.cloned.1.call-update) | async-done | bytes 4194320 | tf_op jit(solution)/shard_map/all_gather | solution.py:675
  116.9 12.1 %mul_mix.3 = (f32[4096,128]{1,0:T(8,128)}, bf16[4096,128]{1,0:T(8,128)(2,1)}) custom-call(bf16[4096,128]{1,0:T(8,128)(2,1)} %mul_proj.7.left_ref, bf16[4,4096,128]{2,1,0:T(8,128)(2,1)} %bitcast.87, bf16[4096,128]{1,0:T(8,128)(2,1)} %get-tuple-element.76.z_ref.refs_3_, bf16[128,128]{1,0:T(8,128)(2,1)} %refs_5_.1, bf16[128,128]{1,0:T(8,128)(2,1)} %wo_ref.16), custom_call_target="tpu_custom_call" | custom-call | flops 3221225472 | bytes 4194304 | tf_op jit(solution)/shard_map/mul_mix/pallas_call | solution.py:115
  129.6 2.5 sing_pre.1
  132.1 1.0 reshape.83
  133.1 0.7 copy.97
  133.8 3.5 all-to-all-start.1
  137.3 0.7 copy.78.mask_ref.m_ref
  138.1 0.8 copy.77
  138.8 1.6 copy.96
  140.5 34.1 %att_fwd.2 = (bf16[4,32,32,128]{3,2,1,0:T(8,128)(2,1)}, bf16[128,512]{1,0:T(8,128)(2,1)}) custom-call(bf16[4096,128]{1,0:T(8,128)(2,1)} %get-tuple-element.78.z_ref, bf16[4,128]{1,0:T(4,128)(2,1)} %bitcast.100, f32[128,1]{1,0:T(8,128)} %copy.78.mask_ref.m_ref, bf16[512,128]{1,0:T(8,128)(2,1)} %bitcast.74, bf16[128,128]{1,0:T(8,128)(2,1)} %wo_ref.15), custom_call_target="tpu_custom_call" | custom-call | flops 3221225472 | bytes 4194304 | tf_op jit(solution)/shard_map/att_fwd/pallas_call | solution.py:115
  174.6 3.5 all-to-all-start
  178.4 0.8 copy.79
  179.8 26.8 %att_fwd.3 = (bf16[4096,128]{1,0:T(8,128)(2,1)}, bf16[128,512]{1,0:T(8,128)(2,1)}) custom-call(bf16[4096,128]{1,0:T(8,128)(2,1)} %bitcast.102, bf16[4,128]{1,0:T(4,128)(2,1)} %bitcast.98, f32[128,1]{1,0:T(8,128)} %copy.78.mask_ref.m_ref, bf16[512,128]{1,0:T(8,128)(2,1)} %bitcast.76, bf16[128,128]{1,0:T(8,128)(2,1)} %wo_ref.14), custom_call_target="tpu_custom_call" | custom-call | flops 3221225472 | bytes 4194304 | tf_op jit(solution)/shard_map/att_fwd/pallas_call | solution.py:115
  206.6 1.1 copy.81
  207.7 11.3 %trans_fwd.1 = (bf16[4096,128]{1,0:T(8,128)(2,1)}, bf16[512,128]{1,0:T(8,128)(2,1)}) custom-call(bf16[4096,128]{1,0:T(8,128)(2,1)} %get-tuple-element.85.z_ref, bf16[128,1024]{1,0:T(8,128)(2,1)} %wu_ref.5, bf16[512,128]{1,0:T(8,128)(2,1)} %wd_ref.5, bf16[16,128]{1,0:T(8,128)(2,1)} %bitcast.96), custom_call_target="tpu_custom_call" | custom-call | flops 2147483648 | bytes 4194304 | tf_op jit(solution)/shard_map/trans_fwd/pallas_call | solution.py:115
  219.1 19.8 %sing_fused.1 = (bf16[32,384]{1,0:T(8,128)(2,1)}, bf16[32,384]{1,0:T(8,128)(2,1)}, bf16[32,8064]{1,0:T(8,128)(2,1)}, bf16[512,128]{1,0:T(8,128)(2,1)}, f32[3,128]{1,0:T(4,128)}) custom-call(bf16[512,128]{1,0:T(8,128)(2,1)} %get-tuple-element.86.bias_ref, bf16[128,96]{1,0:T(8,128)(2,1)} %bitcast.80, bf16[128,96]{1,0:T(8,128)(2,1)} %bitcast.79, ...), custom_call_target="tpu_custom_call" | custom-call | flops 2147483648 | bytes 4194304 | tf_op jit(solution)/shard_map/sing_fused/pallas_call | solution.py:848
  239.0 19.4 %trans_bwd.1 = (bf16[4096,128]{1,0:T(8,128)(2,1)}, f32[1024,128]{1,0:T(8,128)}, f32[512,128]{1,0:T(8,128)}, f32[16,128]{1,0:T(8,128)}) custom-call(bf16[4096,128]{1,0:T(8,128)(2,1)} %get-tuple-element.85.z_ref, bf16[4096,128]{1,0:T(8,128)(2,1)} %get-tuple-element.96.z5_ref, bf16[4096,128]{1,0:T(8,128)(2,1)} %bitcast.68, ...), custom_call_target="tpu_custom_call" | custom-call | flops 6442450944 | bytes 4194304 | tf_op jit(solution)/shard_map/trans_bwd/pallas_call | solution.py:115
  258.4 2.2 all-gather.11.cloned.1.call-done.m_ref
  260.6 3.8 sing_wgrad.1
  264.7 28.3 %att_bwd.2 = (bf16[4096,128]{1,0:T(8,128)(2,1)}, f32[512,128]{1,0:T(8,128)}, f32[128,128]{1,0:T(8,128)}, f32[128,512]{1,0:T(8,128)}) custom-call(bf16[4096,128]{1,0:T(8,128)(2,1)} %bitcast.103, bf16[4096,128]{1,0:T(8,128)(2,1)} %get-tuple-element.101.dz_ref, bf16[128,512]{1,0:T(8,128)(2,1)} %get-tuple-element.102.bias_ref, f32[128,1]{1,0:T(8,128)} %copy.78.mask_ref.m_ref, ...), custom_call_target="tpu_custom_call" | custom-call | flops 8589934592 | bytes 4194304 | tf_op jit(solution)/shard_map/att_bwd/pallas_call | solution.py:115
  293.0 23.9 %bias_bwd.2 = (bf16[4,32,32,128]{3,2,1,0:T(8,128)(2,1)}, f32[4,128]{1,0:T(4,128)}) custom-call(bf16[4096,128]{1,0:T(8,128)(2,1)} %bitcast.104, bf16[4096,128]{1,0:T(8,128)(2,1)} %get-tuple-element.103.dz_ref, f32[128,512]{1,0:T(8,128)} %get-tuple-element.104.db_ref, bf16[4,128]{1,0:T(4,128)(2,1)} %bitcast.99), custom_call_target="tpu_custom_call" | custom-call | flops 1073741824 | bytes 4194304 | tf_op jit(solution)/shard_map/bias_bwd/pallas_call | solution.py:115
  317.0 0.7 copy.86
  317.7 24.8 %all_to_all.41 = bf16[32,128,128]{2,0,1:T(8,128)(2,1)S(1)} all-to-all(bf16[32,128,128]{2,0,1:T(8,128)(2,1)S(1)} %copy.86), channel_id=1, replica_groups=mesh['dp'=4,'dap'=4] {'dap'}, dimensions={1} | all-to-all | bytes 2097152 | tf_op jit(solution)/shard_map/all_to_all | solution.py:93
  343.0 1.4 copy.89
  344.3 28.4 %att_bwd.3 = (bf16[4096,128]{1,0:T(8,128)(2,1)}, f32[512,128]{1,0:T(8,128)}, f32[128,128]{1,0:T(8,128)}, f32[128,512]{1,0:T(8,128)}) custom-call(bf16[4096,128]{1,0:T(8,128)(2,1)} %get-tuple-element.78.z_ref, bf16[4096,128]{1,0:T(8,128)(2,1)} %bitcast.106, bf16[128,512]{1,0:T(8,128)(2,1)} %get-tuple-element.108.bias_ref, f32[128,1]{1,0:T(8,128)} %copy.78.mask_ref.m_ref, ...), custom_call_target="tpu_custom_call" | custom-call | flops 8589934592 | bytes 4194304 | tf_op jit(solution)/shard_map/att_bwd/pallas_call | solution.py:115
  372.8 12.3 %bias_bwd.3 = (bf16[4096,128]{1,0:T(8,128)(2,1)}, f32[4,128]{1,0:T(4,128)}) custom-call(bf16[4096,128]{1,0:T(8,128)(2,1)} %get-tuple-element.78.z_ref, bf16[4096,128]{1,0:T(8,128)(2,1)} %get-tuple-element.109.dz_ref, f32[128,512]{1,0:T(8,128)} %get-tuple-element.110.db_ref, bf16[4,128]{1,0:T(4,128)(2,1)} %bitcast.101), custom_call_target="tpu_custom_call" | custom-call | flops 1073741824 | bytes 4194304 | tf_op jit(solution)/shard_map/bias_bwd/pallas_call | solution.py:115
  385.1 11.3 %mul_post_bwd.2 = (bf16[4096,128]{1,0:T(8,128)(2,1)}, bf16[4096,128]{1,0:T(8,128)(2,1)}, f32[128,128]{1,0:T(8,128)}) custom-call(bf16[4096,128]{1,0:T(8,128)(2,1)} %get-tuple-element.115.dz_ref.refs_7_, f32[4096,128]{1,0:T(8,128)} %get-tuple-element.116.x_ref, bf16[4096,128]{1,0:T(8,128)(2,1)} %get-tuple-element.76.z_ref.refs_3_, bf16[128,128]{1,0:T(8,128)(2,1)} %refs_5_.1, ...), custom_call_target="tpu_custom_call" | custom-call | flops 3221225472 | bytes 4194304 | tf_op jit(solution)/shard_map/mul_post_bwd/pallas_call | solution.py:115
  396.8 7.2 %mul_proj.9.refs_1_ = bf16[4096,128]{1,0:T(8,128)(2,1)} custom-call(bf16[4096,128]{1,0:T(8,128)(2,1)} %get-tuple-element.76.z_ref.refs_3_, bf16[256,128]{1,0:T(8,128)(2,1)} %get-tuple-element.148.wt_ref), custom_call_target="tpu_custom_call" | custom-call | flops 1073741824 | bytes 4194304 | tf_op jit(solution)/shard_map/mul_proj/pallas_call | solution.py:115
  404.1 6.7 %concatenate.6 = f32[2856,128]{1,0:T(8,128)} concatenate(f32[512,128]{1,0:T(8,128)S(1)} %copy-done.7, f32[128,128]{1,0:T(8,128)S(1)} %copy-done.12, f32[512,128]{1,0:T(8,128)S(1)} %copy-done.6, f32[128,128]{1,0:T(8,128)S(1)} %copy-done.11, f32[1024,128]{1,0:T(8,128)S(1)} %copy-done.2, f32[512,128]{1,0:T(8,128)S(1)} %copy-done.5, f32[3,128]{1,0:T(4,128)S(1)} %copy-done.16, ...), dimensions={0} | concatenate | bytes 2924544 | tf_op jit(solution)/shard_map/concatenate | solution.py:54
  410.8 18.2 %all-gather.21.cloned.1.call-done = bf16[16384,128]{1,0:T(8,128)(2,1)} async-done(((bf16[4096,128]{1,0:T(8,128)(2,1)}), bf16[16384,128]{1,0:T(8,128)(2,1)}) %all-gather.21.cloned.1.call-update) | async-done | bytes 4194320 | tf_op jit(solution)/shard_map/all_gather | solution.py:675
  429.1 19.5 %mul_pre_bwd.2 = (bf16[4096,128]{1,0:T(8,128)(2,1)}, f32[512,128]{1,0:T(8,128)}, f32[128,128]{1,0:T(8,128)}) custom-call(bf16[4,4096,128]{2,1,0:T(8,128)(2,1)} %bitcast.86, bf16[4096,128]{1,0:T(8,128)(2,1)} %mul_proj.9.refs_1_, bf16[4096,128]{1,0:T(8,128)(2,1)} %mul_proj.8.refs_2_, bf16[4096,128]{1,0:T(8,128)(2,1)} %get-tuple-element.76.z_ref.refs_3_, ...), custom_call_target="tpu_custom_call" | custom-call | flops 6442450944 | bytes 4194304 | tf_op jit(solution)/shard_map/mul_pre_bwd/pallas_call | solution.py:115
  448.6 23.5 %mul_post_bwd.3 = (bf16[4096,128]{1,0:T(8,128)(2,1)}, bf16[4096,128]{1,0:T(8,128)(2,1)}, f32[128,128]{1,0:T(8,128)}, bf16[4,32,32,128]{3,2,1,0:T(8,128)(2,1)}) custom-call(bf16[4096,128]{1,0:T(8,128)(2,1)} %get-tuple-element.130.dz_ref.refs_8_, f32[4096,128]{1,0:T(8,128)} %get-tuple-element.131.x_ref, bf16[4096,128]{1,0:T(8,128)(2,1)} %bitcast.91, ...), custom_call_target="tpu_custom_call" | custom-call | flops 3221225472 | bytes 4194304 | tf_op jit(solution)/shard_map/mul_post_bwd/pallas_call | solution.py:115
  472.2 22.1 %mul_pre_bwd.3 = (bf16[4096,128]{1,0:T(8,128)(2,1)}, f32[512,128]{1,0:T(8,128)}, f32[128,128]{1,0:T(8,128)}) custom-call(bf16[4096,128]{1,0:T(8,128)(2,1)} %get-tuple-element.132.refs_0_, bf16[4096,128]{1,0:T(8,128)(2,1)} %bitcast.108, bf16[4,4096,128]{2,1,0:T(8,128)(2,1)} %bitcast.85, bf16[4,4096,128]{2,1,0:T(8,128)(2,1)} %bitcast.84, ...), custom_call_target="tpu_custom_call" | custom-call | flops 6442450944 | bytes 4194304 | tf_op jit(solution)/shard_map/mul_pre_bwd/pallas_call | solution.py:115
  494.3 6.1 %all-reduce.2.cloned.1.call-done.refs_7_ = f32[2856,128]{1,0:T(8,128)} async-done(((f32[2856,128]{1,0:T(8,128)}), f32[2856,128]{1,0:T(8,128)}) %all-reduce.2.cloned.1.call-update) | async-done | bytes 1462288 | tf_op jit(solution)/shard_map/psum | solution.py:1089
  500.3 0.7 slice_bitcast_fusion
  501.2 0.7 slice_bitcast_fusion.1
  502.4 0.7 slice.64
  503.0 2.4 concatenate.7.refs_8_
  505.5 29.8 %finish.1 = f32[5992,128]{1,0:T(8,128)} custom-call(f32[512,128]{1,0:T(8,128)} %get-tuple-element.137.refs_0_, f32[128,128]{1,0:T(8,128)} %get-tuple-element.138.refs_1_, f32[128,128]{1,0:T(8,128)} %get-tuple-element.139.refs_2_, f32[512,128]{1,0:T(8,128)} %get-tuple-element.140.refs_3_, f32[128,128]{1,0:T(8,128)} %get-tuple-element.141.refs_4_, ...), custom_call_target="tpu_custom_call" | custom-call | flops 1073741824 | bytes 4194304 | tf_op jit(solution)/shard_map/finish/pallas_call | solution.py:1020
  536.5 3.7 copy.104
  (79 shorter events, 5.5 us)
Async XLA Ops:
  7.2 43.8 %all-gather.15.cloned.1.call-start = ((), (), s32[]{:S(2)}) async-start(), calls=%async_computation.8 | async-start | bytes 5242880 | tf_op jit(solution)/shard_map/all_gather | solution.py:675
  8.2 7.8 %copy-start.3 = (bf16[128,512]{0,1:T(8,128)(2,1)}, bf16[128,512]{0,1:T(8,128)(2,1)S(1)}, u32[]{:S(2)}) copy-start(bf16[128,512]{0,1:T(8,128)(2,1)S(1)} %copy.75) | copy-start | bytes 393220
  8.9 7.2 %copy-start.8 = (bf16[128,512]{1,0:T(8,128)(2,1)S(1)}, bf16[128,512]{1,0:T(8,128)(2,1)}, u32[]{:S(2)}) copy-start(bf16[128,512]{1,0:T(8,128)(2,1)} %param.33) | copy-start | bytes 393220
  16.1 100.8 %all-gather.17.cloned.1.call-start = ((), (), s32[]{:S(2)}) async-start(), calls=%async_computation.9 | async-start | bytes 5242880 | tf_op jit(solution)/shard_map/all_gather | solution.py:675
  16.3 59.9 %copy-start.4 = (bf16[128,512]{0,1:T(8,128)(2,1)}, bf16[128,512]{0,1:T(8,128)(2,1)S(1)}, u32[]{:S(2)}) copy-start(bf16[128,512]{0,1:T(8,128)(2,1)S(1)} %copy.76) | copy-start | bytes 393220
  83.4 124.4 %all-gather.19.cloned.1.call-start = ((), (), s32[]{:S(2)}) async-start(), calls=%async_computation.10 | async-start | bytes 5242880 | tf_op jit(solution)/shard_map/all_gather | solution.py:675
  116.9 12.1 %copy-start.19 = (bf16[384]{0:T(512)(128)(2,1)S(1)}, bf16[384]{0:T(512)(128)(2,1)}, u32[]{:S(2)}) copy-start(bf16[384]{0:T(512)(128)(2,1)} %param.45) | copy-start | bytes 2308
  129.1 8.3 %copy-start.20 = (s32[1,128]{1,0:T(1,128)S(1)}, s32[1,128]{1,0:T(1,128)}, u32[]{:S(2)}) copy-start(s32[1,128]{1,0:T(1,128)} %param.27) | copy-start | bytes 1540
  129.1 9.0 %copy-start.9 = (bf16[128,512]{1,0:T(8,128)(2,1)S(1)}, bf16[128,512]{1,0:T(8,128)(2,1)}, u32[]{:S(2)}) copy-start(bf16[128,512]{1,0:T(8,128)(2,1)} %param.36) | copy-start | bytes 393220
  129.6 9.2 %copy-start = (bf16[1,32,128,128]{3,2,1,0:T(8,128)(2,1)S(1)}, bf16[1,32,128,128]{3,2,1,0:T(8,128)(2,1)}, u32[]{:S(2)}) copy-start(bf16[1,32,128,128]{3,2,1,0:T(8,128)(2,1)} %param.29) | copy-start | bytes 3145732
  133.8 40.8 %all-to-all-start.1 = ((bf16[4,3,32,96]{3,2,1,0:T(8,128)(2,1)}), bf16[4,3,32,96]{3,2,1,0:T(8,128)(2,1)S(1)}, u32[]{:S(2)}, u32[]{:S(2)}) async-start(bf16[4,3,32,96]{3,2,1,0:T(8,128)(2,1)} %bitcast.58), calls=%async_computation.1 | async-start | bytes 196608 | tf_op jit(solution)/shard_map/all_to_all | solution.py:93
  140.5 37.9 %copy-start.10 = (bf16[128,512]{1,0:T(8,128)(2,1)S(1)}, bf16[128,512]{1,0:T(8,128)(2,1)}, u32[]{:S(2)}) copy-start(bf16[128,512]{1,0:T(8,128)(2,1)} %param.39) | copy-start | bytes 393220
  174.6 32.0 %all-to-all-start = ((bf16[32,128,128]{2,0,1:T(8,128)(2,1)}), bf16[32,128,128]{2,0,1:T(8,128)(2,1)S(1)}, u32[]{:S(2)}, u32[]{:S(2)}) async-start(bf16[32,128,128]{2,0,1:T(8,128)(2,1)} %bitcast.57), calls=%async_computation | async-start | bytes 2097152 | tf_op jit(solution)/shard_map/all_to_all | solution.py:93
  178.1 82.5 %all-gather.11.cloned.1.call-start = ((), (), s32[]{:S(2)}) async-start(), calls=%async_computation.4 | async-start | bytes 2580480 | tf_op jit(solution)/shard_map/all_gather | solution.py:16
  238.9 78.0 %reduce-scatter.2.cloned.1.call-start = ((), (), s32[]{:S(2)}) async-start(), calls=%async_computation.5 | async-start | bytes 4177920 | tf_op jit(solution)/shard_map/reduce_scatter | solution.py:1077
  264.5 120.6 %all-gather.13.cloned.1.call-start = ((), (), s32[]{:S(2)}) async-start(), calls=%async_computation.6 | async-start | bytes 4177920 | tf_op jit(solution)/shard_map/all_gather | solution.py:16
  293.0 24.0 %copy-start.1 = (bf16[4096,128]{1,0:T(8,128)(2,1)S(1)}, bf16[4096,128]{1,0:T(8,128)(2,1)}, u32[]{:S(2)}) copy-start(bf16[4096,128]{1,0:T(8,128)(2,1)} %get-tuple-element.96.z5_ref) | copy-start | bytes 3145732
  317.0 112.1 %all-gather.21.cloned.1.call-start = ((), (), s32[]{:S(2)}) async-start(), calls=%async_computation.11 | async-start | bytes 5242880 | tf_op jit(solution)/shard_map/all_gather | solution.py:675
  396.4 7.7 %copy-start.2 = (f32[1024,128]{1,0:T(8,128)S(1)}, f32[1024,128]{1,0:T(8,128)}, u32[]{:S(2)}) copy-start(f32[1024,128]{1,0:T(8,128)} %get-tuple-element.122) | copy-start | bytes 1572868
  396.4 7.7 %copy-start.5 = (f32[512,128]{1,0:T(8,128)S(1)}, f32[512,128]{1,0:T(8,128)}, u32[]{:S(2)}) copy-start(f32[512,128]{1,0:T(8,128)} %get-tuple-element.123) | copy-start | bytes 786436
  396.4 7.7 %copy-start.6 = (f32[512,128]{1,0:T(8,128)S(1)}, f32[512,128]{1,0:T(8,128)}, u32[]{:S(2)}) copy-start(f32[512,128]{1,0:T(8,128)} %get-tuple-element.120) | copy-start | bytes 786436
  396.4 7.7 %copy-start.7 = (f32[512,128]{1,0:T(8,128)S(1)}, f32[512,128]{1,0:T(8,128)}, u32[]{:S(2)}) copy-start(f32[512,128]{1,0:T(8,128)} %get-tuple-element.118) | copy-start | bytes 786436
  396.4 7.7 %copy-start.11 = (f32[128,128]{1,0:T(8,128)S(1)}, f32[128,128]{1,0:T(8,128)}, u32[]{:S(2)}) copy-start(f32[128,128]{1,0:T(8,128)} %get-tuple-element.121) | copy-start | bytes 196612
  396.4 7.7 %copy-start.12 = (f32[128,128]{1,0:T(8,128)S(1)}, f32[128,128]{1,0:T(8,128)}, u32[]{:S(2)}) copy-start(f32[128,128]{1,0:T(8,128)} %get-tuple-element.119) | copy-start | bytes 196612
  396.4 7.7 %copy-start.15 = (f32[16,128]{1,0:T(8,128)S(1)}, f32[16,128]{1,0:T(8,128)}, u32[]{:S(2)}) copy-start(f32[16,128]{1,0:T(8,128)} %get-tuple-element.125) | copy-start | bytes 24580
  396.5 7.7 %copy-start.16 = (f32[3,128]{1,0:T(4,128)S(1)}, f32[3,128]{1,0:T(4,128)}, u32[]{:S(2)}) copy-start(f32[3,128]{1,0:T(4,128)} %get-tuple-element.124) | copy-start | bytes 4612
  396.5 7.7 %copy-start.17 = (f32[4,128]{1,0:T(4,128)S(1)}, f32[4,128]{1,0:T(4,128)}, u32[]{:S(2)}) copy-start(f32[4,128]{1,0:T(4,128)} %get-tuple-element.127) | copy-start | bytes 6148
  396.5 7.7 %copy-start.18 = (f32[4,128]{1,0:T(4,128)S(1)}, f32[4,128]{1,0:T(4,128)}, u32[]{:S(2)}) copy-start(f32[4,128]{1,0:T(4,128)} %get-tuple-element.126) | copy-start | bytes 6148
  396.5 103.8 %all-reduce.2.cloned.1.call-start = ((), (), s32[]{:S(2)}) async-start(), calls=%async_computation.7 | async-start | bytes 2924544 | tf_op jit(solution)/shard_map/psum | solution.py:1089
  505.5 29.8 %copy-start.14 = (bf16[32,384]{1,0:T(8,128)(2,1)S(1)}, bf16[32,384]{1,0:T(8,128)(2,1)}, u32[]{:S(2)}) copy-start(bf16[32,384]{1,0:T(8,128)(2,1)} %get-tuple-element.91) | copy-start | bytes 73732
  505.5 30.5 %copy-start.13 = (bf16[32,384]{1,0:T(8,128)(2,1)S(1)}, bf16[32,384]{1,0:T(8,128)(2,1)}, u32[]{:S(2)}) copy-start(bf16[32,384]{1,0:T(8,128)(2,1)} %get-tuple-element.114) | copy-start | bytes 73732
Sparse Core Ops, SparseCore 0:
  16.2 34.7 all-gather.14
  83.5 33.3 all-gather.16
  129.2 39.1 all-gather.18
  239.1 21.5 all-gather.10
  264.6 40.9 reduce-scatter.1
  317.1 36.9 all-gather.12
  396.6 32.3 all-gather.20
  434.1 66.2 all-reduce.1

commit v2 on v1

--- a/solution.py
+++ b/solution.py
@@ -159,6 +159,61 @@
             c.wait_send()
 
 
+PACK = 8
+CHUNKS = 4
+CHUNK_ROWS = N_POS // CHUNKS
+
+
+class Gather:
+    def __init__(self, me, own_ref, all_ref, send, recv):
+        self.all, self.send, self.recv = all_ref, send, recv
+        self.partner, self.across = me + 1 - 2 * lax.rem(me, 2), lax.rem(me + 2, GRP)
+        self.far = [self.copy(own_ref.at[self.rows(c), :], me, self.across, 0, c) for c in range(CHUNKS)]
+        self.near = [self.copy(own_ref.at[self.rows(c), :], me, self.partner, 1, c) for c in range(CHUNKS)]
+        self.passed = []
+        for c in self.far + self.near:
+            c.start()
+        all_ref[me] = own_ref[...]
+
+    def rows(self, c):
+        return pl.ds(c * CHUNK_ROWS, CHUNK_ROWS)
+
+    def copy(self, src, slot, dest, kind, c):
+        return pltpu.make_async_remote_copy(
+            src_ref=src, dst_ref=self.all.at[slot, self.rows(c), :], send_sem=self.send.at[kind, c], recv_sem=self.recv.at[kind, c],
+            device_id={GROUP_AXIS: dest}, device_id_type=MESH_ID)
+
+    def each(self, work):
+        for c in range(CHUNKS + 1):
+            if c < CHUNKS:
+                self.far[c].wait_recv()
+                self.passed.append(self.copy(self.all.at[self.across, self.rows(c), :], self.across, self.partner, 2, c))
+                self.passed[c].start()
+            if c:
+                self.near[c - 1].wait_recv()
+                self.passed[c - 1].wait_recv()
+                loop(CH // CHUNKS, lambda k: work(k + (c - 1) * (CH // CHUNKS)), PACK)
+
+    def pass_on(self):
+        for c in range(CHUNKS):
+            self.far[c].wait_recv()
+            self.passed.append(self.copy(self.all.at[self.across, self.rows(c), :], self.across, self.partner, 2, c))
+            self.passed[c].start()
+
+    def arrive(self):
+        for c in self.near + self.passed:
+            c.wait_recv()
+
+    def leave(self):
+        for c in self.far + self.near + self.passed:
+            c.wait_send()
+
+
+def gather_sems():
+    sems = pltpu.SemaphoreType.DMA((3, CHUNKS))
+    return [sems, sems]
+
+
 def own_rows(p, size=ROWS):
     return pl.ds(pl.multiple_of(p * size, size), size)
 
@@ -201,7 +256,6 @@
 
 
 ATT_STEP = 4
-PACK = 8
 BWD_STEP = 4
 
 
@@ -232,7 +286,13 @@
     return cat0([dot_nn(head_rows(xt, h), wide[:, h * COLS:(h + 1) * COLS]) for h in range(TRI_HEADS)])
 
 
-def att_fwd_kernel(ending, z_ref, wbt_ref, mask_ref, wt_ref, wo_ref, o_ref, bias_ref, bm_ref, own_ref, send, recv, *rest):
+def att_fwd_kernel(ending, z_ref, wbt_ref, mask_ref, w_ref, wo_ref, *rest):
+    *rest, wt_ref = rest
+    wt_ref[...] = w_ref[...].T
+    if ending:
+        dp_ref, o_ref, bias_ref, dpt_ref, bm_ref, own_ref, send, recv, dp_send, dp_recv = rest
+    else:
+        o_ref, bias_ref, bm_ref, own_ref, send, recv, *rest = rest
     me = lax.axis_index(GROUP_AXIS)
     greet(me)
     turn = None if ending else Turn(me, rest[0], rest[1], o_ref, *rest[2:])
@@ -249,6 +309,9 @@
     await_group()
     ex = Exchange(me, lambda p: bias_ref.at[own_rows(me), :], lambda m: bias_ref.at[own_rows(m), :], send, recv)
     ex.arrive()
+    if ending:
+        ex_dp = Exchange(me, lambda p: dp_ref.at[:, own_rows(p), :], lambda m: dpt_ref.at[m], dp_send, dp_recv)
+        dpt_ref[me] = dp_ref[:, own_rows(me), :]
     fill_bias(bias_ref, mask_ref, bm_ref)
 
     def step(t):
@@ -276,9 +339,12 @@
 
     halves(ROWS // ATT_STEP, step, turn)
     ex.leave()
-
-
-def halves(count, step, turn):
+    if ending:
+        ex_dp.arrive()
+        ex_dp.leave()
+
+
+def halves(count, step, turn, filler=None):
     if turn is None:
         loop(count, step)
         return
@@ -286,18 +352,35 @@
     turn.half(0)
     loop(count // 2, lambda t: step(t + count // 2))
     turn.half(1)
+    if filler:
+        filler()
     turn.finish()
 
 
-def att_fwd(z, w_b, mask_col, wt, w_o, ending):
+def att_fwd(z, w_b, mask_col, wt, w_o, d_pair=None):
+    ending = d_pair is not None
     scr = [pltpu.VMEM((COLS, TRI_HEADS * COLS), F32), pltpu.VMEM((ROWS, TRI_HEADS * COLS), F32)] + peer_sems()
-    out = sds((N_POS, CH) if ending else TURNED, BF16)
-    return call(functools.partial(att_fwd_kernel, ending), [out, sds((COLS, TRI_HEADS * COLS), BF16)],
-                scr if ending else scr + turn_scratch(), flops=3 * GIGA, name='att_fwd', comm=4 if ending else 3,
-                )(z, w_b.T, mask_col, wt, w_o)
-
-
-def att_bwd_kernel(z_blocked, dz_blocked, z_ref, dz_ref, bias_ref, mask_ref, wt_ref, wo_ref, dzo_ref, dwr_ref, dwo_ref, db_ref, bm_ref, acc_ref, dwqg_ref, dwkv_ref):
+    outs = [sds((N_POS, CH) if ending else TURNED, BF16), sds((COLS, TRI_HEADS * COLS), BF16)]
+    args = [z, w_b.T, mask_col, wt, w_o]
+    if ending:
+        outs.append(sds(TURNED, BF16))
+        args.append(d_pair)
+    return call(functools.partial(att_fwd_kernel, ending), outs, scr + (peer_sems() if ending else turn_scratch()) + [pltpu.VMEM((4 * CH, CH), BF16)],
+                flops=3 * GIGA, name='att_fwd', comm=4 if ending else 3)(*args)
+
+
+def att_bwd_kernel(ending, z_ref, dz_ref, bias_ref, mask_ref, w_ref, wo_ref, *rest):
+    *rest, wt_ref = rest
+    wt_ref[...] = w_ref[...].T
+    z_blocked, dz_blocked = ending, not ending
+    if ending:
+        own_ref, all_ref, *rest = rest
+        *rest, send, recv = rest
+        me = lax.axis_index(GROUP_AXIS)
+        greet(me)
+        await_group()
+        gather = Gather(me, own_ref, all_ref, send, recv)
+    dzo_ref, dwr_ref, dwo_ref, db_ref, bm_ref, acc_ref, dwqg_ref, dwkv_ref = rest
     fill_bias(bias_ref, mask_ref, bm_ref)
     acc_ref[...] = jnp.zeros_like(acc_ref)
     dwqg_ref[...] = jnp.zeros_like(dwqg_ref)
@@ -339,20 +422,31 @@
         dzo_ref[chunk_ds(t, BWD_STEP * COLS), :] = (dz.astype(F32) + norm_back(dn, nhat, r_std)).astype(BF16)
 
     loop(ROWS // BWD_STEP, step)
+    if ending:
+        gather.pass_on()
     for h in range(TRI_HEADS):
         cols = slice(h * COLS, (h + 1) * COLS)
         db_ref[:, cols] = acc_ref[:, cols].T
     for m in range(2):
         dwr_ref[pl.ds(3 * m, CH, stride=4), :] = dwqg_ref[m * CH:(m + 1) * CH, :].T
         dwr_ref[pl.ds(1 + m, CH, stride=4), :] = dwkv_ref[:, m * CH:(m + 1) * CH]
-
-
-def att_bwd(z, dz, bias_all, mask_col, wt, w_o, z_blocked, dz_blocked):
-    return call(functools.partial(att_bwd_kernel, z_blocked, dz_blocked),
-                [sds((N_POS, CH), BF16), sds((4 * CH, CH), F32), sds((CH, CH), F32), sds((COLS, TRI_HEADS * COLS), F32)],
-                [pltpu.VMEM((COLS, TRI_HEADS * COLS), F32), pltpu.VMEM((COLS, TRI_HEADS * COLS), F32),
-                 pltpu.VMEM((2 * CH, CH), F32), pltpu.VMEM((CH, 2 * CH), F32)],
-                flops=8 * GIGA, name='att_bwd')(z, dz, bias_all, mask_col, wt, w_o)
+    if ending:
+        gather.arrive()
+        gather.leave()
+
+
+def att_bwd(z, dz, bias_all, mask_col, wt, w_o, left=None):
+    ending = left is not None
+    outs = [sds((N_POS, CH), BF16), sds((4 * CH, CH), F32), sds((CH, CH), F32), sds((COLS, TRI_HEADS * COLS), F32)]
+    wide = pltpu.VMEM((COLS, TRI_HEADS * COLS), F32)
+    scr = [wide, wide, pltpu.VMEM((HALF, CH), F32), pltpu.VMEM((CH, HALF), F32)]
+    args = [z, dz, bias_all, mask_col, wt, w_o]
+    if ending:
+        outs = [sds((GRP, N_POS, CH), BF16)] + outs
+        scr = scr + gather_sems()
+        args.append(left)
+    scr.append(pltpu.VMEM((4 * CH, CH), BF16))
+    return call(functools.partial(att_bwd_kernel, ending), outs, scr, flops=8 * GIGA, name='att_bwd', comm=9 if ending else None)(*args)
 
 
 def bias_bwd_kernel(ending, z_ref, dz_ref, db_ref, wbt_ref, dzo_ref, dwt_ref, parts_ref, send, recv, *rest):
@@ -399,7 +493,7 @@
 SING_HEADS = 16
 
 
-def trans_fwd_kernel(z_ref, wu_ref, wd_ref, wpt_ref, o_ref, b_ref, scr_ref):
+def trans_fwd_kernel(z_ref, wu_ref, wd_ref, wpt_ref, o_ref, b_ref, turned_ref, scr_ref, turn_ref):
     def step(t):
         z = z_ref[chunk_ds(t), :].astype(F32)
         nhat, _ = norm_parts(z)
@@ -408,6 +502,8 @@
         act = (jax.nn.sigmoid(h1) * h1 * h2).astype(BF16)
         out = (z + dot_nn(act, wd_ref[...])).astype(BF16)
         o_ref[chunk_ds(t), :] = out
+        for r in range(STEP_ROWS):
+            put_strided(turn_ref, t * STEP_ROWS + r, out[r * COLS:(r + 1) * COLS].astype(F32))
         n5, _ = norm_parts(out.astype(F32))
         n5 = n5.astype(BF16)
         for r in range(STEP_ROWS):
@@ -415,15 +511,26 @@
 
     loop(ROWS // STEP_ROWS, step)
     b_ref[...] = scr_ref[...].astype(BF16)
+    cast_out(turn_ref, turned_ref)
 
 
 def trans_fwd(z, w_up, w_down, w_pb):
-    return call(trans_fwd_kernel, [sds((N_POS, CH), BF16), sds((SING_HEADS * ROWS, COLS), BF16)],
-                [pltpu.VMEM((SING_HEADS * ROWS, COLS), F32)],
+    return call(trans_fwd_kernel, [sds((N_POS, CH), BF16), sds((SING_HEADS * ROWS, COLS), BF16), sds((N_POS, CH), BF16)],
+                [pltpu.VMEM((SING_HEADS * ROWS, COLS), F32), pltpu.VMEM((N_POS, CH), F32)],
                 flops=2 * GIGA, name='trans_fwd')(z, w_up, w_down, w_pb.T)
 
 
-def trans_bwd_kernel(z_ref, z5_ref, dz_ref, db_ref, wu_ref, wd_ref, wpt_ref, dzo_ref, dwr_ref, dwd_ref, dwpt_ref, dwu_ref, scr_ref):
+def trans_bwd_kernel(z_ref, z5_ref, dz_ref, db_ref, wu_ref, wd_ref, wpt_ref,
+                     dzo_ref, dwr_ref, dwd_ref, dwpt_ref, dwu_ref, scr_ref, dzs_ref):
+
+    def convert(t):
+        dzs_ref[chunk_ds(t, WIDE), :] = dz_ref[chunk_ds(t, WIDE), :].astype(F32)
+
+    loop(N_POS // WIDE, convert)
+
+    def dz_row(j):
+        return cat0([dzs_ref[pl.ds(g * ROWS * ROWS + j, ROWS, stride=ROWS), :] for g in range(GRP)])
+
     dwu_ref[...] = jnp.zeros_like(dwu_ref)
     dwd_ref[...] = jnp.zeros_like(dwd_ref)
     dwpt_ref[...] = jnp.zeros_like(dwpt_ref)
@@ -437,7 +544,7 @@
             db = scr_ref[pl.ds(t * STEP_ROWS + r, SING_HEADS, stride=ROWS), :].astype(BF16)
             dwpt_ref[...] += dot_nn(db, n5b[r * COLS:(r + 1) * COLS])
             dn5.append(dot_tn(db, wpt_ref[...]))
-        dz = dz_ref[chunk_ds(t), :].astype(F32) + norm_back(cat0(dn5), n5, r5)
+        dz = cat0([dz_row(t * STEP_ROWS + r) for r in range(STEP_ROWS)]) + norm_back(cat0(dn5), n5, r5)
         dzb = dz.astype(BF16)
         nhat, r_std = norm_parts(z_ref[chunk_ds(t), :].astype(F32))
         nb = nhat.astype(BF16)
@@ -453,14 +560,13 @@
         dzo_ref[chunk_ds(t), :] = (dz + norm_back(dn, nhat, r_std)).astype(BF16)
 
     loop(ROWS // STEP_ROWS, step)
-    store_rows(dwr_ref, dwu_ref[...], 8)
+    store_rows(dwr_ref, dwu_ref[...], PACK)
 
 
 def trans_bwd(z, z5, dz, db, w_up, w_down, w_pb):
-    return call(trans_bwd_kernel,
-                [sds((N_POS, CH), BF16), sds((8 * CH, CH), F32), sds((4 * CH, CH), F32), sds((SING_HEADS, CH), F32)],
-                [pltpu.VMEM((CH, 8 * CH), F32), pltpu.VMEM((SING_HEADS * ROWS, COLS), F32)],
-                flops=6 * GIGA, name='trans_bwd')(z, z5, dz, db, w_up, w_down, w_pb.T)
+    outs = [sds((N_POS, CH), BF16), sds((8 * CH, CH), F32), sds((4 * CH, CH), F32), sds((SING_HEADS, CH), F32)]
+    scr = [pltpu.VMEM((CH, 8 * CH), F32), pltpu.VMEM((SING_HEADS * ROWS, COLS), F32), pltpu.VMEM((N_POS, CH), F32)]
+    return call(trans_bwd_kernel, outs, scr, flops=6 * GIGA, name='trans_bwd')(z, z5, dz, db, w_up, w_down, w_pb.T)
 
 
 def load_row(ref, i, blocked):
@@ -498,49 +604,66 @@
     return cat0([ref[s, chunk_ds(c, ROWS), :] for s in range(GRP)])
 
 
-def make_proj(n_out, blocked):
-    def kernel(z_ref, wt_ref, *rest):
-        outs, scrs = rest[:n_out], rest[n_out:]
-
-        def step(t):
-            z = cat0([load_row(z_ref, t * FOUR + r, blocked) for r in range(FOUR)]).astype(F32)
-            nhat, _ = norm_parts(z)
-            pt = dot_nt(wt_ref[...], nhat.astype(BF16))
-            for m in range(n_out):
-                val = jax.nn.sigmoid(pt[(2 * m + 1) * CH:(2 * m + 2) * CH]) * pt[2 * m * CH:(2 * m + 1) * CH]
-                for r in range(FOUR):
-                    put_strided(scrs[m], t * FOUR + r, val[:, r * COLS:(r + 1) * COLS])
-
-        loop(ROWS // FOUR, step)
-        for m in range(n_out):
-            cast_out(scrs[m], outs[m])
-
-    return kernel
-
-
-def mul_proj(z, wt, blocked=False):
-    n_out = wt.shape[0] // (2 * CH)
-    return call(make_proj(n_out, blocked), [sds((N_POS, CH), BF16)] * n_out, [pltpu.VMEM((N_POS, CH), F32)] * n_out,
-                flops=GIGA, name='mul_proj')(z, wt)
-
-
-def start_turn(rest):
-    me = lax.axis_index(GROUP_AXIS)
-    greet(me)
-    out_ref, scr_ref, stage_ref, send, recv = rest
-    return Turn(me, scr_ref, stage_ref, out_ref, send, recv)
+def project(z_ref, wt_ref, scr_ref, out_ref, blocked):
+    def step(t):
+        z = cat0([load_row(z_ref, t * FOUR + r, blocked) for r in range(FOUR)]).astype(F32)
+        nhat, _ = norm_parts(z)
+        pt = dot_nt(wt_ref[...], nhat.astype(BF16))
+        val = jax.nn.sigmoid(pt[CH:]) * pt[:CH]
+        for r in range(FOUR):
+            put_strided(scr_ref, t * FOUR + r, val[:, r * COLS:(r + 1) * COLS])
+
+    loop(ROWS // FOUR, step)
+    cast_out(scr_ref, out_ref)
+
+
+def proj_kernel(z_ref, w_ref, o_ref, scr_ref, wt_ref):
+    wt_ref[...] = w_ref[:, HALF:].T
+    project(z_ref, wt_ref, scr_ref, o_ref, False)
+
+
+def mul_proj(z, w):
+    return call(proj_kernel, [sds((N_POS, CH), BF16)], [pltpu.VMEM((N_POS, CH), F32), pltpu.VMEM((HALF, CH), BF16)],
+                flops=GIGA, name='mul_proj')(z, w)
+
+
+def sing_heads(me, s_ref, w_ref, qb_ref, gate_ref, out_ref, in_ref, send, recv):
+    nhat, _ = norm_parts(s_ref[...].astype(F32))
+    p_all = dot_nn(nhat.astype(BF16), w_ref[...])
+    gate_ref[...] = jax.nn.sigmoid(p_all[:, 3 * C_S:])
+    qkv = cat1([p_all[:, :C_S] + qb_ref[...].astype(F32), p_all[:, C_S:3 * C_S]]).astype(BF16)
+    for t in range(3):
+        for g in range(GRP):
+            at = t * C_S + g * GRP_W
+            out_ref[g, t] = qkv[:, at:at + GRP_W]
+    in_ref[me] = out_ref[me]
+    return Exchange(me, lambda p: out_ref.at[p], lambda m: in_ref.at[m], send, recv)
 
 
 def make_mix(outgoing):
-    def kernel(left_ref, right_ref, z_ref, wg_ref, wo_ref, x_ref, o_ref, *rest):
-        turn = start_turn(rest) if outgoing else None
+    def kernel(*refs):
+        turn = None
+        me = lax.axis_index(GROUP_AXIS)
+        greet(me)
+        if outgoing:
+            (zl_ref, wl_ref, own_ref, z_ref, wg_ref, wo_ref, wn_ref, x_ref, o_ref, right_ref, left_ref, turned_ref, next_ref,
+             scr_ref, stage_ref, send, recv, g_send, g_recv, wt_ref) = refs
+            turn = Turn(me, scr_ref, stage_ref, turned_ref, send, recv)
+        else:
+            (zl_ref, wl_ref, own_ref, z_ref, wg_ref, wo_ref, s_ref, wq_ref, qb_ref, x_ref, o_ref, right_ref, left_ref, gate_ref, heads_ref,
+             heads_out, send, recv, g_send, g_recv, wt_ref) = refs
+        await_group()
+        gather = Gather(me, own_ref, right_ref, g_send, g_recv)
+        ex = None if outgoing else sing_heads(me, s_ref, wq_ref, qb_ref, gate_ref, heads_out, heads_ref, send, recv)
+        wt_ref[...] = wl_ref[:, :HALF].T
+        project(zl_ref, wt_ref, x_ref, left_ref, not outgoing)
 
         def mix(c):
             a = left_ref[chunk_ds(c, ROWS), :]
             b = group_rows(right_ref, c)
             x_ref[chunk_ds(c, ROWS), :] = dot_nt(a, b) if outgoing else dot_nn(a, b)
 
-        loop(CH, mix, 8)
+        gather.each(mix)
 
         def step(t):
             x = get_four(x_ref, t)
@@ -554,26 +677,43 @@
                     put_strided(turn.scr, t * FOUR + r, out[r * COLS:(r + 1) * COLS])
             o_ref[chunk_ds(t, WIDE), :] = out.astype(BF16)
 
-        if outgoing:
-            await_group()
-        halves(ROWS // FOUR, step, turn)
+        def following():
+            wt_ref[...] = wn_ref[:, HALF:].T
+            project(o_ref, wt_ref, scr_ref, next_ref, False)
+
+        halves(ROWS // FOUR, step, turn, following)
+        gather.leave()
+        if ex is not None:
+            ex.arrive()
+            ex.leave()
 
     return kernel
 
 
-def mul_mix(left, right_all, z, w_gate, w_out, outgoing):
-    outs = [sds((N_POS, COLS), F32), sds((N_POS, CH), BF16)]
-    scr = []
+def mul_mix(z_left, wt_left, right, z, w_gate, w_out, wt_next=None, single=None):
+    outgoing = single is None
+    flat = sds((N_POS, CH), BF16)
+    outs = [sds((N_POS, COLS), F32), flat, sds((GRP, N_POS, CH), BF16), flat]
+    scr = gather_sems() + [pltpu.VMEM((HALF, CH), BF16)]
     if outgoing:
-        outs.append(sds(TURNED, BF16))
-        scr = turn_scratch()
-    return call(make_mix(outgoing), outs, scr, flops=3 * GIGA, name='mul_mix', comm=7 if outgoing else None)(left, right_all, z, w_gate, w_out)
+        outs += [sds(TURNED, BF16), flat]
+        scr = turn_scratch() + scr
+    else:
+        heads = (GRP, 3, ROWS, GRP_W)
+        outs += [sds((ROWS, C_S), F32), sds(heads, BF16)]
+        scr = [pltpu.VMEM(heads, BF16)] + peer_sems() + scr
+    return call(make_mix(outgoing), outs, scr, flops=3 * GIGA, name='mul_mix', comm=7 if outgoing else 10)(z_left, wt_left, right, z, w_gate, w_out, *(single or (wt_next,)))
 
 
 def make_post_bwd(outgoing):
     def kernel(dz_ref, x_ref, z_ref, wg_ref, wo_ref, dx_ref, dgl_ref, dwo_ref, *rest):
         scr_ref, rest = rest[-1], rest[:-1]
-        turn = start_turn(rest) if outgoing else None
+        turn = None
+        if outgoing:
+            me = lax.axis_index(GROUP_AXIS)
+            greet(me)
+            turned_ref, turn_scr, stage_ref, send, recv = rest
+            turn = Turn(me, turn_scr, stage_ref, turned_ref, send, recv)
         dwo_ref[...] = jnp.zeros_like(dwo_ref)
 
         def step(t):
@@ -613,8 +753,16 @@
 
 def make_pre_bwd(outgoing):
     def kernel(*refs):
+        *refs, wt_ref = refs
         if outgoing:
-            dx_ref, dxr_ref, left_ref, right_ref, z_ref, wt_ref, wg_ref, dgl_ref, dz_ref, dzo_ref, dwr_ref, dwg_ref, da_ref, db_ref, dwt_ref, scr_ref = refs
+            (dx_ref, dxr_ref, left_ref, right_ref, z_ref, w_ref, wg_ref, dgl_ref, dz_ref, turned_ref, dzo_ref, dwr_ref, dwg_ref, zrow_ref,
+             da_ref, db_ref, dwt_ref, scr_ref, send, recv) = refs
+            me = lax.axis_index(GROUP_AXIS)
+            greet(me)
+            await_group()
+            ex = Exchange(me, lambda p: turned_ref.at[p], lambda m: zrow_ref.at[:, own_rows(m), :], send, recv)
+            zrow_ref[:, own_rows(me), :] = turned_ref[me]
+            wt_ref[...] = w_ref[...].T
 
             def turn(j):
                 put_strided(scr_ref, j, load_row(dxr_ref, j, True).astype(F32).T)
@@ -625,21 +773,41 @@
                 da_ref[chunk_ds(c, ROWS), :] = dot_nn(dx_ref[chunk_ds(c, ROWS), :], group_rows(right_ref, c))
                 db_ref[chunk_ds(c, ROWS), :] = dot_nn(scr_ref[chunk_ds(c, ROWS), :].astype(BF16), group_rows(left_ref, c))
         else:
-            dx_ref, left_ref, right_ref, z_ref, wt_ref, wg_ref, dgl_ref, dz_ref, dzo_ref, dwr_ref, dwg_ref, da_ref, db_ref, dwt_ref = refs
+            (own_ref, right_ref, z_ref, w_ref, wg_ref, dgl_ref, dz_ref, dzo_ref, dwr_ref, dwg_ref, da_ref, db_ref, dwt_ref,
+             dx_ref, left_ref, pt_ref, send, recv) = refs
+            me = lax.axis_index(GROUP_AXIS)
+            greet(me)
+            await_group()
+            gather = Gather(me, own_ref, dx_ref, send, recv)
+            wt_ref[...] = w_ref[...].T
+
+            def prepare(t):
+                nb = norm_parts(z_ref[chunk_ds(t, WIDE), :].astype(F32))[0].astype(BF16)
+                pt = dot_nt(wt_ref[...], nb)
+                pt_ref[t] = pt
+                val = jax.nn.sigmoid(pt[CH:HALF]) * pt[:CH]
+                for r in range(FOUR):
+                    put_strided(da_ref, t * FOUR + r, val[:, r * COLS:(r + 1) * COLS])
+
+            loop(ROWS // FOUR, prepare)
+            cast_out(da_ref, left_ref)
 
             def mix(c):
                 dx = group_rows(dx_ref, c)
                 da_ref[chunk_ds(c, ROWS), :] = dot_nt(right_ref[chunk_ds(c, ROWS), :], dx)
                 db_ref[chunk_ds(c, ROWS), :] = dot_nn(left_ref[chunk_ds(c, ROWS), :], dx)
 
-        loop(CH, mix, 8)
+        if outgoing:
+            loop(CH, mix, PACK)
+        else:
+            gather.each(mix)
         dwt_ref[...] = jnp.zeros_like(dwt_ref)
         dwg_ref[...] = jnp.zeros_like(dwg_ref)
 
         def step(t):
             nhat, r_std = norm_parts(z_ref[chunk_ds(t, WIDE), :].astype(F32))
             nb = nhat.astype(BF16)
-            pt = dot_nt(wt_ref[...], nb)
+            pt = dot_nt(wt_ref[...], nb) if outgoing else pt_ref[t]
             parts = []
             for m, d_ref in enumerate((da_ref, db_ref)):
                 d = get_four(d_ref, t)
@@ -656,34 +824,35 @@
 
         loop(ROWS // FOUR, step)
         for t in range(FOUR):
-            dwr_ref[pl.ds(t, CH, stride=4), :] = dwt_ref[t * CH:(t + 1) * CH, :].T
+            dwr_ref[pl.ds(t, CH, stride=FOUR), :] = dwt_ref[t * CH:(t + 1) * CH, :].T
+        if outgoing:
+            ex.arrive()
+            ex.leave()
+        else:
+            gather.leave()
 
     return kernel
 
 
-def mul_pre_bwd(dx, left, right, z, wt, w_gate, dgl, dz, dx_turned=None):
+def mul_pre_bwd(dx, left, right, z, wt, w_gate, dgl, dz, dx_turned=None, z_turned=None):
     outgoing = dx_turned is not None
-    args = [dx] + ([dx_turned] if outgoing else []) + [left, right, z, wt, w_gate, dgl, dz]
-    scr = [pltpu.VMEM((N_POS, CH), F32)] * 2 + [pltpu.VMEM((4 * CH, CH), F32)]
+    args = [dx] + ([dx_turned, left] if outgoing else []) + [right, z, wt, w_gate, dgl, dz] + ([z_turned] if outgoing else [])
+    outs = [sds((N_POS, CH), BF16), sds((4 * CH, CH), F32), sds((CH, CH), F32)]
+    block = pltpu.VMEM((N_POS, CH), F32)
+    scr = [block, block, pltpu.VMEM((4 * CH, CH), F32)]
     if outgoing:
-        scr.append(pltpu.VMEM((N_POS, CH), F32))
-    return call(make_pre_bwd(outgoing), [sds((N_POS, CH), BF16), sds((4 * CH, CH), F32), sds((CH, CH), F32)], scr,
-                flops=6 * GIGA, name='mul_pre_bwd')(*args)
-
-
-def gather_blocks(x):
-    return lax.all_gather(x, GROUP_AXIS, axis=0)
-
-
-def swap_rows(x_in):
-    x_t = swap_all(x_in, 1, 0)
-    return jnp.swapaxes(x_t, 0, 1).reshape(N_POS, CH)
-
-
-def att_backward(z, dz, bias_all, mask_col, w_qkvg, w_tb, w_o, ending):
-    dz_part, g_qkvg, g_out, db = att_bwd(z, dz, bias_all, mask_col, w_qkvg.T, w_o, ending, not ending)
-    dz_new, g_bt = bias_bwd(z, dz_part, db, w_tb, ending)
-    return dz_new.reshape(N_POS, CH), [g_qkvg, g_bt, g_out]
+        outs.append(sds((ROWS, COLS, CH), BF16))
+        scr += [block] + peer_sems()
+    else:
+        scr += [pltpu.VMEM((GRP, N_POS, CH), BF16), pltpu.VMEM((N_POS, CH), BF16), pltpu.VMEM((ROWS // FOUR, 4 * CH, WIDE), F32)] + gather_sems()
+    return call(make_pre_bwd(outgoing), outs, scr + [pltpu.VMEM((4 * CH, CH), BF16)],
+                flops=6 * GIGA, name='mul_pre_bwd', comm=12 if outgoing else 11)(*args)
+
+
+def att_backward(z, dz, bias_all, mask_col, w_qkvg, w_tb, w_o, left=None):
+    *left_all, dz_part, g_qkvg, g_out, db = att_bwd(z, dz, bias_all, mask_col, w_qkvg, w_o, left)
+    dz_new, g_bt = bias_bwd(z, dz_part, db, w_tb, left is not None)
+    return dz_new.reshape(N_POS, CH), [g_qkvg, g_bt, g_out], left_all
 
 
 C_S = 384
@@ -703,20 +872,6 @@
         out_ref[pl.ds(t, n, stride=tiles), :] = value[:, t * 128:(t + 1) * 128]
 
 
-def sing_pre_kernel(s_ref, w_ref, qb_ref, qkv_ref, gate_ref):
-    nhat, _ = norm_parts(s_ref[...].astype(F32))
-    nb = nhat.astype(BF16)
-    p_all = dot_nn(nb, w_ref[...])
-    qkv_ref[:, :C_S] = (p_all[:, :C_S] + qb_ref[...].astype(F32)).astype(BF16)
-    qkv_ref[:, C_S:] = p_all[:, C_S:3 * C_S].astype(BF16)
-    gate_ref[...] = jax.nn.sigmoid(p_all[:, 3 * C_S:])
-
-
-def sing_pre(s, w_qkvg, q_bias):
-    return call(sing_pre_kernel, [sds((ROWS, 3 * C_S), BF16), sds((ROWS, C_S), F32)],
-                flops=GIGA, name='sing_pre')(s, w_qkvg, q_bias[None, :])
-
-
 def sing_stack(x):
     lane = lax.broadcasted_iota(jnp.int32, (TOKENS, GRP_W), 1) // SING_DIM
     x = x.astype(F32)
@@ -738,7 +893,7 @@
 P_ALL = 8064
 
 
-def sing_fused_kernel(bias_ref, q_ref, k_ref, v_ref, gate_ref, s_ref, m_ref, wo_ref, wu_ref, wd_ref, wq_ref, ds_ref,
+def sing_fused_kernel(bias_ref, heads_ref, gate_ref, s_ref, m_ref, wo_ref, wu_ref, wd_ref, wq_ref, ds_ref,
                       so_ref, dsi_ref, pk_ref, dbt_ref, qb_ref,
                       b_all, o_out, o_in, do_out, do_in, dq_out, dq_in, db_out, send, recv):
     me = lax.axis_index(GROUP_AXIS)
@@ -763,7 +918,8 @@
     stage = 0
     ex_bias = start(stage, rows_block(bias_ref), block(b_all))
     b_all[me] = bias_ref[pl.ds(pl.multiple_of(me * TOKENS, TOKENS), TOKENS), :]
-    q, ks, vs = q_ref[...], sing_stack(k_ref[...]), sing_stack(v_ref[...])
+    q, k, v = [cat0([heads_ref[g, t] for g in range(GRP)]) for t in range(3)]
+    ks, vs = sing_stack(k), sing_stack(v)
     logits = dot_nt(ks, q) * SING_SCALE
     mask = m_ref[...]
     ex_bias.arrive()
@@ -1026,15 +1182,27 @@
     )(*late, g_all, early, small)
 
 
+def pack_kernel(*refs):
+    *srcs, o_ref = refs
+    at = 0
+    for ref in srcs:
+        n = ref.shape[0]
+        if n % PACK:
+            o_ref[at:at + PACK, :] = jnp.zeros((PACK, CH), F32)
+        o_ref[at:at + n, :] = ref[...]
+        at += padded(n)
+
+
+def padded(n):
+    return -(-n // PACK) * PACK
+
+
+def pack_rows(*arrays):
+    return call(pack_kernel, [sds((sum(padded(a.shape[0]) for a in arrays), CH), F32)], flops=GIGA, name='pack_rows')(*arrays)
+
+
 def flat_cols(x):
     return x.T.reshape(x.shape)
-
-
-def to_heads(x, n):
-    x = x.reshape(ROWS, n, GRP, GRP_W)
-    x = swap_all(jnp.transpose(x, (2, 1, 0, 3)), 0, 0)
-    x = jnp.transpose(x, (1, 0, 2, 3)).reshape(n, TOKENS, GRP_W)
-    return [x[t] for t in range(n)]
 
 
 def device_step(single_blk, pair_blk, mask_blk, d_single_blk, d_pair_blk, *weights):
@@ -1044,57 +1212,42 @@
     z_zero = pair_blk[0].reshape(N_POS, CH)
     mask_bias = (mask_blk[0].astype(jnp.float32) - 1.0) * MASK_PENALTY
     mask_col = mask_bias[:, None]
-    wt_out, wt_in = w1_in.T, w2_in.T
-    right_out = mul_proj(z_zero, wt_out[HALF:])
-    right_out_all = gather_blocks(right_out)
-    left_out = mul_proj(z_zero, wt_out[:HALF])
-    x_out, z_one, z_one_turned = mul_mix(left_out, right_out_all, z_zero, w1_gate, w1_out, True)
-    right_in = mul_proj(z_one, wt_in[HALF:])
-    right_in_all = gather_blocks(right_in)
-    zt_one = z_one_turned.reshape(N_POS, CH)
-    left_in = mul_proj(z_one, wt_in[:HALF])
-    left_in_t = mul_proj(zt_one, wt_in[:HALF], True)
-    x_in, z_two = mul_mix(left_in_t, right_in_all, z_one, w2_gate, w2_out, False)
-    left_out, z_two = lax.optimization_barrier((left_out, z_two))
-    left_out_all = gather_blocks(left_out)
-    z_three_turned, bias_st = att_fwd(z_two, st_bias, mask_col, st_qkvg.T, st_proj, False)
-    zt_three = z_three_turned.reshape(N_POS, CH)
-    d_pair, zt_three = lax.optimization_barrier((d_pair_blk[0], zt_three))
-    dzt_out = swap_rows(d_pair)
-    zt_four, bias_en = att_fwd(zt_three, en_bias, mask_col, en_qkvg.T, en_proj, True)
-    s_qkv, s_gate = sing_pre(s_rows, s_qkvg, s_qbias)
-    qkv_heads = to_heads(s_qkv, 3)
-    zt_four, left_out_all, dzt_out, qkv_heads = lax.optimization_barrier((zt_four, left_out_all, dzt_out, qkv_heads))
-    zt_five, bias_t = trans_fwd(zt_four, p_up, p_down, s_pbias)
+    right_out = mul_proj(z_zero, w1_in)
+    x_out, z_one, right_out_all, left_out, turned, right_in = mul_mix(z_zero, w1_in, right_out, z_zero, w1_gate, w1_out, w2_in)
+    x_in, z_two, _, _, s_gate, s_heads = mul_mix(
+        turned.reshape(N_POS, CH), w2_in, right_in, z_one, w2_gate, w2_out, single=(s_rows, s_qkvg, s_qbias[None, :]))
+    z_three, bias_st = att_fwd(z_two, st_bias, mask_col, st_qkvg, st_proj)
+    zt_three = z_three.reshape(N_POS, CH)
+    zt_four, bias_en, dzt_out = att_fwd(zt_three, en_bias, mask_col, en_qkvg, en_proj, d_pair_blk[0])
+    zt_five, bias_t, turned_five = trans_fwd(zt_four, p_up, p_down, s_pbias)
     s_out, ds_in, packed, d_bias_t, g_qb = sing_fused(
-        bias_t, *qkv_heads, s_gate, s_rows, mask_col, s_proj, s_up, s_down, s_qkvg, d_single_blk[0])
-    packed, zt_five, d_bias_t, dzt_out = lax.optimization_barrier((packed, zt_five, d_bias_t, dzt_out))
+        bias_t, s_heads, s_gate, s_rows, mask_col, s_proj, s_up, s_down, s_qkvg, d_single_blk[0])
+    packed, d_bias_t = lax.optimization_barrier((packed, d_bias_t))
     packed_all = gather_rows(packed)
-    z_five = swap_rows(zt_five.reshape(ROWS, COLS, CH))
-    dzt_four, g_pup, g_pdown, g_pbt = trans_bwd(zt_four, zt_five, dzt_out, d_bias_t, p_up, p_down, s_pbias)
+    dzt_four, g_pup, g_pdown, g_pbt = trans_bwd(
+        zt_four, zt_five, dzt_out.reshape(N_POS, CH), d_bias_t, p_up, p_down, s_pbias)
     windows = sing_wgrad(packed_all)
     dzt_four, windows = lax.optimization_barrier((dzt_four, windows))
     piece = lax.psum_scatter(windows.reshape(4 * W_ROWS, 128), BATCH_AXIS, scatter_dimension=0, tiled=True)
-    dz_three, end_grads = att_backward(zt_three, dzt_four, bias_en, mask_col, en_qkvg, en_bias, en_proj, True)
+    dz_three, end_grads, (left_out_all,) = att_backward(zt_three, dzt_four, bias_en, mask_col, en_qkvg, en_bias, en_proj, left_out)
     dz_three, piece = lax.optimization_barrier((dz_three, piece))
     pieces = gather_rows(piece)
-    dz_two, start_grads = att_backward(z_two, dz_three, bias_st, mask_col, st_qkvg, st_bias, st_proj, False)
-    dz_two, pieces, z_five = lax.optimization_barrier((dz_two, pieces, z_five))
+    dz_two, start_grads, _ = att_backward(z_two, dz_three, bias_st, mask_col, st_qkvg, st_bias, st_proj)
+    dz_two, pieces = lax.optimization_barrier((dz_two, pieces))
     dx_in, dgl_in, g_in_out = mul_post_bwd(dz_two, x_in, z_one, w2_gate, w2_out, False)
-    dx_all = gather_blocks(dx_in)
     five = jnp.zeros((5, 128), F32)
-    early = cat0([start_grads[0], start_grads[2], end_grads[0], end_grads[2], g_pup, g_pdown, g_qb, five, g_pbt,
-                             start_grads[1], five[:4], end_grads[1], five[:4]])
-    dx_all, early = lax.optimization_barrier((dx_all, early))
+    early = pack_rows(start_grads[0], start_grads[2], end_grads[0], end_grads[2], g_pup, g_pdown, g_qb, g_pbt, start_grads[1], end_grads[1])
+    early, dx_in = lax.optimization_barrier((early, dx_in))
     early = lax.psum(early, (BATCH_AXIS, GROUP_AXIS))
     tail = early[sum(EARLY_SIZES):]
     small = cat0([tail[:8], flat_cols(tail[8:24]), flat_cols(tail[24:28]), five[:4], flat_cols(tail[32:36]), five[:4]])
-    dz_one, g_in_in, g_in_gate = mul_pre_bwd(dx_all, left_in, right_in, z_one, wt_in, w2_gate, dgl_in, dz_two)
+    dz_one, g_in_in, g_in_gate = mul_pre_bwd(dx_in, None, right_in, z_one, w2_in, w2_gate, dgl_in, dz_two)
     dx_out, dgl_out, g_out_out, dx_turned = mul_post_bwd(dz_one, x_out, z_zero, w1_gate, w1_out, True)
-    dz_zero, g_out_in, g_out_gate = mul_pre_bwd(dx_out, left_out_all, right_out_all, z_zero, wt_out, w1_gate, dgl_out, dz_one, dx_turned.reshape(N_POS, CH))
+    dz_zero, g_out_in, g_out_gate, z_five = mul_pre_bwd(
+        dx_out, left_out_all, right_out_all, z_zero, w1_in, w1_gate, dgl_out, dz_one,
+        dx_turned.reshape(N_POS, CH), turned_five.reshape(TURNED))
     late = (g_out_in, g_out_gate, g_out_out, g_in_in, g_in_gate, g_in_out)
     grad_flat = finish(late, pieces.reshape(4, W_ROWS, 128), early, small).reshape(-1)[:PART]
-    z_five = z_five.reshape(ROWS, COLS, CH)
     dz_zero = dz_zero.reshape(ROWS, COLS, CH)
     return s_out[None], z_five[None], ds_in[None], dz_zero[None], grad_flat
 

time: 555 us -> 483 us (0.87)
  waiting for transfers between devices: 80 us -> 0.11 us
  Pallas kernels: 390 us -> 447 us
  blocking collectives: 24.8 us -> 0 us
  local copies, waits for them, and re-layouts: 29.6 us -> 12.1 us
  starting transfers between devices: 8.03 us -> 0.16 us
    all_gather x4 -> x0, waiting for transfers between devices: 71.5 us -> none  [gather_blocks(): return lax.all_gather(x, GROUP_AXIS, axis=0)]
    pallas_call x21 -> x17, Pallas kernels: 340 us -> 399 us  [run(): pl.pallas_call(kernel, out_shape=tuple(out_shape), in_specs=[vm] * len(ar...]
    all_to_all x1 -> x0, blocking collectives: 24.8 us -> none  [swap_all(): return lax.all_to_all(x, GROUP_AXIS, split, join, tiled=True)]
    all_to_all x2 -> x0, starting transfers between devices: 7.06 us -> none  [swap_all(): return lax.all_to_all(x, GROUP_AXIS, split, join, tiled=True)]
    concatenate x2 -> x1, local copies, waits for them, and re-layouts: 9.1 us -> 2.4 us  [cat0(): return jnp.concatenate(xs, axis=0)]
    psum x1, waiting for transfers between devices: 6.08 us -> 0.02 us  [device_step(): early = lax.psum(early, (BATCH_AXIS, GROUP_AXIS))]
  transfers between devices with their start and end apart: 10 -> 4, of which waited for: 5 -> 0; matrix products, arithmetic and copies ran while one was open for 3% -> 0% of each run, Pallas kernels for 48% -> 46%
where the time goes in v2:
time: 483 us; the launch traced here: 474 us
  Pallas kernels  447 us (93%)
  between operations  14.4 us (3%)
  local copies, waits for them, and re-layouts  12.1 us (3%)
    pallas_call x17, Pallas kernels, run(): pl.pallas_call(kernel, out_shape=tuple(out_shape), in_specs=[vm] * len(ar...  399 us
    pallas_call x1, Pallas kernels, finish(): pl.pallas_call(finish_kernel, out_shape=sds((OUT_ROWS, 128), F32), in_spe...  27.5 us
    pallas_call x1, Pallas kernels, sing_fused(): pl.pallas_call(sing_fused_kernel, out_shape=outs, in_specs=[vm] * len(arg...  20.7 us
  transfers between devices with their start and end apart: 4, of which 0 were waited for; matrix products, arithmetic and copies ran while one was open for 0% of the time, Pallas kernels for 46%

profile of v2, /device:TPU:1, one launch (start us, length us, event | category | flops | bytes accessed | tf_op | source)
XLA Modules:
  0.0 474.5 jit_solution(327787086346017349)
XLA Ops:
  7.2 0.0 all-gather.3.cloned.1.call-start
  7.2 0.7 multiply_bitcast_fusion
  7.9 1.2 broadcast_in_dim.13.refs_8_
  9.1 0.7 copy.38.mask_ref.m_ref
  9.9 7.1 %mul_proj.1.refs_2_ = bf16[4096,128]{1,0:T(8,128)(2,1)} custom-call(bf16[4096,128]{1,0:T(8,128)(2,1)} %bitcast.37, bf16[128,512]{1,0:T(8,128)(2,1)} %refs_5_.5), custom_call_target="tpu_custom_call" | custom-call | flops 1073741824 | bytes 4194304 | tf_op jit(solution)/shard_map/mul_proj/pallas_call | solution.py:115
  17.0 52.7 %mul_mix.2 = (f32[4096,128]{1,0:T(8,128)}, bf16[4096,128]{1,0:T(8,128)(2,1)}, bf16[4,4096,128]{2,1,0:T(8,128)(2,1)}, bf16[4096,128]{1,0:T(8,128)(2,1)}, bf16[4,3...) custom-call(bf16[4096,128]{1,0:T(8,128)(2,1)} %bitcast.38, bf16[128,512]{1,0:T(8,128)(2,1)} %refs_5_.5, ...), custom_call_target="tpu_custom_call" | custom-call | flops 3221225472 | bytes 4194304 | tf_op jit(solution)/shard_map/mul_mix/pallas_call | solution.py:115
  69.7 39.0 %mul_mix.3 = (f32[4096,128]{1,0:T(8,128)}, bf16[4096,128]{1,0:T(8,128)(2,1)}, bf16[4,4096,128]{2,1,0:T(8,128)(2,1)}, bf16[4096,128]{1,0:T(8,128)(2,1)}, f32[32,3...) custom-call(bf16[4096,128]{1,0:T(8,128)(2,1)} %bitcast.58, bf16[128,512]{1,0:T(8,128)(2,1)} %refs_3_.1, ...), custom_call_target="tpu_custom_call" | custom-call | flops 3221225472 | bytes 4194304 | tf_op jit(solution)/shard_map/mul_mix/pallas_call | solution.py:115
  108.7 31.5 %att_fwd.2 = (bf16[4,32,32,128]{3,2,1,0:T(8,128)(2,1)}, bf16[128,512]{1,0:T(8,128)(2,1)}) custom-call(bf16[4096,128]{1,0:T(8,128)(2,1)} %get-tuple-element.72.z_ref, bf16[4,128]{1,0:T(4,128)(2,1)} %bitcast.49, f32[128,1]{1,0:T(8,128)} %copy.38.mask_ref.m_ref, bf16[128,512]{1,0:T(8,128)(2,1)} %w_ref.9, bf16[128,128]{1,0:T(8,128)(2,1)} %wo_ref.11), custom_call_target="tpu_custom_call" | custom-call | flops 3221225472 | bytes 4194304 | tf_op jit(solution)/shard_map/att_fwd/pallas_call | solution.py:115
  140.2 21.5 %att_fwd.3 = (bf16[4096,128]{1,0:T(8,128)(2,1)}, bf16[128,512]{1,0:T(8,128)(2,1)}, bf16[4,32,32,128]{3,2,1,0:T(8,128)(2,1)}) custom-call(bf16[4096,128]{1,0:T(8,128)(2,1)} %bitcast.52, bf16[4,128]{1,0:T(4,128)(2,1)} %bitcast.47, f32[128,1]{1,0:T(8,128)} %copy.38.mask_ref.m_ref, bf16[128,512]{1,0:T(8,128)(2,1)} %w_ref.8, bf16[128,128]{1,0:T(8,128)(2,1)} %wo_ref.10, ...), custom_call_target="tpu_custom_call" | custom-call | flops 3221225472 | bytes 4194304 | tf_op jit(solution)/shard_map/att_fwd/pallas_call | solution.py:115
  161.8 13.5 %trans_fwd.1 = (bf16[4096,128]{1,0:T(8,128)(2,1)}, bf16[512,128]{1,0:T(8,128)(2,1)}, bf16[4096,128]{1,0:T(8,128)(2,1)}) custom-call(bf16[4096,128]{1,0:T(8,128)(2,1)} %get-tuple-element.74.z_ref, bf16[128,1024]{1,0:T(8,128)(2,1)} %wu_ref.5, bf16[512,128]{1,0:T(8,128)(2,1)} %wd_ref.5, bf16[16,128]{1,0:T(8,128)(2,1)} %bitcast.45), custom_call_target="tpu_custom_call" | custom-call | flops 2147483648 | bytes 4194304 | tf_op jit(solution)/shard_map/trans_fwd/pallas_call | solution.py:115
  175.3 20.7 %sing_fused.1 = (bf16[32,384]{1,0:T(8,128)(2,1)}, bf16[32,384]{1,0:T(8,128)(2,1)}, bf16[32,8064]{1,0:T(8,128)(2,1)}, bf16[512,128]{1,0:T(8,128)(2,1)}, f32[3,128]{1,0:T(4,128)}) custom-call(bf16[512,128]{1,0:T(8,128)(2,1)} %get-tuple-element.75.bias_ref, bf16[4,3,32,96]{3,2,1,0:T(8,128)(2,1)} %get-tuple-element.76.heads_ref, ...), custom_call_target="tpu_custom_call" | custom-call | flops 2147483648 | bytes 4194304 | tf_op jit(solution)/shard_map/sing_fused/pallas_call | solution.py:1004
  196.0 0.0 all-gather.3.cloned.1.call-update
  196.0 0.0 reduce-scatter.2.cloned.1.call-start
  196.1 21.0 %trans_bwd.1 = (bf16[4096,128]{1,0:T(8,128)(2,1)}, f32[1024,128]{1,0:T(8,128)}, f32[512,128]{1,0:T(8,128)}, f32[16,128]{1,0:T(8,128)}) custom-call(bf16[4096,128]{1,0:T(8,128)(2,1)} %get-tuple-element.74.z_ref, bf16[4096,128]{1,0:T(8,128)(2,1)} %get-tuple-element.79.z5_ref, bf16[4096,128]{1,0:T(8,128)(2,1)} %bitcast.55, ...), custom_call_target="tpu_custom_call" | custom-call | flops 6442450944 | bytes 4194304 | tf_op jit(solution)/shard_map/trans_bwd/pallas_call | solution.py:115
  217.1 3.8 sing_wgrad.1
  220.9 0.0 reduce-scatter.2.cloned.1.call-update
  221.0 0.0 all-gather.5.cloned.1.call-start
  221.0 33.9 %att_bwd.2 = (bf16[4,4096,128]{2,1,0:T(8,128)(2,1)}, bf16[4096,128]{1,0:T(8,128)(2,1)}, f32[512,128]{1,0:T(8,128)}, f32[128,128]{1,0:T(8,128)}, f32[128,512]{1,0:T(8,128)}) custom-call(bf16[4096,128]{1,0:T(8,128)(2,1)} %bitcast.53, bf16[4096,128]{1,0:T(8,128)(2,1)} %get-tuple-element.86.dz_ref, bf16[128,512]{1,0:T(8,128)(2,1)} %get-tuple-element.87.bias_ref, ...), custom_call_target="tpu_custom_call" | custom-call | flops 8589934592 | bytes 4194304 | tf_op jit(solution)/shard_map/att_bwd/pallas_call | solution.py:115
  254.9 24.4 %bias_bwd.2 = (bf16[4,32,32,128]{3,2,1,0:T(8,128)(2,1)}, f32[4,128]{1,0:T(4,128)}) custom-call(bf16[4096,128]{1,0:T(8,128)(2,1)} %bitcast.54, bf16[4096,128]{1,0:T(8,128)(2,1)} %get-tuple-element.89.dz_ref, f32[128,512]{1,0:T(8,128)} %get-tuple-element.90.db_ref, bf16[4,128]{1,0:T(4,128)(2,1)} %bitcast.48), custom_call_target="tpu_custom_call" | custom-call | flops 1073741824 | bytes 4194304 | tf_op jit(solution)/shard_map/bias_bwd/pallas_call | solution.py:115
  279.4 0.0 reduce-scatter.2.cloned.1.call-done
  279.4 0.0 all-gather.5.cloned.1.call-update
  279.4 0.0 all-reduce.2.cloned.1.call-start
  279.5 28.6 %att_bwd.3 = (bf16[4096,128]{1,0:T(8,128)(2,1)}, f32[512,128]{1,0:T(8,128)}, f32[128,128]{1,0:T(8,128)}, f32[128,512]{1,0:T(8,128)}) custom-call(bf16[4096,128]{1,0:T(8,128)(2,1)} %get-tuple-element.72.z_ref, bf16[4096,128]{1,0:T(8,128)(2,1)} %bitcast.56, bf16[128,512]{1,0:T(8,128)(2,1)} %get-tuple-element.94.bias_ref, f32[128,1]{1,0:T(8,128)} %copy.38.mask_ref.m_ref, ...), custom_call_target="tpu_custom_call" | custom-call | flops 8589934592 | bytes 4194304 | tf_op jit(solution)/shard_map/att_bwd/pallas_call | solution.py:115
  308.1 11.0 %bias_bwd.3 = (bf16[4096,128]{1,0:T(8,128)(2,1)}, f32[4,128]{1,0:T(4,128)}) custom-call(bf16[4096,128]{1,0:T(8,128)(2,1)} %get-tuple-element.72.z_ref, bf16[4096,128]{1,0:T(8,128)(2,1)} %get-tuple-element.103.dz_ref, f32[128,512]{1,0:T(8,128)} %get-tuple-element.104.db_ref, bf16[4,128]{1,0:T(4,128)(2,1)} %bitcast.50), custom_call_target="tpu_custom_call" | custom-call | flops 1073741824 | bytes 4194304 | tf_op jit(solution)/shard_map/bias_bwd/pallas_call | solution.py:115
  319.1 2.6 pack_rows.1
  321.7 11.3 %mul_post_bwd.2 = (bf16[4096,128]{1,0:T(8,128)(2,1)}, bf16[4096,128]{1,0:T(8,128)(2,1)}, f32[128,128]{1,0:T(8,128)}) custom-call(bf16[4096,128]{1,0:T(8,128)(2,1)} %get-tuple-element.109.dz_ref.refs_6_, f32[4096,128]{1,0:T(8,128)} %get-tuple-element.110.x_ref, bf16[4096,128]{1,0:T(8,128)(2,1)} %get-tuple-element.71.refs_3_.z_ref.refs_2_, ...), custom_call_target="tpu_custom_call" | custom-call | flops 3221225472 | bytes 4194304 | tf_op jit(solution)/shard_map/mul_post_bwd/pallas_call | solution.py:115
  333.0 0.0 all-reduce.2.cloned.1.call-update
  333.0 46.2 %mul_pre_bwd.2 = (bf16[4096,128]{1,0:T(8,128)(2,1)}, f32[512,128]{1,0:T(8,128)}, f32[128,128]{1,0:T(8,128)}) custom-call(bf16[4096,128]{1,0:T(8,128)(2,1)} %get-tuple-element.112.refs_0_, bf16[4096,128]{1,0:T(8,128)(2,1)} %get-tuple-element.70.refs_2_.refs_1_, bf16[4096,128]{1,0:T(8,128)(2,1)} %get-tuple-element.71.refs_3_.z_ref.refs_2_, ...), custom_call_target="tpu_custom_call" | custom-call | flops 6442450944 | bytes 4194304 | tf_op jit(solution)/shard_map/mul_pre_bwd/pallas_call | solution.py:115
  379.2 27.0 %mul_post_bwd.3 = (bf16[4096,128]{1,0:T(8,128)(2,1)}, bf16[4096,128]{1,0:T(8,128)(2,1)}, f32[128,128]{1,0:T(8,128)}, bf16[4,32,32,128]{3,2,1,0:T(8,128)(2,1)}) custom-call(bf16[4096,128]{1,0:T(8,128)(2,1)} %get-tuple-element.114.dz_ref.refs_8_, f32[4096,128]{1,0:T(8,128)} %get-tuple-element.115.x_ref, bf16[4096,128]{1,0:T(8,128)(2,1)} %bitcast.40, ...), custom_call_target="tpu_custom_call" | custom-call | flops 3221225472 | bytes 4194304 | tf_op jit(solution)/shard_map/mul_post_bwd/pallas_call | solution.py:115
  406.2 23.6 %mul_pre_bwd.3 = (bf16[4096,128]{1,0:T(8,128)(2,1)}, f32[512,128]{1,0:T(8,128)}, f32[128,128]{1,0:T(8,128)}, bf16[32,128,128]{2,1,0:T(8,128)(2,1)}) custom-call(bf16[4096,128]{1,0:T(8,128)(2,1)} %get-tuple-element.116.refs_0_, bf16[4096,128]{1,0:T(8,128)(2,1)} %bitcast.57, bf16[4,4096,128]{2,1,0:T(8,128)(2,1)} %get-tuple-element.118.refs_2_, ...), custom_call_target="tpu_custom_call" | custom-call | flops 6442450944 | bytes 4194304 | tf_op jit(solution)/shard_map/mul_pre_bwd/pallas_call | solution.py:115
  429.8 0.0 all-reduce.2.cloned.1.call-done.refs_7_
  429.8 0.7 slice_bitcast_fusion
  430.5 0.1 copy.43
  430.6 0.1 reshape.75
  430.7 0.7 slice_bitcast_fusion.1
  431.4 0.1 copy.45
  431.5 0.1 reshape.77
  431.6 0.1 copy.44
  431.8 0.1 reshape.76
  431.9 0.7 slice.25
  432.6 2.4 concatenate.3.refs_8_
  435.0 27.5 %finish.1 = f32[5992,128]{1,0:T(8,128)} custom-call(f32[512,128]{1,0:T(8,128)} %get-tuple-element.125.refs_0_, f32[128,128]{1,0:T(8,128)} %get-tuple-element.126.refs_1_, f32[128,128]{1,0:T(8,128)} %get-tuple-element.127.refs_2_, f32[512,128]{1,0:T(8,128)} %get-tuple-element.128.refs_3_, f32[128,128]{1,0:T(8,128)} %get-tuple-element.129.refs_4_, ...), custom_call_target="tpu_custom_call" | custom-call | flops 1073741824 | bytes 4194304 | tf_op jit(solution)/shard_map/finish/pallas_call | solution.py:1176
  462.5 0.0 copy-start.3
  462.5 0.6 copy.52
  463.1 1.0 copy.53
  464.1 0.6 copy.54
  464.7 1.0 copy.55
  465.7 1.8 copy.56
  (12 shorter events, 0.0 us)
Async XLA Ops:
  7.2 209.9 %all-gather.3.cloned.1.call-start = ((), (), s32[]{:S(2)}) async-start(), calls=%async_computation.1 | async-start | bytes 2580480 | tf_op jit(solution)/shard_map/all_gather | solution.py:16
  196.0 83.4 %reduce-scatter.2.cloned.1.call-start = ((), (), s32[]{:S(2)}) async-start(), calls=%async_computation.2 | async-start | bytes 4177920 | tf_op jit(solution)/shard_map/reduce_scatter | solution.py:1231
  221.0 100.7 %all-gather.5.cloned.1.call-start = ((), (), s32[]{:S(2)}) async-start(), calls=%async_computation.3 | async-start | bytes 4177920 | tf_op jit(solution)/shard_map/all_gather | solution.py:16
  279.4 150.4 %all-reduce.2.cloned.1.call-start = ((), (), s32[]{:S(2)}) async-start(), calls=%async_computation.4 | async-start | bytes 2924544 | tf_op jit(solution)/shard_map/psum | solution.py:1241
  435.0 27.5 %copy-start.4 = (bf16[32,384]{1,0:T(8,128)(2,1)S(1)}, bf16[32,384]{1,0:T(8,128)(2,1)}, u32[]{:S(2)}) copy-start(bf16[32,384]{1,0:T(8,128)(2,1)} %get-tuple-element.78) | copy-start | bytes 73732
  435.0 28.1 %copy-start.2 = (bf16[32,128,128]{2,1,0:T(8,128)(2,1)S(1)}, bf16[32,128,128]{2,1,0:T(8,128)(2,1)}, u32[]{:S(2)}) copy-start(bf16[32,128,128]{2,1,0:T(8,128)(2,1)} %get-tuple-element.122) | copy-start | bytes 3145732
  462.5 1.6 copy-start.3
  462.5 2.2 copy-start.1
  463.1 2.6 copy-start
Sparse Core Ops, SparseCore 0:
  196.2 20.8 all-gather.2
  221.1 41.5 reduce-scatter.1
  279.5 27.7 all-gather.4
  333.2 70.2 all-reduce.1

commit v3 on v2

--- a/solution.py
+++ b/solution.py
@@ -29,12 +29,12 @@
 GRP = 4
 OFFSETS = (1, 2, 3)
 MESH_ID = pl.DeviceIdType.MESH
-FOUR = 4
+FOUR = 8
 N_DEV = 16
 WIDE = FOUR * COLS
 TRI_DIM = 32
 TRI_SCALE = TRI_DIM ** -0.5
-STEP_ROWS = 4
+STEP_ROWS = 8
 CHUNK = STEP_ROWS * COLS
 
 
@@ -255,8 +255,8 @@
     return [sems, sems]
 
 
-ATT_STEP = 4
-BWD_STEP = 4
+ATT_STEP = 8
+BWD_STEP = 8
 
 
 def fill_bias(bias_ref, mask_ref, bm_ref):
@@ -823,8 +823,8 @@
             dzo_ref[chunk_ds(t, WIDE), :] = (dz_ref[chunk_ds(t, WIDE), :].astype(F32) + norm_back(dn, nhat, r_std)).astype(BF16)
 
         loop(ROWS // FOUR, step)
-        for t in range(FOUR):
-            dwr_ref[pl.ds(t, CH, stride=FOUR), :] = dwt_ref[t * CH:(t + 1) * CH, :].T
+        for t in range(GRP):
+            dwr_ref[pl.ds(t, CH, stride=GRP), :] = dwt_ref[t * CH:(t + 1) * CH, :].T
         if outgoing:
             ex.arrive()
             ex.leave()
@@ -1114,11 +1114,12 @@
                 w_ref[pl.ds(first_row + r0 * tiles, r1 - r0, stride=tiles), :] = g_ref[k, src:src + r1 - r0, :]
         if part:
             lane = lax.broadcasted_iota(jnp.int32, (SHIFT_ROWS, CH), 1)
-            for i in range(OUT_ROWS // SHIFT_ROWS):
-                rows = slice(i * SHIFT_ROWS, (i + 1) * SHIFT_ROWS)
-                a = pltpu.roll(w_ref[rows, :], CH - lanes_off, 1)
-                b = pltpu.roll(w_ref[rows.start + 1:rows.stop + 1, :], CH - lanes_off, 1)
-                o_ref[rows, :] = jnp.where(lane < CH - lanes_off, a, b)
+
+            def shift(i):
+                w = pltpu.roll(w_ref[pl.ds(pl.multiple_of(i * SHIFT_ROWS, PACK), SHIFT_ROWS + PACK), :], CH - lanes_off, 1)
+                o_ref[chunk_ds(i, SHIFT_ROWS), :] = jnp.where(lane < CH - lanes_off, w[:SHIFT_ROWS], w[1:SHIFT_ROWS + 1])
+
+            loop(OUT_ROWS // SHIFT_ROWS, shift)
         else:
             o_ref[LATE_ROWS:, :] = w_ref[LATE_ROWS:OUT_ROWS, :]
 
@@ -1147,7 +1148,7 @@
             src_ref=sum_ref, dst_ref=o_ref.at[piece(src), :], send_sem=send2.at[k], recv_sem=recv2.at[src],
             device_id={BATCH_AXIS: 0, GROUP_AXIS: k}, device_id_type=MESH_ID)
 
-    for k in range(FOUR):
+    for k in range(GRP):
         @pl.when(me != k)
         def _():
             second(k, me).start()
@@ -1156,7 +1157,7 @@
     def _():
         o_ref[piece(me), :] = total
 
-    for k in range(FOUR):
+    for k in range(GRP):
         @pl.when(me != k)
         def _():
             second(k, me).wait_send()

time: 483 us -> 469 us (0.971)
  Pallas kernels: 447 us -> 432 us
    pallas_call x17, Pallas kernels: 399 us -> 383 us  [run(): pl.pallas_call(kernel, out_shape=tuple(out_shape), in_specs=[vm] * len(ar...]
  transfers between devices with their start and end apart: 4 -> 4, of which waited for: 0 -> 1; matrix products, arithmetic and copies ran while one was open for 0% -> 0% of each run, Pallas kernels for 46% -> 46%
where the time goes in v3:
time: 469 us; the launch traced here: 460 us
  Pallas kernels  432 us (92%)
  between operations  14.4 us (3%)
  local copies, waits for them, and re-layouts  12.1 us (3%)
    pallas_call x17, Pallas kernels, run(): pl.pallas_call(kernel, out_shape=tuple(out_shape), in_specs=[vm] * len(ar...  383 us
    pallas_call x1, Pallas kernels, finish(): pl.pallas_call(finish_kernel, out_shape=sds((OUT_ROWS, 128), F32), in_spe...  28 us
    pallas_call x1, Pallas kernels, sing_fused(): pl.pallas_call(sing_fused_kernel, out_shape=outs, in_specs=[vm] * len(arg...  20.6 us
  transfers between devices with their start and end apart: 4, of which 1 were waited for; matrix products, arithmetic and copies ran while one was open for 0% of the time, Pallas kernels for 46%

profile of v3, /device:TPU:1, one launch (start us, length us, event | category | flops | bytes accessed | tf_op | source)
XLA Modules:
  0.0 460.4 jit_solution(4306086577755637745)
XLA Ops:
  7.2 0.0 all-gather.3.cloned.1.call-start
  7.2 0.7 multiply_bitcast_fusion
  7.9 1.2 broadcast_in_dim.13.refs_8_
  9.1 0.7 copy.38.mask_ref.m_ref
  9.9 5.8 %mul_proj.1.refs_2_ = bf16[4096,128]{1,0:T(8,128)(2,1)} custom-call(bf16[4096,128]{1,0:T(8,128)(2,1)} %bitcast.37, bf16[128,512]{1,0:T(8,128)(2,1)} %refs_5_.5), custom_call_target="tpu_custom_call" | custom-call | flops 1073741824 | bytes 4194304 | tf_op jit(solution)/shard_map/mul_proj/pallas_call | solution.py:115
  15.6 52.0 %mul_mix.2 = (f32[4096,128]{1,0:T(8,128)}, bf16[4096,128]{1,0:T(8,128)(2,1)}, bf16[4,4096,128]{2,1,0:T(8,128)(2,1)}, bf16[4096,128]{1,0:T(8,128)(2,1)}, bf16[4,3...) custom-call(bf16[4096,128]{1,0:T(8,128)(2,1)} %bitcast.38, bf16[128,512]{1,0:T(8,128)(2,1)} %refs_5_.5, ...), custom_call_target="tpu_custom_call" | custom-call | flops 3221225472 | bytes 4194304 | tf_op jit(solution)/shard_map/mul_mix/pallas_call | solution.py:115
  67.6 37.6 %mul_mix.3 = (f32[4096,128]{1,0:T(8,128)}, bf16[4096,128]{1,0:T(8,128)(2,1)}, bf16[4,4096,128]{2,1,0:T(8,128)(2,1)}, bf16[4096,128]{1,0:T(8,128)(2,1)}, f32[32,3...) custom-call(bf16[4096,128]{1,0:T(8,128)(2,1)} %bitcast.58, bf16[128,512]{1,0:T(8,128)(2,1)} %refs_3_.1, ...), custom_call_target="tpu_custom_call" | custom-call | flops 3221225472 | bytes 4194304 | tf_op jit(solution)/shard_map/mul_mix/pallas_call | solution.py:115
  105.3 30.6 %att_fwd.2 = (bf16[4,32,32,128]{3,2,1,0:T(8,128)(2,1)}, bf16[128,512]{1,0:T(8,128)(2,1)}) custom-call(bf16[4096,128]{1,0:T(8,128)(2,1)} %get-tuple-element.72.z_ref, bf16[4,128]{1,0:T(4,128)(2,1)} %bitcast.49, f32[128,1]{1,0:T(8,128)} %copy.38.mask_ref.m_ref, bf16[128,512]{1,0:T(8,128)(2,1)} %w_ref.9, bf16[128,128]{1,0:T(8,128)(2,1)} %wo_ref.11), custom_call_target="tpu_custom_call" | custom-call | flops 3221225472 | bytes 4194304 | tf_op jit(solution)/shard_map/att_fwd/pallas_call | solution.py:115
  135.9 20.7 %att_fwd.3 = (bf16[4096,128]{1,0:T(8,128)(2,1)}, bf16[128,512]{1,0:T(8,128)(2,1)}, bf16[4,32,32,128]{3,2,1,0:T(8,128)(2,1)}) custom-call(bf16[4096,128]{1,0:T(8,128)(2,1)} %bitcast.52, bf16[4,128]{1,0:T(4,128)(2,1)} %bitcast.47, f32[128,1]{1,0:T(8,128)} %copy.38.mask_ref.m_ref, bf16[128,512]{1,0:T(8,128)(2,1)} %w_ref.8, bf16[128,128]{1,0:T(8,128)(2,1)} %wo_ref.10, ...), custom_call_target="tpu_custom_call" | custom-call | flops 3221225472 | bytes 4194304 | tf_op jit(solution)/shard_map/att_fwd/pallas_call | solution.py:115
  156.7 11.2 %trans_fwd.1 = (bf16[4096,128]{1,0:T(8,128)(2,1)}, bf16[512,128]{1,0:T(8,128)(2,1)}, bf16[4096,128]{1,0:T(8,128)(2,1)}) custom-call(bf16[4096,128]{1,0:T(8,128)(2,1)} %get-tuple-element.74.z_ref, bf16[128,1024]{1,0:T(8,128)(2,1)} %wu_ref.5, bf16[512,128]{1,0:T(8,128)(2,1)} %wd_ref.5, bf16[16,128]{1,0:T(8,128)(2,1)} %bitcast.45), custom_call_target="tpu_custom_call" | custom-call | flops 2147483648 | bytes 4194304 | tf_op jit(solution)/shard_map/trans_fwd/pallas_call | solution.py:115
  167.9 20.6 %sing_fused.1 = (bf16[32,384]{1,0:T(8,128)(2,1)}, bf16[32,384]{1,0:T(8,128)(2,1)}, bf16[32,8064]{1,0:T(8,128)(2,1)}, bf16[512,128]{1,0:T(8,128)(2,1)}, f32[3,128]{1,0:T(4,128)}) custom-call(bf16[512,128]{1,0:T(8,128)(2,1)} %get-tuple-element.75.bias_ref, bf16[4,3,32,96]{3,2,1,0:T(8,128)(2,1)} %get-tuple-element.76.heads_ref, ...), custom_call_target="tpu_custom_call" | custom-call | flops 2147483648 | bytes 4194304 | tf_op jit(solution)/shard_map/sing_fused/pallas_call | solution.py:1004
  188.5 0.0 all-gather.3.cloned.1.call-update
  188.5 0.0 reduce-scatter.2.cloned.1.call-start
  188.6 19.6 %trans_bwd.1 = (bf16[4096,128]{1,0:T(8,128)(2,1)}, f32[1024,128]{1,0:T(8,128)}, f32[512,128]{1,0:T(8,128)}, f32[16,128]{1,0:T(8,128)}) custom-call(bf16[4096,128]{1,0:T(8,128)(2,1)} %get-tuple-element.74.z_ref, bf16[4096,128]{1,0:T(8,128)(2,1)} %get-tuple-element.79.z5_ref, bf16[4096,128]{1,0:T(8,128)(2,1)} %bitcast.55, ...), custom_call_target="tpu_custom_call" | custom-call | flops 6442450944 | bytes 4194304 | tf_op jit(solution)/shard_map/trans_bwd/pallas_call | solution.py:115
  208.2 1.4 all-gather.3.cloned.1.call-done.m_ref
  209.5 3.8 sing_wgrad.1
  213.4 0.0 reduce-scatter.2.cloned.1.call-update
  213.4 0.0 all-gather.5.cloned.1.call-start
  213.4 31.6 %att_bwd.2 = (bf16[4,4096,128]{2,1,0:T(8,128)(2,1)}, bf16[4096,128]{1,0:T(8,128)(2,1)}, f32[512,128]{1,0:T(8,128)}, f32[128,128]{1,0:T(8,128)}, f32[128,512]{1,0:T(8,128)}) custom-call(bf16[4096,128]{1,0:T(8,128)(2,1)} %bitcast.53, bf16[4096,128]{1,0:T(8,128)(2,1)} %get-tuple-element.86.dz_ref, bf16[128,512]{1,0:T(8,128)(2,1)} %get-tuple-element.87.bias_ref, ...), custom_call_target="tpu_custom_call" | custom-call | flops 8589934592 | bytes 4194304 | tf_op jit(solution)/shard_map/att_bwd/pallas_call | solution.py:115
  245.1 24.8 %bias_bwd.2 = (bf16[4,32,32,128]{3,2,1,0:T(8,128)(2,1)}, f32[4,128]{1,0:T(4,128)}) custom-call(bf16[4096,128]{1,0:T(8,128)(2,1)} %bitcast.54, bf16[4096,128]{1,0:T(8,128)(2,1)} %get-tuple-element.89.dz_ref, f32[128,512]{1,0:T(8,128)} %get-tuple-element.90.db_ref, bf16[4,128]{1,0:T(4,128)(2,1)} %bitcast.48), custom_call_target="tpu_custom_call" | custom-call | flops 1073741824 | bytes 4194304 | tf_op jit(solution)/shard_map/bias_bwd/pallas_call | solution.py:115
  269.9 0.0 reduce-scatter.2.cloned.1.call-done
  269.9 0.0 all-gather.5.cloned.1.call-update
  269.9 0.0 all-reduce.2.cloned.1.call-start
  270.0 26.8 %att_bwd.3 = (bf16[4096,128]{1,0:T(8,128)(2,1)}, f32[512,128]{1,0:T(8,128)}, f32[128,128]{1,0:T(8,128)}, f32[128,512]{1,0:T(8,128)}) custom-call(bf16[4096,128]{1,0:T(8,128)(2,1)} %get-tuple-element.72.z_ref, bf16[4096,128]{1,0:T(8,128)(2,1)} %bitcast.56, bf16[128,512]{1,0:T(8,128)(2,1)} %get-tuple-element.94.bias_ref, f32[128,1]{1,0:T(8,128)} %copy.38.mask_ref.m_ref, ...), custom_call_target="tpu_custom_call" | custom-call | flops 8589934592 | bytes 4194304 | tf_op jit(solution)/shard_map/att_bwd/pallas_call | solution.py:115
  296.8 11.0 %bias_bwd.3 = (bf16[4096,128]{1,0:T(8,128)(2,1)}, f32[4,128]{1,0:T(4,128)}) custom-call(bf16[4096,128]{1,0:T(8,128)(2,1)} %get-tuple-element.72.z_ref, bf16[4096,128]{1,0:T(8,128)(2,1)} %get-tuple-element.103.dz_ref, f32[128,512]{1,0:T(8,128)} %get-tuple-element.104.db_ref, bf16[4,128]{1,0:T(4,128)(2,1)} %bitcast.50), custom_call_target="tpu_custom_call" | custom-call | flops 1073741824 | bytes 4194304 | tf_op jit(solution)/shard_map/bias_bwd/pallas_call | solution.py:115
  307.8 2.6 pack_rows.1
  310.4 10.6 %mul_post_bwd.2 = (bf16[4096,128]{1,0:T(8,128)(2,1)}, bf16[4096,128]{1,0:T(8,128)(2,1)}, f32[128,128]{1,0:T(8,128)}) custom-call(bf16[4096,128]{1,0:T(8,128)(2,1)} %get-tuple-element.109.dz_ref.refs_6_, f32[4096,128]{1,0:T(8,128)} %get-tuple-element.110.x_ref, bf16[4096,128]{1,0:T(8,128)(2,1)} %get-tuple-element.71.refs_3_.z_ref.refs_2_, ...), custom_call_target="tpu_custom_call" | custom-call | flops 3221225472 | bytes 4194304 | tf_op jit(solution)/shard_map/mul_post_bwd/pallas_call | solution.py:115
  321.0 0.0 all-reduce.2.cloned.1.call-update
  321.1 45.2 %mul_pre_bwd.2 = (bf16[4096,128]{1,0:T(8,128)(2,1)}, f32[512,128]{1,0:T(8,128)}, f32[128,128]{1,0:T(8,128)}) custom-call(bf16[4096,128]{1,0:T(8,128)(2,1)} %get-tuple-element.112.refs_0_, bf16[4096,128]{1,0:T(8,128)(2,1)} %get-tuple-element.70.refs_2_.refs_1_, bf16[4096,128]{1,0:T(8,128)(2,1)} %get-tuple-element.71.refs_3_.z_ref.refs_2_, ...), custom_call_target="tpu_custom_call" | custom-call | flops 6442450944 | bytes 4194304 | tf_op jit(solution)/shard_map/mul_pre_bwd/pallas_call | solution.py:115
  366.3 27.0 %mul_post_bwd.3 = (bf16[4096,128]{1,0:T(8,128)(2,1)}, bf16[4096,128]{1,0:T(8,128)(2,1)}, f32[128,128]{1,0:T(8,128)}, bf16[4,32,32,128]{3,2,1,0:T(8,128)(2,1)}) custom-call(bf16[4096,128]{1,0:T(8,128)(2,1)} %get-tuple-element.114.dz_ref.refs_8_, f32[4096,128]{1,0:T(8,128)} %get-tuple-element.115.x_ref, bf16[4096,128]{1,0:T(8,128)(2,1)} %bitcast.40, ...), custom_call_target="tpu_custom_call" | custom-call | flops 3221225472 | bytes 4194304 | tf_op jit(solution)/shard_map/mul_post_bwd/pallas_call | solution.py:115
  393.3 22.0 %mul_pre_bwd.3 = (bf16[4096,128]{1,0:T(8,128)(2,1)}, f32[512,128]{1,0:T(8,128)}, f32[128,128]{1,0:T(8,128)}, bf16[32,128,128]{2,1,0:T(8,128)(2,1)}) custom-call(bf16[4096,128]{1,0:T(8,128)(2,1)} %get-tuple-element.116.refs_0_, bf16[4096,128]{1,0:T(8,128)(2,1)} %bitcast.57, bf16[4,4096,128]{2,1,0:T(8,128)(2,1)} %get-tuple-element.118.refs_2_, ...), custom_call_target="tpu_custom_call" | custom-call | flops 6442450944 | bytes 4194304 | tf_op jit(solution)/shard_map/mul_pre_bwd/pallas_call | solution.py:115
  415.3 0.0 all-reduce.2.cloned.1.call-done.refs_7_
  415.3 0.7 slice_bitcast_fusion
  416.0 0.1 copy.43
  416.1 0.1 reshape.75
  416.2 0.7 slice_bitcast_fusion.1
  416.9 0.1 copy.45
  417.0 0.1 reshape.77
  417.1 0.1 copy.44
  417.2 0.1 reshape.76
  417.4 0.7 slice.25
  418.0 2.4 concatenate.3.refs_8_
  420.4 28.0 %finish.1 = f32[5992,128]{1,0:T(8,128)} custom-call(f32[512,128]{1,0:T(8,128)} %get-tuple-element.125.refs_0_, f32[128,128]{1,0:T(8,128)} %get-tuple-element.126.refs_1_, f32[128,128]{1,0:T(8,128)} %get-tuple-element.127.refs_2_, f32[512,128]{1,0:T(8,128)} %get-tuple-element.128.refs_3_, f32[128,128]{1,0:T(8,128)} %get-tuple-element.129.refs_4_, ...), custom_call_target="tpu_custom_call" | custom-call | flops 1073741824 | bytes 4194304 | tf_op jit(solution)/shard_map/finish/pallas_call | solution.py:1177
  448.4 0.6 copy.52
  449.1 1.0 copy.53
  450.0 0.6 copy.54
  450.6 1.0 copy.55
  451.6 1.8 copy.56
  (12 shorter events, 0.0 us)
Async XLA Ops:
  7.2 202.4 %all-gather.3.cloned.1.call-start = ((), (), s32[]{:S(2)}) async-start(), calls=%async_computation.1 | async-start | bytes 2580480 | tf_op jit(solution)/shard_map/all_gather | solution.py:16
  188.5 81.4 %reduce-scatter.2.cloned.1.call-start = ((), (), s32[]{:S(2)}) async-start(), calls=%async_computation.2 | async-start | bytes 4177920 | tf_op jit(solution)/shard_map/reduce_scatter | solution.py:1232
  213.4 97.0 %all-gather.5.cloned.1.call-start = ((), (), s32[]{:S(2)}) async-start(), calls=%async_computation.3 | async-start | bytes 4177920 | tf_op jit(solution)/shard_map/all_gather | solution.py:16
  269.9 145.4 %all-reduce.2.cloned.1.call-start = ((), (), s32[]{:S(2)}) async-start(), calls=%async_computation.4 | async-start | bytes 2924544 | tf_op jit(solution)/shard_map/psum | solution.py:1242
  420.4 28.0 %copy-start.4 = (bf16[32,384]{1,0:T(8,128)(2,1)S(1)}, bf16[32,384]{1,0:T(8,128)(2,1)}, u32[]{:S(2)}) copy-start(bf16[32,384]{1,0:T(8,128)(2,1)} %get-tuple-element.78) | copy-start | bytes 73732
  420.4 28.6 %copy-start.2 = (bf16[32,128,128]{2,1,0:T(8,128)(2,1)S(1)}, bf16[32,128,128]{2,1,0:T(8,128)(2,1)}, u32[]{:S(2)}) copy-start(bf16[32,128,128]{2,1,0:T(8,128)(2,1)} %get-tuple-element.122) | copy-start | bytes 3145732
  448.4 1.6 copy-start.3
  448.4 2.2 copy-start.1
  449.1 2.6 copy-start
Sparse Core Ops, SparseCore 0:
  188.6 20.8 all-gather.2
  213.5 40.9 reduce-scatter.1
  270.1 27.3 all-gather.4
  321.2 69.8 all-reduce.1

commit v4 on v3

--- a/solution.py
+++ b/solution.py
@@ -160,7 +160,7 @@
 
 
 PACK = 8
-CHUNKS = 4
+CHUNKS = 8
 CHUNK_ROWS = N_POS // CHUNKS
 
 
@@ -736,8 +736,12 @@
 
         if outgoing:
             await_group()
-        halves(ROWS // FOUR, step, turn)
-        cast_out(scr_ref, dx_ref)
+        def store_dx():
+            cast_out(scr_ref, dx_ref)
+
+        halves(ROWS // FOUR, step, turn, store_dx)
+        if not outgoing:
+            store_dx()
 
     return kernel
 
@@ -1236,12 +1240,11 @@
     dz_two, start_grads, _ = att_backward(z_two, dz_three, bias_st, mask_col, st_qkvg, st_bias, st_proj)
     dz_two, pieces = lax.optimization_barrier((dz_two, pieces))
     dx_in, dgl_in, g_in_out = mul_post_bwd(dz_two, x_in, z_one, w2_gate, w2_out, False)
-    five = jnp.zeros((5, 128), F32)
     early = pack_rows(start_grads[0], start_grads[2], end_grads[0], end_grads[2], g_pup, g_pdown, g_qb, g_pbt, start_grads[1], end_grads[1])
     early, dx_in = lax.optimization_barrier((early, dx_in))
     early = lax.psum(early, (BATCH_AXIS, GROUP_AXIS))
     tail = early[sum(EARLY_SIZES):]
-    small = cat0([tail[:8], flat_cols(tail[8:24]), flat_cols(tail[24:28]), five[:4], flat_cols(tail[32:36]), five[:4]])
+    small = cat0([tail[:8], flat_cols(tail[8:24]), flat_cols(tail[24:28]), tail[28:32], flat_cols(tail[32:36]), tail[36:]])
     dz_one, g_in_in, g_in_gate = mul_pre_bwd(dx_in, None, right_in, z_one, w2_in, w2_gate, dgl_in, dz_two)
     dx_out, dgl_out, g_out_out, dx_turned = mul_post_bwd(dz_one, x_out, z_zero, w1_gate, w1_out, True)
     dz_zero, g_out_in, g_out_gate, z_five = mul_pre_bwd(

time: 469 us -> 467 us (level)
  no operation moved by 1% of the time
where the time goes in v4:
time: 467 us; the launch traced here: 459 us
  Pallas kernels  430 us (92%)
  between operations  14.4 us (3%)
  local copies, waits for them, and re-layouts  12.2 us (3%)
    pallas_call x17, Pallas kernels, run(): pl.pallas_call(kernel, out_shape=tuple(out_shape), in_specs=[vm] * len(ar...  381 us
    pallas_call x1, Pallas kernels, finish(): pl.pallas_call(finish_kernel, out_shape=sds((OUT_ROWS, 128), F32), in_spe...  28.1 us
    pallas_call x1, Pallas kernels, sing_fused(): pl.pallas_call(sing_fused_kernel, out_shape=outs, in_specs=[vm] * len(arg...  20.6 us
  transfers between devices with their start and end apart: 4, of which 1 were waited for; matrix products, arithmetic and copies ran while one was open for 0% of the time, Pallas kernels for 46%

profile of v4, /device:TPU:1, one launch (start us, length us, event | category | flops | bytes accessed | tf_op | source)
XLA Modules:
  0.0 458.6 jit_solution(1783569952561998582)
XLA Ops:
  7.2 0.0 all-gather.3.cloned.1.call-start
  7.2 0.7 multiply_bitcast_fusion
  7.9 1.2 broadcast_in_dim.13.refs_8_
  9.1 0.7 copy.35.mask_ref.m_ref
  9.9 5.8 %mul_proj.1.refs_2_ = bf16[4096,128]{1,0:T(8,128)(2,1)} custom-call(bf16[4096,128]{1,0:T(8,128)(2,1)} %bitcast.37, bf16[128,512]{1,0:T(8,128)(2,1)} %refs_5_.5), custom_call_target="tpu_custom_call" | custom-call | flops 1073741824 | bytes 4194304 | tf_op jit(solution)/shard_map/mul_proj/pallas_call | solution.py:115
  15.6 51.4 %mul_mix.2 = (f32[4096,128]{1,0:T(8,128)}, bf16[4096,128]{1,0:T(8,128)(2,1)}, bf16[4,4096,128]{2,1,0:T(8,128)(2,1)}, bf16[4096,128]{1,0:T(8,128)(2,1)}, bf16[4,3...) custom-call(bf16[4096,128]{1,0:T(8,128)(2,1)} %bitcast.38, bf16[128,512]{1,0:T(8,128)(2,1)} %refs_5_.5, ...), custom_call_target="tpu_custom_call" | custom-call | flops 3221225472 | bytes 4194304 | tf_op jit(solution)/shard_map/mul_mix/pallas_call | solution.py:115
  67.0 37.3 %mul_mix.3 = (f32[4096,128]{1,0:T(8,128)}, bf16[4096,128]{1,0:T(8,128)(2,1)}, bf16[4,4096,128]{2,1,0:T(8,128)(2,1)}, bf16[4096,128]{1,0:T(8,128)(2,1)}, f32[32,3...) custom-call(bf16[4096,128]{1,0:T(8,128)(2,1)} %bitcast.58, bf16[128,512]{1,0:T(8,128)(2,1)} %refs_3_.1, ...), custom_call_target="tpu_custom_call" | custom-call | flops 3221225472 | bytes 4194304 | tf_op jit(solution)/shard_map/mul_mix/pallas_call | solution.py:115
  104.4 30.5 %att_fwd.2 = (bf16[4,32,32,128]{3,2,1,0:T(8,128)(2,1)}, bf16[128,512]{1,0:T(8,128)(2,1)}) custom-call(bf16[4096,128]{1,0:T(8,128)(2,1)} %get-tuple-element.72.z_ref, bf16[4,128]{1,0:T(4,128)(2,1)} %bitcast.49, f32[128,1]{1,0:T(8,128)} %copy.35.mask_ref.m_ref, bf16[128,512]{1,0:T(8,128)(2,1)} %w_ref.9, bf16[128,128]{1,0:T(8,128)(2,1)} %wo_ref.11), custom_call_target="tpu_custom_call" | custom-call | flops 3221225472 | bytes 4194304 | tf_op jit(solution)/shard_map/att_fwd/pallas_call | solution.py:115
  134.8 20.7 %att_fwd.3 = (bf16[4096,128]{1,0:T(8,128)(2,1)}, bf16[128,512]{1,0:T(8,128)(2,1)}, bf16[4,32,32,128]{3,2,1,0:T(8,128)(2,1)}) custom-call(bf16[4096,128]{1,0:T(8,128)(2,1)} %bitcast.52, bf16[4,128]{1,0:T(4,128)(2,1)} %bitcast.47, f32[128,1]{1,0:T(8,128)} %copy.35.mask_ref.m_ref, bf16[128,512]{1,0:T(8,128)(2,1)} %w_ref.8, bf16[128,128]{1,0:T(8,128)(2,1)} %wo_ref.10, ...), custom_call_target="tpu_custom_call" | custom-call | flops 3221225472 | bytes 4194304 | tf_op jit(solution)/shard_map/att_fwd/pallas_call | solution.py:115
  155.6 11.2 %trans_fwd.1 = (bf16[4096,128]{1,0:T(8,128)(2,1)}, bf16[512,128]{1,0:T(8,128)(2,1)}, bf16[4096,128]{1,0:T(8,128)(2,1)}) custom-call(bf16[4096,128]{1,0:T(8,128)(2,1)} %get-tuple-element.74.z_ref, bf16[128,1024]{1,0:T(8,128)(2,1)} %wu_ref.5, bf16[512,128]{1,0:T(8,128)(2,1)} %wd_ref.5, bf16[16,128]{1,0:T(8,128)(2,1)} %bitcast.45), custom_call_target="tpu_custom_call" | custom-call | flops 2147483648 | bytes 4194304 | tf_op jit(solution)/shard_map/trans_fwd/pallas_call | solution.py:115
  166.8 20.6 %sing_fused.1 = (bf16[32,384]{1,0:T(8,128)(2,1)}, bf16[32,384]{1,0:T(8,128)(2,1)}, bf16[32,8064]{1,0:T(8,128)(2,1)}, bf16[512,128]{1,0:T(8,128)(2,1)}, f32[3,128]{1,0:T(4,128)}) custom-call(bf16[512,128]{1,0:T(8,128)(2,1)} %get-tuple-element.75.bias_ref, bf16[4,3,32,96]{3,2,1,0:T(8,128)(2,1)} %get-tuple-element.76.heads_ref, ...), custom_call_target="tpu_custom_call" | custom-call | flops 2147483648 | bytes 4194304 | tf_op jit(solution)/shard_map/sing_fused/pallas_call | solution.py:1008
  187.4 0.0 all-gather.3.cloned.1.call-update
  187.4 0.0 reduce-scatter.2.cloned.1.call-start
  187.5 19.6 %trans_bwd.1 = (bf16[4096,128]{1,0:T(8,128)(2,1)}, f32[1024,128]{1,0:T(8,128)}, f32[512,128]{1,0:T(8,128)}, f32[16,128]{1,0:T(8,128)}) custom-call(bf16[4096,128]{1,0:T(8,128)(2,1)} %get-tuple-element.74.z_ref, bf16[4096,128]{1,0:T(8,128)(2,1)} %get-tuple-element.79.z5_ref, bf16[4096,128]{1,0:T(8,128)(2,1)} %bitcast.55, ...), custom_call_target="tpu_custom_call" | custom-call | flops 6442450944 | bytes 4194304 | tf_op jit(solution)/shard_map/trans_bwd/pallas_call | solution.py:115
  207.1 1.4 all-gather.3.cloned.1.call-done.m_ref
  208.5 3.8 sing_wgrad.1
  212.3 0.0 reduce-scatter.2.cloned.1.call-update
  212.3 0.0 all-gather.5.cloned.1.call-start
  212.4 31.8 %att_bwd.2 = (bf16[4,4096,128]{2,1,0:T(8,128)(2,1)}, bf16[4096,128]{1,0:T(8,128)(2,1)}, f32[512,128]{1,0:T(8,128)}, f32[128,128]{1,0:T(8,128)}, f32[128,512]{1,0:T(8,128)}) custom-call(bf16[4096,128]{1,0:T(8,128)(2,1)} %bitcast.53, bf16[4096,128]{1,0:T(8,128)(2,1)} %get-tuple-element.86.dz_ref, bf16[128,512]{1,0:T(8,128)(2,1)} %get-tuple-element.87.bias_ref, ...), custom_call_target="tpu_custom_call" | custom-call | flops 8589934592 | bytes 4194304 | tf_op jit(solution)/shard_map/att_bwd/pallas_call | solution.py:115
  244.2 24.9 %bias_bwd.2 = (bf16[4,32,32,128]{3,2,1,0:T(8,128)(2,1)}, f32[4,128]{1,0:T(4,128)}) custom-call(bf16[4096,128]{1,0:T(8,128)(2,1)} %bitcast.54, bf16[4096,128]{1,0:T(8,128)(2,1)} %get-tuple-element.89.dz_ref, f32[128,512]{1,0:T(8,128)} %get-tuple-element.90.db_ref, bf16[4,128]{1,0:T(4,128)(2,1)} %bitcast.48), custom_call_target="tpu_custom_call" | custom-call | flops 1073741824 | bytes 4194304 | tf_op jit(solution)/shard_map/bias_bwd/pallas_call | solution.py:115
  269.0 0.0 reduce-scatter.2.cloned.1.call-done
  269.1 0.0 all-gather.5.cloned.1.call-update
  269.1 0.0 all-reduce.2.cloned.1.call-start
  269.1 26.8 %att_bwd.3 = (bf16[4096,128]{1,0:T(8,128)(2,1)}, f32[512,128]{1,0:T(8,128)}, f32[128,128]{1,0:T(8,128)}, f32[128,512]{1,0:T(8,128)}) custom-call(bf16[4096,128]{1,0:T(8,128)(2,1)} %get-tuple-element.72.z_ref, bf16[4096,128]{1,0:T(8,128)(2,1)} %bitcast.56, bf16[128,512]{1,0:T(8,128)(2,1)} %get-tuple-element.94.bias_ref, f32[128,1]{1,0:T(8,128)} %copy.35.mask_ref.m_ref, ...), custom_call_target="tpu_custom_call" | custom-call | flops 8589934592 | bytes 4194304 | tf_op jit(solution)/shard_map/att_bwd/pallas_call | solution.py:115
  295.9 11.0 %bias_bwd.3 = (bf16[4096,128]{1,0:T(8,128)(2,1)}, f32[4,128]{1,0:T(4,128)}) custom-call(bf16[4096,128]{1,0:T(8,128)(2,1)} %get-tuple-element.72.z_ref, bf16[4096,128]{1,0:T(8,128)(2,1)} %get-tuple-element.103.dz_ref, f32[128,512]{1,0:T(8,128)} %get-tuple-element.104.db_ref, bf16[4,128]{1,0:T(4,128)(2,1)} %bitcast.50), custom_call_target="tpu_custom_call" | custom-call | flops 1073741824 | bytes 4194304 | tf_op jit(solution)/shard_map/bias_bwd/pallas_call | solution.py:115
  307.0 2.6 pack_rows.1
  309.6 10.6 %mul_post_bwd.2 = (bf16[4096,128]{1,0:T(8,128)(2,1)}, bf16[4096,128]{1,0:T(8,128)(2,1)}, f32[128,128]{1,0:T(8,128)}) custom-call(bf16[4096,128]{1,0:T(8,128)(2,1)} %get-tuple-element.109.dz_ref.refs_6_, f32[4096,128]{1,0:T(8,128)} %get-tuple-element.110.x_ref, bf16[4096,128]{1,0:T(8,128)(2,1)} %get-tuple-element.71.refs_3_.z_ref.refs_2_, ...), custom_call_target="tpu_custom_call" | custom-call | flops 3221225472 | bytes 4194304 | tf_op jit(solution)/shard_map/mul_post_bwd/pallas_call | solution.py:115
  320.2 0.0 all-reduce.2.cloned.1.call-update
  320.2 44.6 %mul_pre_bwd.2 = (bf16[4096,128]{1,0:T(8,128)(2,1)}, f32[512,128]{1,0:T(8,128)}, f32[128,128]{1,0:T(8,128)}) custom-call(bf16[4096,128]{1,0:T(8,128)(2,1)} %get-tuple-element.112.refs_0_, bf16[4096,128]{1,0:T(8,128)(2,1)} %get-tuple-element.70.refs_2_.refs_1_, bf16[4096,128]{1,0:T(8,128)(2,1)} %get-tuple-element.71.refs_3_.z_ref.refs_2_, ...), custom_call_target="tpu_custom_call" | custom-call | flops 6442450944 | bytes 4194304 | tf_op jit(solution)/shard_map/mul_pre_bwd/pallas_call | solution.py:115
  364.8 26.4 %mul_post_bwd.3 = (bf16[4096,128]{1,0:T(8,128)(2,1)}, bf16[4096,128]{1,0:T(8,128)(2,1)}, f32[128,128]{1,0:T(8,128)}, bf16[4,32,32,128]{3,2,1,0:T(8,128)(2,1)}) custom-call(bf16[4096,128]{1,0:T(8,128)(2,1)} %get-tuple-element.114.dz_ref.refs_8_, f32[4096,128]{1,0:T(8,128)} %get-tuple-element.115.x_ref, bf16[4096,128]{1,0:T(8,128)(2,1)} %bitcast.40, ...), custom_call_target="tpu_custom_call" | custom-call | flops 3221225472 | bytes 4194304 | tf_op jit(solution)/shard_map/mul_post_bwd/pallas_call | solution.py:115
  391.3 22.0 %mul_pre_bwd.3 = (bf16[4096,128]{1,0:T(8,128)(2,1)}, f32[512,128]{1,0:T(8,128)}, f32[128,128]{1,0:T(8,128)}, bf16[32,128,128]{2,1,0:T(8,128)(2,1)}) custom-call(bf16[4096,128]{1,0:T(8,128)(2,1)} %get-tuple-element.116.refs_0_, bf16[4096,128]{1,0:T(8,128)(2,1)} %bitcast.57, bf16[4,4096,128]{2,1,0:T(8,128)(2,1)} %get-tuple-element.118.refs_2_, ...), custom_call_target="tpu_custom_call" | custom-call | flops 6442450944 | bytes 4194304 | tf_op jit(solution)/shard_map/mul_pre_bwd/pallas_call | solution.py:115
  413.3 0.0 all-reduce.2.cloned.1.call-done.refs_7_
  413.3 0.7 slice_bitcast_fusion
  414.0 0.1 copy.40
  414.1 0.1 reshape.75
  414.2 0.8 fusion
  415.0 0.1 copy.42
  415.1 0.1 reshape.77
  415.2 0.1 copy.41
  415.3 0.1 reshape.76
  415.4 0.7 slice.35
  416.1 2.4 concatenate.3.refs_8_
  418.5 28.1 %finish.1 = f32[5992,128]{1,0:T(8,128)} custom-call(f32[512,128]{1,0:T(8,128)} %get-tuple-element.125.refs_0_, f32[128,128]{1,0:T(8,128)} %get-tuple-element.126.refs_1_, f32[128,128]{1,0:T(8,128)} %get-tuple-element.127.refs_2_, f32[512,128]{1,0:T(8,128)} %get-tuple-element.128.refs_3_, f32[128,128]{1,0:T(8,128)} %get-tuple-element.129.refs_4_, ...), custom_call_target="tpu_custom_call" | custom-call | flops 1073741824 | bytes 4194304 | tf_op jit(solution)/shard_map/finish/pallas_call | solution.py:1181
  446.6 0.6 copy.49
  447.2 1.0 copy.50
  448.2 0.6 copy.51
  448.8 1.0 copy.52
  449.8 1.8 copy.53
  (11 shorter events, 0.0 us)
Async XLA Ops:
  7.2 201.3 %all-gather.3.cloned.1.call-start = ((), (), s32[]{:S(2)}) async-start(), calls=%async_computation.1 | async-start | bytes 2580480 | tf_op jit(solution)/shard_map/all_gather | solution.py:16
  187.4 81.6 %reduce-scatter.2.cloned.1.call-start = ((), (), s32[]{:S(2)}) async-start(), calls=%async_computation.2 | async-start | bytes 4177920 | tf_op jit(solution)/shard_map/reduce_scatter | solution.py:1236
  212.3 97.2 %all-gather.5.cloned.1.call-start = ((), (), s32[]{:S(2)}) async-start(), calls=%async_computation.3 | async-start | bytes 4177920 | tf_op jit(solution)/shard_map/all_gather | solution.py:16
  269.1 144.2 %all-reduce.2.cloned.1.call-start = ((), (), s32[]{:S(2)}) async-start(), calls=%async_computation.4 | async-start | bytes 2924544 | tf_op jit(solution)/shard_map/psum | solution.py:1245
  418.5 28.1 %copy-start.4 = (bf16[32,384]{1,0:T(8,128)(2,1)S(1)}, bf16[32,384]{1,0:T(8,128)(2,1)}, u32[]{:S(2)}) copy-start(bf16[32,384]{1,0:T(8,128)(2,1)} %get-tuple-element.78) | copy-start | bytes 73732
  418.5 28.7 %copy-start.2 = (bf16[32,128,128]{2,1,0:T(8,128)(2,1)S(1)}, bf16[32,128,128]{2,1,0:T(8,128)(2,1)}, u32[]{:S(2)}) copy-start(bf16[32,128,128]{2,1,0:T(8,128)(2,1)} %get-tuple-element.122) | copy-start | bytes 3145732
  446.6 1.6 copy-start.3
  446.6 2.2 copy-start.1
  447.2 2.6 copy-start
Sparse Core Ops, SparseCore 0:
  187.5 20.8 all-gather.2
  212.4 40.9 reduce-scatter.1
  269.2 27.3 all-gather.4
  320.3 69.6 all-reduce.1
